TPU v7x, 32 devices: a whole 2x2x4 slice. The times are simulated.
32 devices in a mesh: dp: 4 (over z), ep: 8 (over y, x, core).
Axes of the slice: x: 2, y: 2, z: 4, core: 2. Of those that a mesh axis runs over, the one named last changes fastest.
Arguments:
- x_tokens: bfloat16 [49152, 1024], P(('dp', 'ep'))
- w_router: float32 [1024, 32], replicated
- expert_ids: int32 [49152, 8], P(('dp', 'ep'))
- w_gate: bfloat16 [32, 1024, 512], P('ep')
- w_up: bfloat16 [32, 1024, 512], P('ep')
- w_down: bfloat16 [32, 512, 1024], P('ep')
- dy_tokens: bfloat16 [49152, 1024], P(('dp', 'ep'))
Outputs:
- output 1: bfloat16 [49152, 1024], P(('dp', 'ep'))
- output 2: float32 [], replicated
- output 3: bfloat16 [49152, 1024], P(('dp', 'ep'))
- output 4: float32 [1024, 32], replicated
- output 5: bfloat16 [32, 1024, 512], P('ep')
- output 6: bfloat16 [32, 1024, 512], P('ep')
- output 7: bfloat16 [32, 512, 1024], P('ep')
All inputs are finite; a program needn't handle non-finite values.
Results may differ from a plain program's by a relative error of at most 0.012767.
Values are sent between devices in bfloat16 or wider.
A program may use at most 1 GiB of HBM per device.

v0:
```python
import functools

import jax
import jax.numpy as jnp
import numpy as np
from jax import lax
from jax.experimental import pallas as pl
from jax.experimental.pallas import tpu as pltpu
from jax.sharding import PartitionSpec as P


AUX_COEF = 0.01
BLK = 256
TILE = 256
WIN = 128
LANES = 128
ALIGN = 16
NOT_KEPT = -65536.0
VMEM_LIMIT = 63 * 1024 * 1024
CORE, X, Y = 1, 2, 4
FAR = X | Y
HALVES = TENSORS = range(2)
RING = 4
SOURCES = range(8)
FIRST, LAST = 0, -1
SEND, RECV = 0, 1
STAGES = 3
SLOTS = 16
SPLIT = range(4)
LAG = 3
MESH = pl.DeviceIdType.MESH

WHOLE, PARTS = (0, 6), ((0, 3), (3, 3))
GROUPS = (
    [(src, *WHOLE) for src in (FIRST, CORE)],
    [(bit | core, *PARTS[FIRST]) for bit in (X, Y) for core in (FIRST, CORE)],
    [(bit | core, *PARTS[1]) for bit in (X, Y) for core in (FIRST, CORE)],
    [(FAR | core, *part) for part in PARTS for core in (FIRST, CORE)],
)


f32 = jnp.float32
bf16 = jnp.bfloat16
i32 = jnp.int32
ANY = pl.BlockSpec(memory_space=pl.ANY)
SMEM = pl.BlockSpec(memory_space=pltpu.SMEM)
VMEM = pl.BlockSpec(memory_space=pltpu.VMEM)
DMA = pltpu.SemaphoreType.DMA
Shape = jax.ShapeDtypeStruct


def capacity_of(tokens, top_k, experts):
    return (5 * top_k * tokens + 4 * experts - 1) // (4 * experts)


def dot(a, b, ca=1, cb=0):
    return lax.dot_general(a, b, (((ca,), (cb,)), ((), ())), preferred_element_type=f32)


def dot_nt(a, b):
    return dot(a, b, 1, 1)


def dot_tn(a, b):
    return dot(a, b, 0, 0)


def grid_params(dims):
    return pltpu.CompilerParams(dimension_semantics=("arbitrary",) * dims, vmem_limit_bytes=VMEM_LIMIT)


def params():
    return grid_params(1)


def cost(flops, moved):
    return pl.CostEstimate(flops=flops, bytes_accessed=moved, transcendentals=FIRST)


def iota(shape, dim):
    return lax.broadcasted_iota(i32, shape, dim)


def span(start, size, multiple=None):
    return pl.ds(pl.multiple_of(start, multiple or size), size)


def lane_sum(v):
    return jnp.sum(v, axis=1, keepdims=True)


def row_sum(v):
    return jnp.sum(v, axis=0, keepdims=True)


def where0(mask, v):
    return jnp.where(mask, v, jnp.zeros_like(v))


def one_hot(mask):
    return jnp.where(mask, 1.0, 0.0).astype(bf16)


def split3(v):
    hi = v.astype(bf16)
    rest = v - hi.astype(f32)
    mid = rest.astype(bf16)
    return hi, mid, (rest - mid.astype(f32)).astype(bf16)


def loop(start, stop, body):
    def step(i, carry):
        body(i)
        return carry

    lax.fori_loop(start, stop, step, FIRST)


def chosen_mask(ids, experts):
    rows = iota((experts, ids.shape[1]), FIRST)
    return functools.reduce(jnp.logical_or, [rows == ids[j : j + 1, :] for j in range(ids.shape[FIRST])])


def router_kernel(capacity, local, x_ref, w_ref, ids_ref, tab_ref, prob_ref, carry):
    step = pl.program_id(FIRST)
    steps = pl.num_programs(FIRST)
    experts = w_ref.shape[1]

    @pl.when(step == FIRST)
    def _():
        carry[...] = jnp.zeros_like(carry)
        tab_ref[...] = jnp.zeros_like(tab_ref)

    x = x_ref[...]
    hi, mid, low = [dot(x, part) for part in split3(w_ref[...])]
    logits = jnp.transpose(hi + (mid + low))
    expo = jnp.exp(logits - jnp.max(logits, axis=FIRST, keepdims=True))
    prob = expo / row_sum(expo)
    chosen = chosen_mask(ids_ref[...], experts)
    hits = jnp.where(chosen, 1.0, 0.0)
    gate = where0(chosen, prob / row_sum(where0(chosen, prob)))
    earlier = one_hot(iota((BLK, BLK), FIRST) < iota((BLK, BLK), 1))
    before = carry[:, :1]
    pos = dot(hits.astype(bf16), earlier) + before
    pos = jnp.where(chosen & (pos < capacity), pos, NOT_KEPT)
    prob_ref[...] = prob
    after = before + lane_sum(hits)
    lane = iota((experts, LANES), 1)
    first = where0(lane == step, jnp.minimum(before, capacity) + jnp.zeros((experts, LANES), f32))
    first = first + where0((lane == step + 1) & (step == steps - 1), jnp.minimum(after, capacity) + jnp.zeros((experts, LANES), f32))
    stat = where0(lane == FIRST, lane_sum(hits) + jnp.zeros((experts, LANES), f32))
    stat = stat + where0(lane == 1, lane_sum(prob) + jnp.zeros((experts, LANES), f32))
    tail = slice(tab_ref.shape[LAST] - LANES, None)
    for d in range(experts // local):
        rows = slice(d * local, (d + 1) * local)
        tab_ref[d, :local, span(step * BLK, BLK)] = gate[rows]
        tab_ref[d, local:, span(step * BLK, BLK)] = pos[rows]
        tab_ref[d, :local, tail] += stat[rows]
        tab_ref[d, local:, tail] += first[rows]
    carry[:, :1] = after


def run_router(x_loc, w_router, ids_t, capacity, local, devices):
    tokens, d_model = x_loc.shape
    experts = w_router.shape[1]
    top_k = ids_t.shape[FIRST]
    table = (devices, 2 * local, tokens + LANES)
    return pl.pallas_call(
        functools.partial(router_kernel, capacity, local),
        grid=(tokens // BLK,),
        in_specs=[pl.BlockSpec((BLK, d_model), lambda i: (i, FIRST)), VMEM, pl.BlockSpec((top_k, BLK), lambda i: (FIRST, i))],
        out_specs=[VMEM, pl.BlockSpec((experts, BLK), lambda i: (FIRST, i))],
        out_shape=[Shape(table, f32), Shape((experts, tokens), f32)],
        scratch_shapes=[pltpu.VMEM((experts, LANES), f32)],
        compiler_params=params(),
        cost_estimate=cost(2 * tokens * d_model * BLK, 2 * tokens * d_model),
        name="router",
    )(x_loc, w_router, ids_t)


class Blocks:
    def __init__(self, starts_ref, bmap_ref):
        self.starts, self.bmap = starts_ref, bmap_ref

    def info(self, i, e):
        at = self.bmap[2 * i + 1] + e * ALIGN
        first = self.starts[at]
        return self.bmap[2 * i], first, self.starts[at + 1] - first

    def total(self, start, count, e):
        return lax.fori_loop(start, start + count, lambda i, n: n + self.info(i, e)[LAST], i32(FIRST))


def aligned(row):
    base = (row // ALIGN) * ALIGN
    return base, row - base


def window_count(shift, count):
    return (shift + count + WIN - 1) // WIN


def padded(total):
    return (total + TILE - 1) // TILE * TILE


def row_tiles(total, body, size):
    tiles = (total + size - 1 - size // 2) // size
    loop(FIRST, tiles, lambda i: body(i * size, size))
    pl.when(padded(total) > tiles * size)(lambda: body(tiles * size, size // 2))


def start(copies):
    for cp in copies:
        cp.start()


def wait(copies):
    for cp in copies:
        cp.wait()


def taker(refs):
    refs = list(refs)

    def take(n=None):
        got = refs[:n]
        del refs[:n]
        return got

    return take


def block_count(pieces):
    return sum(count for _, _, count in pieces)


def offsets(pieces):
    counts = [count for _, _, count in pieces]
    return [(sum(counts[:k]), count) for k, count in enumerate(counts)]


def block_rows(first, count):
    return pl.ds(first * BLK, count * BLK)


def grad_kernel(g, last, local, pieces, *refs):
    take = taker(refs)
    n = len(pieces)
    starts_ref, bmap_ref, tab_ref = take(3)
    tok_refs = take(n), take(n)
    w1_ref, w3_ref, w2_ref = take(3)
    acc_in = take(2 * bool(g))
    take(3 * bool(g))
    row_outs = take(3)
    outs = take(3 if last else 2)
    xv, dv, xr, dr, acc13, acc2, stage, tok_sem, in_sem, out_sem, row_sem = take()
    accs = acc13, acc2
    e = pl.program_id(FIRST)
    slot = e % 2
    d_model = xv.shape[1]
    d_ff = w1_ref.shape[LAST]
    blocks = Blocks(starts_ref, bmap_ref)
    count = xv.shape[FIRST] // BLK

    parts = [(c, at, first + at) for c, (first, size) in enumerate(offsets(pieces)) for at in range(FIRST, size, 3)]

    def token_copies(k):
        c, at, to = parts[k]
        src_rows, dst_rows = block_rows(at, 3), block_rows(to, 3)
        return [pltpu.make_async_copy(src[c].at[src_rows], dst.at[dst_rows], tok_sem.at[w, k]) for w, (src, dst) in enumerate(zip(tok_refs, (xv, dv)))]

    def in_copies(ee, ss):
        return [pltpu.make_async_copy(src.at[ee], dst.at[ss], in_sem.at[ss, k]) for k, (src, dst) in enumerate(zip(acc_in, accs))]

    def out_copies(ee, ss):
        return [pltpu.make_async_copy(src.at[ss], dst.at[ee], out_sem.at[ss, k]) for k, (src, dst) in enumerate(zip(accs, outs))]

    @pl.when(e == FIRST)
    def _():
        for k in range(len(parts)):
            start(token_copies(k))

    if g:
        pl.when(e == FIRST)(lambda: start(in_copies(e, slot)))
    else:
        pl.when(e >= 2)(lambda: wait(out_copies(e - 2, slot)))
        for acc in accs:
            acc[slot] = jnp.zeros(acc.shape[1:], f32)

    def prefetch():
        if not last:
            pl.when(e > FIRST)(lambda: wait(out_copies(e - 1, 1 - slot)))
        start(in_copies(e + 1, 1 - slot))

    def maybe_prefetch(now):
        if g:
            pl.when(now & (e + 1 < local))(prefetch)

    row_iota = iota((WIN, BLK), FIRST).astype(f32)
    head_row = iota((ALIGN, d_model), FIRST)
    both = tuple(HALVES)

    def dispatch(i, rows_at):
        for k, (_, _, first) in enumerate(parts):
            pl.when((e == FIRST) & (i == first))(lambda: wait(token_copies(k)))
        tok = span(i * BLK, BLK)
        infos = [blocks.info(i, e + q) for q in both]
        places = [aligned(r) for r in rows_at]
        flat = infos[FIRST][FIRST]

        def picks(q, k):
            pos = tab_ref[flat, pl.ds(local + e + q, 1), :]
            gate = tab_ref[flat, pl.ds(e + q, 1), :]
            pick = (pos + (places[q][1] - infos[q][1] - k * WIN).astype(f32)) == row_iota
            return one_hot(pick), lane_sum(where0(pick, gate + jnp.zeros_like(row_iota)))

        def rows_for(one, gate_row):
            return dot(one, xv[tok, :]).astype(bf16), (dot(one, dv[tok, :]) * gate_row).astype(bf16)

        pair = [picks(q, i32(FIRST)) for q in both]
        new = rows_for(*[jnp.concatenate(v, axis=FIRST) for v in zip(*pair)])
        for q in both:
            base, shift = places[q]
            head = span(base, ALIGN)
            for value, rows in zip(new, (xr, dr)):
                value = value[q * WIN : (q + 1) * WIN]
                rows[q, head, :] = jnp.where(head_row < shift, rows[q, head, :], value[:ALIGN])
                rows[q, span(base + ALIGN, WIN - ALIGN, ALIGN), :] = value[ALIGN:]

            def more(k):
                for value, rows in zip(rows_for(*picks(q, k)), (xr, dr)):
                    rows[q, span(base + k * WIN, WIN, ALIGN), :] = value

            loop(1, window_count(shift, infos[q][LAST]), more)
        return tuple(r + info[LAST] for r, info in zip(rows_at, infos))

    @pl.when(slot == FIRST)
    def _():
        totals = lax.fori_loop(FIRST, count, dispatch, (i32(FIRST),) * len(both))
        for q in both:

            def clear(i):
                for rows in (xr, dr):
                    rows[q, span(i * ALIGN, ALIGN), :] = jnp.zeros((ALIGN, d_model), bf16)

            loop((totals[q] + ALIGN - 1) // ALIGN, padded(totals[q]) // ALIGN, clear)

    wait(in_copies(e, slot))

    def tile(at, size):
        maybe_prefetch(at == FIRST)
        rows = span(at, size)
        xt = xr[slot, rows, :]
        dt = dr[slot, rows, :]
        act_a = dot(xt, w1_ref[FIRST])
        act_b = dot(xt, w3_ref[FIRST])
        d_hidden = dot_nt(dt, w2_ref[FIRST]).astype(bf16).astype(f32)
        sig = 1.0 / (1.0 + jnp.exp(-act_a))
        silu = act_a * sig
        hidden = (silu * act_b).astype(bf16)
        d_a = (d_hidden * act_b * sig * (1.0 + act_a * (1.0 - sig))).astype(bf16)
        d_b = (d_hidden * silu).astype(bf16)
        copies = []
        for k, (value, out) in enumerate(zip((hidden, d_a, d_b), row_outs)):
            stage[k, :size] = value
            copies.append(pltpu.make_async_copy(stage.at[k, :size], out.at[g, e, rows], row_sem.at[k]))
        start(copies)
        acc13[slot, :, :d_ff] += dot_tn(xt, d_a)
        acc13[slot, :, d_ff:] += dot_tn(xt, d_b)
        acc2[slot] += dot_tn(hidden, dt)
        wait(copies)

    total = blocks.total(FIRST, count, e)
    maybe_prefetch(total == FIRST)
    row_tiles(total, tile, 2 * TILE)

    if last:
        for out, value in zip(outs, (acc13[slot, :, :d_ff], acc13[slot, :, d_ff:], acc2[slot])):
            out[FIRST] = value.astype(bf16)
    else:
        start(out_copies(e, slot))

        @pl.when(e == pl.num_programs(FIRST) - 1)
        def _():
            wait(out_copies(e - 1, 1 - slot))
            wait(out_copies(e, slot))


def per_expert(*shape):
    return pl.BlockSpec((1, *shape), lambda e: (e,) + (FIRST,) * len(shape))


def block_map(pieces, nb):
    spots = [(src, first + b) for src, first, count in pieces for b in range(count)]
    return np.asarray([v for src, b in spots for v in (src * nb + b, src * 4 * ALIGN + b)], np.int32)


def run_grad(starts, tab, g, xs, ds, weights, acc, rows, nb, row_cap):
    pieces = GROUPS[g]
    last = g == len(GROUPS) - 1
    local, d_model, d_ff = weights[FIRST].shape
    count = block_count(pieces) * BLK
    w_specs = [per_expert(*w.shape[1:]) for w in weights]
    sums = [(local, d_model, 2 * d_ff), (local, d_ff, d_model)]
    row_shape = [Shape((len(GROUPS), local, row_cap, d_ff), bf16)] * 3
    out_shape = row_shape + ([Shape(w.shape, bf16) for w in weights] if last else [Shape(s, f32) for s in sums])
    out_specs = [ANY] * 3 + (w_specs if last else [ANY] * 2)
    tokens = pltpu.VMEM((count, d_model), bf16)
    packed = pltpu.VMEM((2, row_cap + WIN, d_model), bf16)
    ins = [starts, block_map(pieces, nb), tab, *xs, *ds, *weights, *acc, *rows]
    out = pl.pallas_call(
        functools.partial(grad_kernel, g, last, local, pieces),
        grid=(local,),
        in_specs=[SMEM, SMEM, VMEM] + [ANY] * (2 * len(pieces)) + w_specs + [ANY] * (len(acc) + len(rows)),
        out_specs=out_specs,
        out_shape=out_shape,
        scratch_shapes=[tokens, tokens, packed, packed]
        + [pltpu.VMEM((2, *s[1:]), f32) for s in sums]
        + [pltpu.VMEM((3, 2 * TILE, d_ff), bf16), DMA((2, count // (3 * BLK))), DMA((2, 2)), DMA((2, 2)), DMA((3,))],
        input_output_aliases={len(ins) - len(rows) + k: k for k in range(len(rows))},
        compiler_params=params(),
        cost_estimate=cost(12 * count * d_model * d_ff, 40 << 20),
        name="expert_grad",
    )(*ins)
    return out[:3], out[3:]


def group_spans(groups):
    counts = [block_count(GROUPS[g]) for g in groups]
    return np.asarray([v for k, c in enumerate(counts) for v in (sum(counts[:k]), c)], np.int32)


def per_group(groups, *shape):
    return pl.BlockSpec((1, 1, *shape), lambda step, e: (step + groups[FIRST], e) + (FIRST,) * len(shape))


def per_local(*shape):
    return pl.BlockSpec((1, *shape), lambda g, e: (e,) + (FIRST,) * len(shape))


class Combine:
    def __init__(self, local, starts_ref, bmap_ref, spans_ref, tab_ref, rows_ref, out_ref, ring, sems):
        step = pl.program_id(FIRST)
        self.e = pl.program_id(1)
        self.blocks = Blocks(starts_ref, bmap_ref)
        self.first, self.count = spans_ref[2 * step], spans_ref[2 * step + 1]
        self.total = self.blocks.total(self.first, self.count, self.e)
        self.local, self.tab_ref, self.rows_ref = local, tab_ref, rows_ref
        self.out_ref, self.ring, self.sems = out_ref, ring, sems
        self.lane = iota((BLK, WIN), 1).astype(f32)

    def zero_tail(self):
        rows = span(padded(self.total), WIN)
        self.rows_ref[self.e, rows, :] = jnp.zeros((WIN, self.rows_ref.shape[LAST]), bf16)

    def pick(self, ee, k):
        place, info = self.places[ee], self.infos[ee]
        pos = self.tab_t[:, self.local + ee : self.local + ee + 1]
        return one_hot((pos + (place[1] - info[1] - k * WIN).astype(f32)) == self.lane)

    def held(self, ee, k, cols=slice(None)):
        return self.rows_ref[ee, span(self.places[ee][FIRST] + k * WIN, WIN, ALIGN), cols]

    def out_copy(self, i):
        slot = i % RING
        place = self.blocks.bmap[2 * i] - self.blocks.bmap[FIRST]
        return pltpu.make_async_copy(self.ring.at[slot], self.out_ref.at[place], self.sems.at[slot])

    def run(self, simple_body, full_body):
        def block(i, rows_at):
            ee = range(self.local)
            self.infos = [self.blocks.info(i, k) for k in ee]
            self.places = [aligned(r) for r in rows_at]
            self.windows = [window_count(self.places[k][1], self.infos[k][LAST]) for k in ee]
            self.flat = self.infos[FIRST][FIRST]
            self.tab_t = jnp.transpose(self.tab_ref[self.flat])
            self.tok = span((i - self.first) * BLK, BLK)
            pl.when(i - self.first >= RING)(lambda: self.out_copy(i - RING).wait())
            simple = functools.reduce(jnp.logical_and, [w <= 1 for w in self.windows])
            out = self.ring.at[i % RING]
            pl.when(simple)(lambda: simple_body(out))
            pl.when(jnp.logical_not(simple))(lambda: full_body(out))
            self.out_copy(i).start()
            return tuple(r + info[LAST] for r, info in zip(rows_at, self.infos))

        stop = self.first + self.count
        lax.fori_loop(self.first, stop, block, (i32(FIRST),) * self.local)
        loop(stop - RING, stop, lambda i: self.out_copy(i).wait())


def y_kernel(groups, local, starts_ref, bmap_ref, spans_ref, tab_ref, h_ref, w2_ref, *refs):
    take = taker(refs)
    d_refs = [take(len(GROUPS[g])) for g in groups]
    y_ref, dg_ref, o_rows, dv, ring, zacc, yacc, dgacc, tok_sem, out_sem = take()
    all_rows = Combine(local, starts_ref, bmap_ref, spans_ref, tab_ref, o_rows, y_ref, ring, out_sem)
    e = all_rows.e
    d_model = dv.shape[1]

    def token_copies(step):
        spots = offsets(GROUPS[groups[step]])
        return [pltpu.make_async_copy(src, dv.at[block_rows(*spot)], tok_sem.at[c]) for c, (src, spot) in enumerate(zip(d_refs[step], spots))]

    for step in range(len(groups)):
        pl.when((pl.program_id(FIRST) == step) & (e == FIRST))(lambda: start(token_copies(step)))

    def tile(at, size):
        rows = span(at, size)
        o_rows[e, rows, :] = dot(h_ref[FIRST, FIRST, rows, :], w2_ref[FIRST]).astype(bf16)

    row_tiles(all_rows.total, tile, 2 * TILE)
    all_rows.zero_tail()

    @pl.when(e == local - 1)
    def _():
        for step in range(len(groups)):
            pl.when(pl.program_id(FIRST) == step)(lambda: wait(token_copies(step)))
        dg_lane = iota((BLK, LANES), 1)
        width = 2 * LANES
        columns = [slice(k * width, (k + 1) * width) for k in range(d_model // width)]

        def gate(ee):
            return all_rows.tab_t[:, ee : ee + 1]

        def put_dg(sums):
            dg = sum(where0(dg_lane == ee, lane_sum(s) + jnp.zeros((BLK, LANES), f32)) for ee, s in enumerate(sums))
            dg_ref[all_rows.flat - all_rows.blocks.bmap[FIRST]] = jnp.transpose(dg)[: 2 * local, :]

        def simple(out):
            picks = [all_rows.pick(ee, i32(FIRST)) for ee in range(local)]
            sums = [None] * local
            for cols in columns:
                dy = dv[all_rows.tok, cols].astype(f32)
                y = None
                for ee in range(local):
                    z = dot(picks[ee], all_rows.held(ee, i32(FIRST), cols))
                    prod = dy * z
                    part = prod[:, :LANES] + prod[:, LANES:]
                    sums[ee] = part if sums[ee] is None else sums[ee] + part
                    y = gate(ee) * z if y is None else y + gate(ee) * z
                out[:, cols] = y.astype(bf16)
            put_dg(sums)

        def full(out):
            yacc[...] = jnp.zeros_like(yacc)
            for ee in range(local):
                zacc[...] = jnp.zeros_like(zacc)

                def more(k):
                    zacc[...] += dot(all_rows.pick(ee, k), all_rows.held(ee, k))

                loop(FIRST, all_rows.windows[ee], more)
                yacc[...] += gate(ee) * zacc[...]
                dgacc[ee] = lane_sum(dv[all_rows.tok, :].astype(f32) * zacc[...]) * jnp.where(dg_lane == FIRST, 1.0, 0.0)
            out[...] = yacc[...].astype(bf16)
            put_dg([dgacc[ee] for ee in range(local)])

        all_rows.run(simple, full)


def combine_scratch(local, row_cap, d_model):
    return [pltpu.VMEM((local, row_cap + WIN, d_model), bf16)], [pltpu.VMEM((RING, BLK, d_model), bf16), pltpu.VMEM((BLK, d_model), f32)]


def run_y(groups, starts, tab, h_rows, w2, ds, nb):
    local, d_ff, d_model = w2.shape
    row_cap = h_rows.shape[2]
    pieces = [p for g in groups for p in GROUPS[g]]
    spans = group_spans(groups)
    blocks = block_count(pieces)
    rows, work = combine_scratch(local, row_cap, d_model)
    return pl.pallas_call(
        functools.partial(y_kernel, groups, local),
        grid=(len(groups), local),
        in_specs=[SMEM, SMEM, SMEM, VMEM, per_group(groups, row_cap, d_ff), per_local(d_ff, d_model)] + [ANY] * len(pieces),
        out_specs=[ANY, VMEM],
        out_shape=[Shape((blocks, BLK, d_model), bf16), Shape((blocks, 2 * local, BLK), f32)],
        scratch_shapes=rows + [pltpu.VMEM((max(spans[1::2]) * BLK, d_model), bf16)] + work + [work[LAST], pltpu.VMEM((local, BLK, LANES), f32), DMA((4,)), DMA((RING,))],
        compiler_params=grid_params(2),
        cost_estimate=cost(4 * blocks * BLK * d_model * d_ff, 20 << 20),
        name="expert_y",
    )(starts, block_map(pieces, nb), spans, tab, h_rows, w2, *[ds[p] for p in pieces])


def dx_kernel(local, starts_ref, bmap_ref, spans_ref, tab_ref, da_ref, db_ref, w1_ref, w3_ref, dx_ref, o_rows, ring, zacc, out_sem):
    all_rows = Combine(local, starts_ref, bmap_ref, spans_ref, tab_ref, o_rows, dx_ref, ring, out_sem)
    e = all_rows.e

    def tile(at, size):
        rows = span(at, size)
        grad = dot_nt(da_ref[FIRST, FIRST, rows, :], w1_ref[FIRST]) + dot_nt(db_ref[FIRST, FIRST, rows, :], w3_ref[FIRST])
        o_rows[e, rows, :] = grad.astype(bf16)

    row_tiles(all_rows.total, tile, 2 * TILE)
    all_rows.zero_tail()

    @pl.when(e == local - 1)
    def _():
        def simple(out):
            pairs = [(ee, ee + 1) for ee in range(FIRST, local, 2)]
            zero = i32(FIRST)
            sums = [
                dot(jnp.concatenate([all_rows.pick(ee, zero) for ee in pair], axis=1), jnp.concatenate([all_rows.held(ee, zero) for ee in pair], axis=FIRST))
                for pair in pairs
            ]
            out[...] = sum(sums[1:], sums[FIRST]).astype(bf16)

        def full(out):
            zacc[...] = jnp.zeros_like(zacc)
            for ee in range(local):

                def more(k):
                    zacc[...] += dot(all_rows.pick(ee, k), all_rows.held(ee, k))

                loop(FIRST, all_rows.windows[ee], more)
            out[...] = zacc[...].astype(bf16)

        all_rows.run(simple, full)


def run_dx(groups, starts, tab, da_rows, db_rows, w1, w3, nb):
    local, d_model, d_ff = w1.shape
    row_cap = da_rows.shape[2]
    pieces = [p for g in groups for p in GROUPS[g]]
    blocks = block_count(pieces)
    rows, work = combine_scratch(local, row_cap, d_model)
    return pl.pallas_call(
        functools.partial(dx_kernel, local),
        grid=(len(groups), local),
        in_specs=[SMEM, SMEM, SMEM, VMEM] + [per_group(groups, row_cap, d_ff)] * 2 + [per_local(d_model, d_ff)] * 2,
        out_specs=ANY,
        out_shape=Shape((blocks, BLK, d_model), bf16),
        scratch_shapes=rows + work + [DMA((RING,))],
        compiler_params=grid_params(2),
        cost_estimate=cost(6 * blocks * BLK * d_model * d_ff, 20 << 20),
        name="expert_dx",
    )(starts, block_map(pieces, nb), group_spans(groups), tab, da_rows, db_rows, w1, w3)


def router_grad_kernel(scale, x_ref, prob_ref, dg_ref, ids_ref, load_ref, dlog_ref, dw_ref):
    step = pl.program_id(FIRST)
    prob = prob_ref[...]
    dg = dg_ref[...]
    chosen = chosen_mask(ids_ref[...], prob.shape[FIRST])
    gate_sum = row_sum(where0(chosen, prob))
    gate = where0(chosen, prob / gate_sum)
    d_pick = (dg - row_sum(gate * dg)) / gate_sum
    d_prob = where0(chosen, d_pick) + scale * load_ref[:, :1]
    d_logit = prob * (d_prob - row_sum(prob * d_prob))
    dlog_ref[...] = d_logit
    hi, mid, low = [dot(part, x_ref[...]) for part in split3(d_logit)]

    @pl.when(step == FIRST)
    def _():
        dw_ref[...] = jnp.zeros_like(dw_ref)

    dw_ref[...] += hi + (mid + low)


def run_router_grad(x_loc, prob_t, dg_t, ids_t, load, scale):
    tokens, d_model = x_loc.shape
    experts = prob_t.shape[FIRST]
    lanes = lambda n: pl.BlockSpec((n, BLK), lambda i: (FIRST, i))
    return pl.pallas_call(
        functools.partial(router_grad_kernel, scale),
        grid=(tokens // BLK,),
        in_specs=[pl.BlockSpec((BLK, d_model), lambda i: (i, FIRST)), lanes(experts), lanes(experts), lanes(ids_t.shape[FIRST]), VMEM],
        out_specs=[lanes(experts), VMEM],
        out_shape=[Shape((experts, tokens), f32), Shape((experts, d_model), f32)],
        compiler_params=params(),
        cost_estimate=cost(2 * tokens * d_model * BLK, 2 * tokens * d_model),
        name="router_grad",
    )(x_loc, prob_t, dg_t, ids_t, load)


def final_kernel(dlog_ref, wt_ref, *refs):
    take = taker(refs)
    y_terms, dx_terms = [[ref[...].astype(f32) for ref in take(3)] for _ in TENSORS]
    y_ref, dx_ref = take()
    lhs = split3(dlog_ref[...])
    rhs = split3(wt_ref[...])
    terms = [(i, j) for i in range(3) for j in range(3 - i)]
    left = jnp.concatenate([lhs[i] for i, _ in terms], axis=FIRST)
    right = jnp.concatenate([rhs[j] for _, j in terms], axis=FIRST)
    dx_ref[...] = (dot_tn(left, right) + sum(dx_terms[1:], dx_terms[FIRST])).astype(bf16)
    y_ref[...] = sum(y_terms[1:], y_terms[FIRST]).astype(bf16)


def run_final(dlog_t, w_t, y_terms, dx_terms):
    experts, tokens = dlog_t.shape
    d_model = w_t.shape[1]
    size = tokens // 4
    rows = pl.BlockSpec((size, d_model), lambda i: (i, FIRST))
    return pl.pallas_call(
        final_kernel,
        grid=(tokens // size,),
        in_specs=[pl.BlockSpec((experts, size), lambda i: (FIRST, i)), VMEM] + [rows] * len([*y_terms, *dx_terms]),
        out_specs=[rows] * 2,
        out_shape=[Shape((tokens, d_model), bf16)] * 2,
        compiler_params=params(),
        cost_estimate=cost(2 * tokens * d_model * BLK, 16 * tokens * d_model),
        name="final",
    )(dlog_t, w_t, *y_terms, *dx_terms)


NEAR = (X, Y)
RELAYED = {(Y, 0): 0, (X, 1): 1}
OPS = [
    (t, src, h)
    for step in ([(FAR, 0), (FAR, 1)], [(X, 0), (Y, 1)], [(X, 1), (Y, 0)], [(FIRST, 0), (FIRST, 1)])
    for t in TENSORS
    for src, h in step
]


def add_rows(dst, src):
    step = min(LANES, dst.shape[FIRST])

    def body(i):
        rows = span(i * step, step)
        dst[rows, :] = (dst[rows, :].astype(f32) + src[rows, :].astype(f32)).astype(bf16)

    loop(FIRST, dst.shape[FIRST] // step, body)


def exchange_kernel(half, mats, *refs):
    take = taker(refs)
    parts = [take(2) for _ in TENSORS]
    dws = take(mats)
    outs = [take(len(NEAR) + 1) for _ in TENSORS]
    dw_outs = take(mats)
    land, far_land, stage, z_one, z_two, z_stage = take(6)
    core_sem, stage_sem, far_sem, near_sem, own_sem, z_sem, keep_sem, load_sem, credit_one, credit_two = take()

    me = lax.axis_index("ep")
    z = lax.axis_index("dp")
    peer = {bit: me + bit - 2 * bit * ((me // bit) % 2) for bit in (CORE, X, Y)}
    z_peer = z + 1 - 2 * (z % 2)
    z_cross = 3 - z
    is_end = (z % 3) == FIRST
    is_mid = (z % 3) != FIRST

    barrier = pltpu.get_barrier_semaphore()
    ids = [{"ep": p} for p in peer.values()] + [{"dp": z_peer}, {"dp": z_cross}]
    for device in ids:
        pl.semaphore_signal(barrier, device_id=device, device_id_type=MESH)
    pl.semaphore_wait(barrier, len(ids))

    def remote(src, dst, sems, at, device):
        send, recv = sems.at[(SEND, *at)], sems.at[(RECV, *at)]
        return pltpu.make_async_remote_copy(src_ref=src, dst_ref=dst, send_sem=send, recv_sem=recv, device_id=device, device_id_type=MESH)

    def rows_at(h):
        return pl.ds(h * half, half)

    def part(t, src, h):
        own, rest = parts[t]
        return own.at[src, rows_at(h)] if src <= CORE else rest.at[src - 2, rows_at(h)]

    def core_copy(i):
        t, src, h = OPS[i]
        return remote(part(t, src | CORE, h), land.at[i], core_sem, (i,), {"ep": peer[CORE]})

    def stage_copy(i):
        t, src, h = OPS[i]
        return pltpu.make_async_copy(part(t, src, h), stage.at[i % STAGES], stage_sem.at[i % STAGES])

    def far_copy(i):
        t, _, h = OPS[i]
        return remote(land.at[i], far_land.at[t, h], far_sem, (t, h), {"ep": peer[NEAR[h]]})

    def near_copy(i):
        t, src, h = OPS[i]
        k = NEAR.index(src)
        return remote(land.at[i], outs[t][k].at[rows_at(h)], near_sem, (t, k, h), {"ep": peer[src]})

    def own_copy(i):
        t, _, h = OPS[i]
        return pltpu.make_async_copy(land.at[i], outs[t][LAST].at[rows_at(h)], own_sem.at[t, h])

    def out_copy(i):
        src = OPS[i][1]
        return (far_copy if src == FAR else near_copy if src else own_copy)(i)

    def reduce_op(i):
        t, src, h = OPS[i]
        stage_copy(i).wait()
        core_copy(i).wait_recv()
        add_rows(land.at[i], stage.at[i % STAGES])
        if i + STAGES < len(OPS):
            stage_copy(i + STAGES).start()
        if (src, h) in RELAYED:
            far_copy(OPS.index((t, FAR, RELAYED[src, h]))).wait_recv()
            add_rows(land.at[i], far_land.at[t, RELAYED[src, h]])

    rows_per = z_one.shape[1]
    chunks = [(m, e, k) for e in range(dws[FIRST].shape[FIRST]) for m in range(mats) for k in SPLIT]
    n = len(chunks)

    def piece(arrays, c):
        m, e, k = chunks[c]
        return arrays[m].at[e, pl.ds(k * rows_per, rows_per)]

    def one_copy(c):
        return remote(piece(dws, c), z_one.at[c % SLOTS], z_sem, (FIRST, c), {"dp": z_peer})

    def two_copy(c):
        return remote(z_one.at[c % SLOTS], z_two.at[c % SLOTS], z_sem, (1, c), {"dp": z_cross})

    def three_copy(c):
        return remote(z_two.at[c % SLOTS], piece(dw_outs, c), z_sem, (2, c), {"dp": z_peer})

    def keep_copy(c):
        return pltpu.make_async_copy(z_two.at[c % SLOTS], piece(dw_outs, c), keep_sem.at[c])

    def load_copy(c):
        return pltpu.make_async_copy(piece(dws, c), z_stage.at[c % STAGES], load_sem.at[c % STAGES])

    def first_add(c):
        load_copy(c).wait()
        one_copy(c).wait_recv()
        add_rows(z_one.at[c % SLOTS], z_stage.at[c % STAGES])
        if c + STAGES < n:
            load_copy(c + STAGES).start()

    def second_add(c):
        two_copy(c).wait()
        add_rows(z_two.at[c % SLOTS], z_one.at[c % SLOTS])
        if c + SLOTS < n:
            pl.semaphore_signal(credit_one, device_id={"dp": z_peer}, device_id_type=MESH)

    def retire(c):
        three_copy(c).wait_send()
        keep_copy(c).wait()
        if c + SLOTS < n:
            pl.semaphore_signal(credit_two, device_id={"dp": z_cross}, device_id_type=MESH)

    @pl.when(is_end)
    def _():
        for c in range(SLOTS):
            one_copy(c).start()

    @pl.when(is_mid)
    def _():
        for c in range(STAGES):
            load_copy(c).start()

    for i in range(len(OPS)):
        core_copy(i).start()
        if i < STAGES:
            stage_copy(i).start()

    todo = list(range(len(OPS)))
    for tick in range(n + LAG):
        mine = todo[: 2 if tick < 2 else tick % 2]
        todo = todo[len(mine) :]
        for i in mine:
            reduce_op(i)

        @pl.when(is_mid)
        def _():
            back = tick - 1
            if tick < n:
                first_add(tick)
            if back in range(n):
                second_add(back)
            if tick < n:
                if tick >= SLOTS:
                    pl.semaphore_wait(credit_two, 1)
                two_copy(tick).start()
            if back in range(n):
                three_copy(back).start()
                keep_copy(back).start()
            if tick >= LAG:
                retire(tick - LAG)

        for i in mine:
            out_copy(i).start()

        @pl.when(is_end)
        def _():
            if tick + SLOTS < n:
                pl.semaphore_wait(credit_one, 1)
                one_copy(tick + SLOTS).start()

    for i in todo:
        reduce_op(i)
        out_copy(i).start()

    @pl.when(is_end)
    def _():
        for c in range(n):
            one_copy(c).wait_send()
            three_copy(c).wait_recv()

    for i in range(len(OPS)):
        core_copy(i).wait_send()
        (out_copy(i).wait_send if OPS[i][1] == FAR else out_copy(i).wait)()


def run_exchange(parts, dws):
    tokens, d_model = parts[FIRST][FIRST].shape[1:]
    half = tokens // 2
    local, rows, cols = dws[FIRST].shape
    chunk = (rows // len(SPLIT), cols)
    n = local * len(dws) * len(SPLIT)
    whole = Shape((tokens, d_model), bf16)
    flat = [v for tensor in parts for v in tensor] + list(dws)
    terms = len(NEAR) + 1
    out = pl.pallas_call(
        functools.partial(exchange_kernel, half, len(dws)),
        in_specs=[ANY] * len(flat),
        out_specs=[ANY] * (terms * len(TENSORS) + len(dws)),
        out_shape=[whole] * (terms * len(TENSORS)) + [Shape(v.shape, bf16) for v in dws],
        scratch_shapes=[
            pltpu.VMEM((len(OPS), half, d_model), bf16),
            pltpu.VMEM((len(TENSORS), len(HALVES), half, d_model), bf16),
            pltpu.VMEM((STAGES, half, d_model), bf16),
            pltpu.VMEM((SLOTS, *chunk), bf16),
            pltpu.VMEM((SLOTS, *chunk), bf16),
            pltpu.VMEM((STAGES, *chunk), bf16),
            DMA((2, len(OPS))),
            DMA((STAGES,)),
            DMA((2, 2, 2)),
            DMA((2, 2, 2, 2)),
            DMA((2, 2)),
            DMA((2, 3, n)),
            DMA((n,)),
            DMA((STAGES,)),
            pltpu.SemaphoreType.REGULAR,
            pltpu.SemaphoreType.REGULAR,
        ],
        compiler_params=pltpu.CompilerParams(vmem_limit_bytes=VMEM_LIMIT, collective_id=FIRST, has_side_effects=True),
        cost_estimate=cost(1 << 37, 200 << 20),
        name="exchange",
    )(*flat)
    return [out[:terms], out[terms : 2 * terms]], out[2 * terms :]


def hop(v, bit):
    return lax.ppermute(v, "ep", [(i, i ^ bit) for i in SOURCES])


def after(values, token):
    return lax.optimization_barrier((values, token))[FIRST]


def send_own(v):
    pieces = [v[first * BLK : (first + count) * BLK] for first, count in PARTS]
    got = {(FIRST, *WHOLE): v, (CORE, *WHOLE): hop(v, CORE)}
    for part, piece in zip(PARTS, pieces):
        got.update({(bit, *part): hop(piece, bit) for bit in NEAR})
    return got, pieces


def pass_on(got, h):
    part = PARTS[h]
    got[FAR, *part] = hop(got[(Y, X)[h], *part], NEAR[h])
    for bit in NEAR:
        got[bit | CORE, *part] = hop(got[bit, *part], CORE)


def relative(v, me):
    shape = v.shape
    v = v.reshape((2, 2, 2) + shape[1:])
    for axis, bit in enumerate((Y, X, CORE)):
        v = jnp.where((me & bit) != FIRST, jnp.flip(v, axis), v)
    return v.reshape(shape)


def solution(mesh):
    dp_size = mesh.shape["dp"]
    ep_size = mesh.shape["ep"]
    row_spec = P(("dp", "ep"), None)
    expert_spec = P("ep", None, None)
    whole_spec = P(None, None)

    def per_device(x_loc, w_router, ids_loc, w1, w3, w2, dy_loc):
        tokens, d_model = x_loc.shape
        top_k = ids_loc.shape[1]
        experts = w_router.shape[1]
        local = w1.shape[FIRST]
        capacity = capacity_of(tokens, top_k, experts)
        n_total = tokens * dp_size * ep_size
        nb = tokens // BLK
        row_cap = padded(4 * capacity)
        me = lax.axis_index("ep")

        gathered, pieces = zip(*[send_own(v) for v in (x_loc, dy_loc)])

        ids_t, x_router = after((ids_loc.T, x_loc), pieces)
        send_tab, prob_t = run_router(x_router, w_router, ids_t, capacity, local, ep_size)
        tab_rel = relative(lax.all_to_all(send_tab, "ep", FIRST, FIRST, tiled=True), me)
        tab = tab_rel[:, :, :tokens].reshape(ep_size, 2 * local, nb, BLK).transpose(0, 2, 1, 3).reshape(ep_size * nb, 2 * local, BLK)
        starts = tab_rel[:, local:, tokens : tokens + ALIGN].astype(i32).reshape(LAST)

        def y_of(groups, starts):
            return run_y(groups, starts, tab, rows[FIRST], w2, gathered[1], nb)

        def dx_of(groups, starts):
            return run_dx(groups, starts, tab, rows[1], rows[2], w1, w3, nb)

        acc = rows = ()
        own, rest = (FIRST,), (1, 2, 3)
        for g, group in enumerate(GROUPS):
            if g:
                ready = [p for p in group if not p[FIRST] & CORE]
                for got in gathered:
                    got.update(after({p: got[p] for p in ready}, acc[LAST]))
                for got in gathered:
                    if g < len(GROUPS) - 1:
                        pass_on(got, g - 1)
                    else:
                        for src, *part in ready:
                            got[src | CORE, *part] = hop(got[src, *part], CORE)
                here = after(starts, [[got[p] for p in ready] for got in gathered])
                if g == 2:
                    y_own, dg_own = y_of(own, here)
                    starts = after(starts, dg_own)
                if g > 2:
                    dx_own = dx_of(own, here)
                    starts = after(starts, dx_own)
            rows, acc = run_grad(starts, tab, g, *[[got[p] for p in group] for got in gathered], (w1, w3, w2), acc, rows, nb, row_cap)
            if not g:
                stats = jnp.sum(after(tab_rel[:, :local, tokens:], acc[LAST]), axis=FIRST)
                for step in (1, 2):
                    stats = stats + lax.ppermute(stats, "dp", [(i, i ^ step) for i in range(dp_size)])
                starts = after(starts, stats)
        dw1, dw3, dw2 = acc
        starts, dw2 = lax.optimization_barrier((starts, dw2))
        dw2_sum = lax.psum(dw2, "dp")

        y_rest, dg_rest = y_of(rest, starts)
        dg = jnp.concatenate([dg_own, dg_rest], axis=FIRST)
        dg = dg[:, :local].reshape(ep_size, nb, local, BLK).transpose(0, 2, 1, 3).reshape(ep_size, local, tokens)
        dg = jnp.concatenate([relative(dg, me), jnp.broadcast_to(stats, (ep_size, *stats.shape))], axis=2)
        starts, dg = lax.optimization_barrier((starts, dg))
        dx_rest = dx_of(rest, starts)
        dg_all = lax.all_to_all(dg, "ep", FIRST, FIRST, tiled=True).reshape(experts, tokens + LANES)
        load = dg_all[:, tokens:]
        share = AUX_COEF * experts / (n_total * top_k * n_total)
        aux_loss = share * jnp.sum(load[:, FIRST] * load[:, 1])
        dlog_t, dwr_t = run_router_grad(x_loc, prob_t, dg_all[:, :tokens], ids_t, load, share)
        dw_router = lax.psum(dwr_t, ("dp", "ep")).T

        parts = [[v.reshape(LAST, tokens, d_model) for v in pair] for pair in ((y_own, y_rest), (dx_own, dx_rest))]
        sums, grads = run_exchange(parts, [dw1, dw3])
        y_loc, dx_loc = run_final(dlog_t, w_router.T, *sums)
        return y_loc, aux_loss, dx_loc, dw_router, *grads, dw2_sum

    return jax.shard_map(
        per_device,
        mesh=mesh,
        in_specs=(row_spec, whole_spec, row_spec, expert_spec, expert_spec, expert_spec, row_spec),
        out_specs=(row_spec, P(), row_spec, whole_spec, expert_spec, expert_spec, expert_spec),
        check_vma=False,
    )
```

profile of v0, /device:TPU:0, one launch (start us, length us, event | category | flops | bytes accessed | tf_op | source)
XLA Modules:
  0.0 906.8 jit_solution(4458149830118999539)
XLA Ops:
  7.8 4.1 fusion.1
  14.9 7.6 router.1
  22.6 5.1 all-to-all-start
  31.8 5.2 all-to-all-done
  39.0 48.7 %expert_grad.4 = (bf16[4,4,2048,512]{3,2,1,0:T(8,128)(2,1)}, bf16[4,4,2048,512]{3,2,1,0:T(8,128)(2,1)}, bf16[4,4,2048,512]{3,2,1,0:T(8,128)(2,1)}, f32[4,1024,1024]{2,1,0:T(8,128)}, f32[4,512,1024]{2,1,0:T(8,128)}) custom-call(s32[512]{0:T(512)} %reshape.53.refs_0_.starts_ref, s32[24]{0:T(128)} %constant.31.clone.refs_1_.bmap_ref, f32[48,8,256]{2,1,0:T(8,128)} %bitcast.20, ...), custom_call_target="tpu_custom_call" | custom-call | flops 19327352832 | bytes 41943040 | tf_op jit(solution)/shard_map/expert_grad/pallas_call | solution.py:412
  88.8 14.2 %collective-permute-done.6.refs_3_ = bf16[768,1024]{1,0:T(8,128)(2,1)} collective-permute-done((bf16[768,1024]{1,0:T(8,128)(2,1)}, bf16[768,1024]{1,0:T(8,128)(2,1)}, u32[]{:S(2)}, u32[]{:S(2)}) %collective-permute-start.6) | collective-permute-done | bytes 1572896 | tf_op jit(solution)/shard_map/ppermute | solution.py:941
  105.2 2.0 collective-permute-done.2
  107.2 2.6 collective-permute-start.3
  116.3 53.2 %expert_grad.5 = (bf16[4,4,2048,512]{3,2,1,0:T(8,128)(2,1)}, bf16[4,4,2048,512]{3,2,1,0:T(8,128)(2,1)}, bf16[4,4,2048,512]{3,2,1,0:T(8,128)(2,1)}, f32[4,1024,1024]{2,1,0:T(8,128)}, f32[4,512,1024]{2,1,0:T(8,128)}) custom-call(s32[512]{0:T(512)} %reshape.53.refs_0_.starts_ref, ...), custom_call_target="tpu_custom_call", output_to_operand_aliasing={{0}: (16, {}), {1}: (17, {}), {2}: (18, {})} | custom-call | flops 19327352832 | bytes 41943040 | tf_op jit(solution)/shard_map/expert_grad/pallas_call | solution.py:412
  169.5 10.2 %collective-permute-done.4.refs_3_ = bf16[768,1024]{1,0:T(8,128)(2,1)} collective-permute-done((bf16[768,1024]{1,0:T(8,128)(2,1)}, bf16[768,1024]{1,0:T(8,128)(2,1)}, u32[]{:S(2)}, u32[]{:S(2)}) %collective-permute-start.4) | collective-permute-done | bytes 1572896 | tf_op jit(solution)/shard_map/ppermute | solution.py:941
  183.6 24.4 %expert_y.2 = (bf16[12,256,1024]{2,1,0:T(8,128)(2,1)}, f32[12,8,256]{2,1,0:T(8,128)}) custom-call(s32[512]{0:T(512)} %reshape.53.refs_0_.starts_ref, s32[24]{0:T(128)} %constant.31.clone.refs_1_.bmap_ref, s32[2]{0:T(128)} %iota_multiply_fusion.spans_ref, f32[48,8,256]{2,1,0:T(8,128)} %bitcast.22, bf16[4,4,2048,512]{3,2,1,0:T(8,128)(2,1)} %get-tuple-element.91.h_ref.refs_16_, ...), custom_call_target="tpu_custom_call" | custom-call | flops 6442450944 | bytes 20971520 | tf_op jit(solution)/shard_map/expert_y/pallas_call | solution.py:572
  211.4 53.1 %expert_grad.6 = (bf16[4,4,2048,512]{3,2,1,0:T(8,128)(2,1)}, bf16[4,4,2048,512]{3,2,1,0:T(8,128)(2,1)}, bf16[4,4,2048,512]{3,2,1,0:T(8,128)(2,1)}, f32[4,1024,1024]{2,1,0:T(8,128)}, f32[4,512,1024]{2,1,0:T(8,128)}) custom-call(s32[512]{0:T(512)} %reshape.53.refs_0_.starts_ref, ...), custom_call_target="tpu_custom_call", output_to_operand_aliasing={{0}: (16, {}), {1}: (17, {}), {2}: (18, {})} | custom-call | flops 19327352832 | bytes 41943040 | tf_op jit(solution)/shard_map/expert_grad/pallas_call | solution.py:412
  264.5 14.8 %collective-permute-done.17.refs_5_ = bf16[768,1024]{1,0:T(8,128)(2,1)} collective-permute-done((bf16[768,1024]{1,0:T(8,128)(2,1)}, bf16[768,1024]{1,0:T(8,128)(2,1)}, u32[]{:S(2)}, u32[]{:S(2)}) %collective-permute-start.17) | collective-permute-done | bytes 1572896 | tf_op jit(solution)/shard_map/ppermute | solution.py:941
  280.4 22.2 %expert_dx.2 = bf16[12,256,1024]{2,1,0:T(8,128)(2,1)} custom-call(s32[512]{0:T(512)} %reshape.53.refs_0_.starts_ref, s32[24]{0:T(128)} %constant.31.clone.refs_1_.bmap_ref, s32[2]{0:T(128)} %iota_multiply_fusion.spans_ref, f32[48,8,256]{2,1,0:T(8,128)} %bitcast.24, bf16[4,4,2048,512]{3,2,1,0:T(8,128)(2,1)} %get-tuple-element.103.da_ref.refs_17_, ...), custom_call_target="tpu_custom_call" | custom-call | flops 9663676416 | bytes 20971520 | tf_op jit(solution)/shard_map/expert_dx/pallas_call | solution.py:627
  302.7 53.8 %expert_grad.7 = (bf16[4,4,2048,512]{3,2,1,0:T(8,128)(2,1)}, bf16[4,4,2048,512]{3,2,1,0:T(8,128)(2,1)}, bf16[4,4,2048,512]{3,2,1,0:T(8,128)(2,1)}, bf16[4,1024,5...) custom-call(s32[512]{0:T(512)} %reshape.53.refs_0_.starts_ref, ...), custom_call_target="tpu_custom_call", output_to_operand_aliasing={{0}: (16, {}), {1}: (17, {}), {2}: (18, {})} | custom-call | flops 19327352832 | bytes 41943040 | tf_op jit(solution)/shard_map/expert_grad/pallas_call | solution.py:412
  356.5 69.7 %expert_y.3 = (bf16[36,256,1024]{2,1,0:T(8,128)(2,1)}, f32[36,8,256]{2,1,0:T(8,128)}) custom-call(s32[512]{0:T(512)} %reshape.53.refs_0_.starts_ref, s32[72]{0:T(128)} %constant.36.clone.bmap_ref, s32[6]{0:T(128)} %constant.37.clone.spans_ref, f32[48,8,256]{2,1,0:T(8,128)} %bitcast.26, bf16[4,4,2048,512]{3,2,1,0:T(8,128)(2,1)} %get-tuple-element.110.h_ref, ...), custom_call_target="tpu_custom_call" | custom-call | flops 19327352832 | bytes 20971520 | tf_op jit(solution)/shard_map/expert_y/pallas_call | solution.py:572
  427.4 13.5 %all_to_all.10 = f32[8,4,1664]{2,1,0:T(4,128)S(1)} all-to-all(f32[8,4,1664]{2,1,0:T(4,128)S(1)} %pad_maximum_fusion), channel_id=1, replica_groups=mesh['dp'=4,'ep'=8] {'ep'}, dimensions={0} | all-to-all | bytes 425984 | tf_op jit(solution)/shard_map/all_to_all | solution.py:1039
  442.3 5.7 router_grad.1
  448.8 61.0 %expert_dx.3 = bf16[36,256,1024]{2,1,0:T(8,128)(2,1)} custom-call(s32[512]{0:T(512)} %reshape.53.refs_0_.starts_ref, s32[72]{0:T(128)} %constant.36.clone.bmap_ref, s32[6]{0:T(128)} %constant.37.clone.spans_ref, f32[48,8,256]{2,1,0:T(8,128)} %bitcast.27, bf16[4,4,2048,512]{3,2,1,0:T(8,128)(2,1)} %get-tuple-element.117.da_ref, ...), custom_call_target="tpu_custom_call" | custom-call | flops 28991029248 | bytes 20971520 | tf_op jit(solution)/shard_map/expert_dx/pallas_call | solution.py:627
  509.8 364.0 %exchange.1 = (bf16[1536,1024]{1,0:T(8,128)(2,1)}, bf16[1536,1024]{1,0:T(8,128)(2,1)}, bf16[1536,1024]{1,0:T(8,128)(2,1)}, bf16[1536,1024]{1,0:T(8,128)(2,1)}, b...) custom-call(bf16[2,1536,1024]{2,1,0:T(8,128)(2,1)} %bitcast.39, ...), custom_call_target="tpu_custom_call" | custom-call | flops 137438953472 | bytes 209715200 | tf_op jit(solution)/shard_map/exchange/pallas_call | solution.py:910
  875.9 10.7 %final.1 = (bf16[1536,1024]{1,0:T(8,128)(2,1)}, bf16[1536,1024]{1,0:T(8,128)(2,1)}) custom-call(f32[32,1536]{1,0:T(8,128)} %get-tuple-element.113.dlog_ref, f32[32,1024]{1,0:T(8,128)} %bitcast.35, bf16[1536,1024]{1,0:T(8,128)(2,1)} %get-tuple-element.121.refs_0_, bf16[1536,1024]{1,0:T(8,128)(2,1)} %get-tuple-element.122.refs_1_, ...), custom_call_target="tpu_custom_call" | custom-call | flops 805306368 | bytes 25165824 | tf_op jit(solution)/shard_map/final/pallas_call | solution.py:694
  888.3 4.6 copy.50
  892.9 2.1 copy.51
  896.6 2.0 copy.52
  (95 shorter events, 35.7 us)
Async XLA Ops:
  7.2 31.3 %collective-permute-start.1 = (bf16[1536,1024]{1,0:T(8,128)(2,1)}, bf16[1536,1024]{1,0:T(8,128)(2,1)}, u32[]{:S(2)}, u32[]{:S(2)}) collective-permute-start(bf16[1536,1024]{1,0:T(8,128)(2,1)} %refs_0_.1), channel_id=1, source_target_pairs={{0,1},{1,0},{2,3},{3,2},{4,5},{5,4},{6,7},{7,6},{8,9},{9,8},{10,11... | collective-permute-start | bytes 9437192 | tf_op jit(solution)/shard_map/ppermute | solution.py:941
  7.7 31.3 %collective-permute-start = (bf16[1536,1024]{1,0:T(8,128)(2,1)}, bf16[1536,1024]{1,0:T(8,128)(2,1)}, u32[]{:S(2)}, u32[]{:S(2)}) collective-permute-start(bf16[1536,1024]{1,0:T(8,128)(2,1)} %x_ref.2), channel_id=1, source_target_pairs={{0,1},{1,0},{2,3},{3,2},{4,5},{5,4},{6,7},{7,6},{8,9},{9,8},{10,11... | collective-permute-start | bytes 9437192 | tf_op jit(solution)/shard_map/ppermute | solution.py:941
  27.7 859.0 %all-reduce.3.cloned.1.call-start = ((), (), s32[]{:S(2)}) async-start(), calls=%async_computation.2 | async-start | bytes 262144 | tf_op jit(solution)/shard_map/psum | solution.py:1044
  27.8 60.0 %collective-permute-start.10 = (bf16[768,1024]{1,0:T(8,128)(2,1)}, bf16[768,1024]{1,0:T(8,128)(2,1)}, u32[]{:S(2)}, u32[]{:S(2)}) collective-permute-start(bf16[768,1024]{1,0:T(8,128)(2,1)} %get-tuple-element.134), channel_id=1, source_target_pairs={{0,2},{1,3},{2,0},{3,1},{4,6},{5,7},{6,4},{7,5},{8,10},{9,11},{10,... | collective-permute-start | bytes 4718600 | tf_op jit(solution)/shard_map/ppermute | solution.py:941
  29.7 58.0 %collective-permute-start.11 = (bf16[768,1024]{1,0:T(8,128)(2,1)}, bf16[768,1024]{1,0:T(8,128)(2,1)}, u32[]{:S(2)}, u32[]{:S(2)}) collective-permute-start(bf16[768,1024]{1,0:T(8,128)(2,1)} %get-tuple-element.134), channel_id=1, source_target_pairs={{0,4},{1,5},{2,6},{3,7},{4,0},{5,1},{6,2},{7,3},{8,12},{9,13},{10,... | collective-permute-start | bytes 4718600 | tf_op jit(solution)/shard_map/ppermute | solution.py:941
  31.2 71.8 %collective-permute-start.6 = (bf16[768,1024]{1,0:T(8,128)(2,1)}, bf16[768,1024]{1,0:T(8,128)(2,1)}, u32[]{:S(2)}, u32[]{:S(2)}) collective-permute-start(bf16[768,1024]{1,0:T(8,128)(2,1)} %get-tuple-element.136), channel_id=1, source_target_pairs={{0,2},{1,3},{2,0},{3,1},{4,6},{5,7},{6,4},{7,5},{8,10},{9,11},{10,... | collective-permute-start | bytes 4718600 | tf_op jit(solution)/shard_map/ppermute | solution.py:941
  38.5 64.5 %collective-permute-start.7 = (bf16[768,1024]{1,0:T(8,128)(2,1)}, bf16[768,1024]{1,0:T(8,128)(2,1)}, u32[]{:S(2)}, u32[]{:S(2)}) collective-permute-start(bf16[768,1024]{1,0:T(8,128)(2,1)} %get-tuple-element.136), channel_id=1, source_target_pairs={{0,4},{1,5},{2,6},{3,7},{4,0},{5,1},{6,2},{7,3},{8,12},{9,13},{10,... | collective-permute-start | bytes 4718600 | tf_op jit(solution)/shard_map/ppermute | solution.py:941
  87.7 26.0 %collective-permute-start.13 = (bf16[768,1024]{1,0:T(8,128)(2,1)}, bf16[768,1024]{1,0:T(8,128)(2,1)}, u32[]{:S(2)}, u32[]{:S(2)}) collective-permute-start(bf16[768,1024]{1,0:T(8,128)(2,1)} %collective-permute-done.11.refs_9_.refs_2_), channel_id=1, source_target_pairs={{0,1},{1,0},{2,3},{3,2},{4,5},{5,4},{6,7},{7,6},{8,9},{9,8},{10,11... | collective-permute-start | bytes 4718600 | tf_op jit(solution)/shard_map/ppermute | solution.py:941
  88.7 25.6 %collective-permute-start.12 = (bf16[768,1024]{1,0:T(8,128)(2,1)}, bf16[768,1024]{1,0:T(8,128)(2,1)}, u32[]{:S(2)}, u32[]{:S(2)}) collective-permute-start(bf16[768,1024]{1,0:T(8,128)(2,1)} %collective-permute-done.10.refs_7_.refs_0_), channel_id=1, source_target_pairs={{0,1},{1,0},{2,3},{3,2},{4,5},{5,4},{6,7},{7,6},{8,9},{9,8},{10,11... | collective-permute-start | bytes 4718600 | tf_op jit(solution)/shard_map/ppermute | solution.py:941
  111.7 57.8 %collective-permute-start.14 = (bf16[768,1024]{1,0:T(8,128)(2,1)}, bf16[768,1024]{1,0:T(8,128)(2,1)}, u32[]{:S(2)}, u32[]{:S(2)}) collective-permute-start(bf16[768,1024]{1,0:T(8,128)(2,1)} %get-tuple-element.133), channel_id=1, source_target_pairs={{0,2},{1,3},{2,0},{3,1},{4,6},{5,7},{6,4},{7,5},{8,10},{9,11},{10,... | collective-permute-start | bytes 4718600 | tf_op jit(solution)/shard_map/ppermute | solution.py:941
  113.7 55.8 %collective-permute-start.15 = (bf16[768,1024]{1,0:T(8,128)(2,1)}, bf16[768,1024]{1,0:T(8,128)(2,1)}, u32[]{:S(2)}, u32[]{:S(2)}) collective-permute-start(bf16[768,1024]{1,0:T(8,128)(2,1)} %get-tuple-element.133), channel_id=1, source_target_pairs={{0,4},{1,5},{2,6},{3,7},{4,0},{5,1},{6,2},{7,3},{8,12},{9,13},{10,... | collective-permute-start | bytes 4718600 | tf_op jit(solution)/shard_map/ppermute | solution.py:941
  114.3 65.4 %collective-permute-start.4 = (bf16[768,1024]{1,0:T(8,128)(2,1)}, bf16[768,1024]{1,0:T(8,128)(2,1)}, u32[]{:S(2)}, u32[]{:S(2)}) collective-permute-start(bf16[768,1024]{1,0:T(8,128)(2,1)} %get-tuple-element.135), channel_id=1, source_target_pairs={{0,2},{1,3},{2,0},{3,1},{4,6},{5,7},{6,4},{7,5},{8,10},{9,11},{10,... | collective-permute-start | bytes 4718600 | tf_op jit(solution)/shard_map/ppermute | solution.py:941
  115.7 65.8 %collective-permute-start.5 = (bf16[768,1024]{1,0:T(8,128)(2,1)}, bf16[768,1024]{1,0:T(8,128)(2,1)}, u32[]{:S(2)}, u32[]{:S(2)}) collective-permute-start(bf16[768,1024]{1,0:T(8,128)(2,1)} %get-tuple-element.135), channel_id=1, source_target_pairs={{0,4},{1,5},{2,6},{3,7},{4,0},{5,1},{6,2},{7,3},{8,12},{9,13},{10,... | collective-permute-start | bytes 4718600 | tf_op jit(solution)/shard_map/ppermute | solution.py:941
  181.5 26.5 %collective-permute-start.20 = (bf16[768,1024]{1,0:T(8,128)(2,1)}, bf16[768,1024]{1,0:T(8,128)(2,1)}, u32[]{:S(2)}, u32[]{:S(2)}) collective-permute-start(bf16[768,1024]{1,0:T(8,128)(2,1)} %collective-permute-done.14.refs_7_.refs_4_), channel_id=1, source_target_pairs={{0,1},{1,0},{2,3},{3,2},{4,5},{5,4},{6,7},{7,6},{8,9},{9,8},{10,11... | collective-permute-start | bytes 4718600 | tf_op jit(solution)/shard_map/ppermute | solution.py:941
  181.5 27.8 %collective-permute-start.21 = (bf16[768,1024]{1,0:T(8,128)(2,1)}, bf16[768,1024]{1,0:T(8,128)(2,1)}, u32[]{:S(2)}, u32[]{:S(2)}) collective-permute-start(bf16[768,1024]{1,0:T(8,128)(2,1)} %collective-permute-done.15.refs_9_.refs_6_), channel_id=1, source_target_pairs={{0,1},{1,0},{2,3},{3,2},{4,5},{5,4},{6,7},{7,6},{8,9},{9,8},{10,11... | collective-permute-start | bytes 4718600 | tf_op jit(solution)/shard_map/ppermute | solution.py:941
  182.0 27.8 %collective-permute-start.18 = (bf16[768,1024]{1,0:T(8,128)(2,1)}, bf16[768,1024]{1,0:T(8,128)(2,1)}, u32[]{:S(2)}, u32[]{:S(2)}) collective-permute-start(bf16[768,1024]{1,0:T(8,128)(2,1)} %collective-permute-done.4.refs_3_), channel_id=1, source_target_pairs={{0,1},{1,0},{2,3},{3,2},{4,5},{5,4},{6,7},{7,6},{8,9},{9,8},{10,11... | collective-permute-start | bytes 4718600 | tf_op jit(solution)/shard_map/ppermute | solution.py:941
  182.0 29.3 %collective-permute-start.19 = (bf16[768,1024]{1,0:T(8,128)(2,1)}, bf16[768,1024]{1,0:T(8,128)(2,1)}, u32[]{:S(2)}, u32[]{:S(2)}) collective-permute-start(bf16[768,1024]{1,0:T(8,128)(2,1)} %collective-permute-done.5.refs_5_), channel_id=1, source_target_pairs={{0,1},{1,0},{2,3},{3,2},{4,5},{5,4},{6,7},{7,6},{8,9},{9,8},{10,11... | collective-permute-start | bytes 4718600 | tf_op jit(solution)/shard_map/ppermute | solution.py:941
  183.0 81.4 %collective-permute-start.22 = (bf16[768,1024]{1,0:T(8,128)(2,1)}, bf16[768,1024]{1,0:T(8,128)(2,1)}, u32[]{:S(2)}, u32[]{:S(2)}) collective-permute-start(bf16[768,1024]{1,0:T(8,128)(2,1)} %collective-permute-done.11.refs_9_.refs_2_), channel_id=1, source_target_pairs={{0,2},{1,3},{2,0},{3,1},{4,6},{5,7},{6,4},{7,5},{8,10},{9,11},{10,... | collective-permute-start | bytes 4718600 | tf_op jit(solution)/shard_map/ppermute | solution.py:941
  208.0 56.5 %collective-permute-start.16 = (bf16[768,1024]{1,0:T(8,128)(2,1)}, bf16[768,1024]{1,0:T(8,128)(2,1)}, u32[]{:S(2)}, u32[]{:S(2)}) collective-permute-start(bf16[768,1024]{1,0:T(8,128)(2,1)} %collective-permute-done.7.refs_5_), channel_id=1, source_target_pairs={{0,2},{1,3},{2,0},{3,1},{4,6},{5,7},{6,4},{7,5},{8,10},{9,11},{10,... | collective-permute-start | bytes 4718600 | tf_op jit(solution)/shard_map/ppermute | solution.py:941
  209.3 55.2 %collective-permute-start.23 = (bf16[768,1024]{1,0:T(8,128)(2,1)}, bf16[768,1024]{1,0:T(8,128)(2,1)}, u32[]{:S(2)}, u32[]{:S(2)}) collective-permute-start(bf16[768,1024]{1,0:T(8,128)(2,1)} %collective-permute-done.14.refs_7_.refs_4_), channel_id=1, source_target_pairs={{0,4},{1,5},{2,6},{3,7},{4,0},{5,1},{6,2},{7,3},{8,12},{9,13},{10,... | collective-permute-start | bytes 4718600 | tf_op jit(solution)/shard_map/ppermute | solution.py:941
  209.8 69.5 %collective-permute-start.17 = (bf16[768,1024]{1,0:T(8,128)(2,1)}, bf16[768,1024]{1,0:T(8,128)(2,1)}, u32[]{:S(2)}, u32[]{:S(2)}) collective-permute-start(bf16[768,1024]{1,0:T(8,128)(2,1)} %collective-permute-done.4.refs_3_), channel_id=1, source_target_pairs={{0,4},{1,5},{2,6},{3,7},{4,0},{5,1},{6,2},{7,3},{8,12},{9,13},{10,... | collective-permute-start | bytes 4718600 | tf_op jit(solution)/shard_map/ppermute | solution.py:941
  279.4 23.3 %collective-permute-start.26 = (bf16[768,1024]{1,0:T(8,128)(2,1)}, bf16[768,1024]{1,0:T(8,128)(2,1)}, u32[]{:S(2)}, u32[]{:S(2)}) collective-permute-start(bf16[768,1024]{1,0:T(8,128)(2,1)} %collective-permute-done.22.refs_7_.refs_8_), channel_id=1, source_target_pairs={{0,1},{1,0},{2,3},{3,2},{4,5},{5,4},{6,7},{7,6},{8,9},{9,8},{10,11... | collective-permute-start | bytes 4718600 | tf_op jit(solution)/shard_map/ppermute | solution.py:941
  279.4 23.3 %collective-permute-start.27 = (bf16[768,1024]{1,0:T(8,128)(2,1)}, bf16[768,1024]{1,0:T(8,128)(2,1)}, u32[]{:S(2)}, u32[]{:S(2)}) collective-permute-start(bf16[768,1024]{1,0:T(8,128)(2,1)} %collective-permute-done.23.refs_9_.refs_10_), channel_id=1, source_target_pairs={{0,1},{1,0},{2,3},{3,2},{4,5},{5,4},{6,7},{7,6},{8,9},{9,8},{10,11... | collective-permute-start | bytes 4718600 | tf_op jit(solution)/shard_map/ppermute | solution.py:941
  448.1 438.6 %all-reduce.5.cloned.1.call-start = ((), (), s32[]{:S(2)}) async-start(), calls=%async_computation.3 | async-start | bytes 8388608 | tf_op jit(solution)/shard_map/psum | solution.py:1031
  (14 other events, 250.5 us)
Sparse Core Ops, SparseCore 0:
  448.2 126.0 all-reduce.2
  577.2 254.9 all-reduce.4
where the time goes:
time: 915 us; the launch traced here: 907 us
  Pallas kernels  774 us (85%)
  waiting for transfers between devices  51 us (6%)
  starting transfers between devices  26.1 us (3%)
  local copies, waits for them, and re-layouts  21.9 us (2%)
  between operations  16.3 us (2%)
  blocking collectives  13.5 us (1%)
    pallas_call x1, Pallas kernels, run_exchange(): pl.pallas_call(functools.partial(exchange_kernel, half, len(dws)), in_spe...  364 us
    pallas_call x4, Pallas kernels, run_grad(): pl.pallas_call(functools.partial(grad_kernel, g, last, local, pieces), gr...  209 us
    pallas_call x2, Pallas kernels, run_y(): pl.pallas_call(functools.partial(y_kernel, groups, local), grid=(len(grou...  94.1 us
    pallas_call x2, Pallas kernels, run_dx(): pl.pallas_call(functools.partial(dx_kernel, local), grid=(len(groups), lo...  83.2 us
    ppermute x26, waiting for transfers between devices, hop(): return lax.ppermute(v, 'ep', [(i, i ^ bit) for i in SOURCES])  41.2 us
  transfers between devices with their start and end apart: 31, of which 7 were waited for; matrix products, arithmetic and copies ran while one was open for 1% of the time, Pallas kernels for 71%

commit v1 on v0

--- a/solution.py
+++ b/solution.py
@@ -27,7 +27,7 @@
 STAGES = 3
 SLOTS = 16
 SPLIT = range(4)
-LAG = 3
+BACK, LAG = 2, 4
 MESH = pl.DeviceIdType.MESH
 
 WHOLE, PARTS = (0, 6), ((0, 3), (3, 3))
@@ -859,7 +859,7 @@
 
         @pl.when(is_mid)
         def _():
-            back = tick - 1
+            back = tick - BACK
             if tick < n:
                 first_add(tick)
             if back in range(n):
@@ -945,12 +945,12 @@
     return lax.optimization_barrier((values, token))[FIRST]
 
 
-def send_own(v):
-    pieces = [v[first * BLK : (first + count) * BLK] for first, count in PARTS]
+def send_own(v, token):
     got = {(FIRST, *WHOLE): v, (CORE, *WHOLE): hop(v, CORE)}
+    pieces = after([v[first * BLK : (first + count) * BLK] for first, count in PARTS], token)
     for part, piece in zip(PARTS, pieces):
         got.update({(bit, *part): hop(piece, bit) for bit in NEAR})
-    return got, pieces
+    return got
 
 
 def pass_on(got, h):
@@ -986,11 +986,11 @@
         row_cap = padded(4 * capacity)
         me = lax.axis_index("ep")
 
-        gathered, pieces = zip(*[send_own(v) for v in (x_loc, dy_loc)])
-
-        ids_t, x_router = after((ids_loc.T, x_loc), pieces)
-        send_tab, prob_t = run_router(x_router, w_router, ids_t, capacity, local, ep_size)
-        tab_rel = relative(lax.all_to_all(send_tab, "ep", FIRST, FIRST, tiled=True), me)
+        ids_t = ids_loc.T
+        send_tab, prob_t = run_router(x_loc, w_router, ids_t, capacity, local, ep_size)
+        tables = lax.all_to_all(send_tab, "ep", FIRST, FIRST, tiled=True)
+        gathered = [send_own(v, tables) for v in (x_loc, dy_loc)]
+        tab_rel = relative(tables, me)
         tab = tab_rel[:, :, :tokens].reshape(ep_size, 2 * local, nb, BLK).transpose(0, 2, 1, 3).reshape(ep_size * nb, 2 * local, BLK)
         starts = tab_rel[:, local:, tokens : tokens + ALIGN].astype(i32).reshape(LAST)
 
@@ -1006,7 +1006,7 @@
             if g:
                 ready = [p for p in group if not p[FIRST] & CORE]
                 for got in gathered:
-                    got.update(after({p: got[p] for p in ready}, acc[LAST]))
+                    got.update(after({p: got[p] for p in ready}, (acc[LAST], dg_own)))
                 for got in gathered:
                     if g < len(GROUPS) - 1:
                         pass_on(got, g - 1)
@@ -1015,9 +1015,6 @@
                             got[src | CORE, *part] = hop(got[src, *part], CORE)
                 here = after(starts, [[got[p] for p in ready] for got in gathered])
                 if g == 2:
-                    y_own, dg_own = y_of(own, here)
-                    starts = after(starts, dg_own)
-                if g > 2:
                     dx_own = dx_of(own, here)
                     starts = after(starts, dx_own)
             rows, acc = run_grad(starts, tab, g, *[[got[p] for p in group] for got in gathered], (w1, w3, w2), acc, rows, nb, row_cap)
@@ -1025,7 +1022,8 @@
                 stats = jnp.sum(after(tab_rel[:, :local, tokens:], acc[LAST]), axis=FIRST)
                 for step in (1, 2):
                     stats = stats + lax.ppermute(stats, "dp", [(i, i ^ step) for i in range(dp_size)])
-                starts = after(starts, stats)
+                y_own, dg_own = y_of(own, after(starts, stats))
+                starts = after(starts, dg_own)
         dw1, dw3, dw2 = acc
         starts, dw2 = lax.optimization_barrier((starts, dw2))
         dw2_sum = lax.psum(dw2, "dp")

time: 915 us -> 888 us (0.970)
  Pallas kernels: 774 us -> 757 us
  waiting for transfers between devices: 51 us -> 41.3 us
    pallas_call x1, Pallas kernels: 364 us -> 346 us  [run_exchange(): pl.pallas_call(functools.partial(exchange_kernel, half, len(dws)), in_spe...]
  transfers between devices with their start and end apart: 31 -> 31, of which waited for: 7 -> 10; matrix products, arithmetic and copies ran while one was open for 1% -> 1% of each run, Pallas kernels for 71% -> 71%
where the time goes in v1:
time: 888 us; the launch traced here: 885 us
  Pallas kernels  757 us (85%)
  waiting for transfers between devices  41.3 us (5%)
  starting transfers between devices  29.5 us (3%)
  local copies, waits for them, and re-layouts  22.7 us (3%)
  between operations  16.3 us (2%)
  blocking collectives  13.6 us (2%)
    pallas_call x1, Pallas kernels, run_exchange(): pl.pallas_call(functools.partial(exchange_kernel, half, len(dws)), in_spe...  346 us
    pallas_call x4, Pallas kernels, run_grad(): pl.pallas_call(functools.partial(grad_kernel, g, last, local, pieces), gr...  209 us
    pallas_call x2, Pallas kernels, run_y(): pl.pallas_call(functools.partial(y_kernel, groups, local), grid=(len(grou...  94.1 us
    pallas_call x2, Pallas kernels, run_dx(): pl.pallas_call(functools.partial(dx_kernel, local), grid=(len(groups), lo...  83.3 us
    ppermute x26, waiting for transfers between devices, hop(): return lax.ppermute(v, 'ep', [(i, i ^ bit) for i in SOURCES])  32.8 us
    ppermute x26, starting transfers between devices, hop(): return lax.ppermute(v, 'ep', [(i, i ^ bit) for i in SOURCES])  21.7 us
  transfers between devices with their start and end apart: 31, of which 10 were waited for; matrix products, arithmetic and copies ran while one was open for 1% of the time, Pallas kernels for 71%

profile of v1, /device:TPU:0, one launch (start us, length us, event | category | flops | bytes accessed | tf_op | source)
XLA Modules:
  0.0 885.0 jit_solution(13906400026799573275)
XLA Ops:
  9.7 7.6 router.1
  17.3 5.1 all-to-all-start
  22.5 4.0 fusion.1
  38.1 49.2 %expert_grad.4 = (bf16[4,4,2048,512]{3,2,1,0:T(8,128)(2,1)}, bf16[4,4,2048,512]{3,2,1,0:T(8,128)(2,1)}, bf16[4,4,2048,512]{3,2,1,0:T(8,128)(2,1)}, f32[4,1024,1024]{2,1,0:T(8,128)}, f32[4,512,1024]{2,1,0:T(8,128)}) custom-call(s32[512]{0:T(512)} %reshape.53.refs_0_.starts_ref, s32[24]{0:T(128)} %constant.31.clone.refs_1_.bmap_ref, f32[48,8,256]{2,1,0:T(8,128)} %bitcast.20, ...), custom_call_target="tpu_custom_call" | custom-call | flops 19327352832 | bytes 41943040 | tf_op jit(solution)/shard_map/expert_grad/pallas_call | solution.py:412
  87.5 3.5 collective-permute-done.2
  96.1 24.5 %expert_y.2 = (bf16[12,256,1024]{2,1,0:T(8,128)(2,1)}, f32[12,8,256]{2,1,0:T(8,128)}) custom-call(s32[512]{0:T(512)} %reshape.53.refs_0_.starts_ref, s32[24]{0:T(128)} %constant.31.clone.refs_1_.bmap_ref, s32[2]{0:T(128)} %iota_multiply_fusion.spans_ref, f32[48,8,256]{2,1,0:T(8,128)} %bitcast.21, bf16[4,4,2048,512]{3,2,1,0:T(8,128)(2,1)} %get-tuple-element.76.h_ref.refs_16_, ...), custom_call_target="tpu_custom_call" | custom-call | flops 6442450944 | bytes 20971520 | tf_op jit(solution)/shard_map/expert_y/pallas_call | solution.py:572
  125.3 3.2 collective-permute-start.15
  129.8 3.2 collective-permute-start.5
  133.0 53.2 %expert_grad.5 = (bf16[4,4,2048,512]{3,2,1,0:T(8,128)(2,1)}, bf16[4,4,2048,512]{3,2,1,0:T(8,128)(2,1)}, bf16[4,4,2048,512]{3,2,1,0:T(8,128)(2,1)}, f32[4,1024,1024]{2,1,0:T(8,128)}, f32[4,512,1024]{2,1,0:T(8,128)}) custom-call(s32[512]{0:T(512)} %reshape.53.refs_0_.starts_ref, ...), custom_call_target="tpu_custom_call", output_to_operand_aliasing={{0}: (16, {}), {1}: (17, {}), {2}: (18, {})} | custom-call | flops 19327352832 | bytes 41943040 | tf_op jit(solution)/shard_map/expert_grad/pallas_call | solution.py:412
  186.3 7.0 collective-permute-done.4.refs_3_
  193.3 3.9 collective-permute-done.5.refs_5_
  198.5 22.3 %expert_dx.2 = bf16[12,256,1024]{2,1,0:T(8,128)(2,1)} custom-call(s32[512]{0:T(512)} %reshape.53.refs_0_.starts_ref, s32[24]{0:T(128)} %constant.31.clone.refs_1_.bmap_ref, s32[2]{0:T(128)} %iota_multiply_fusion.spans_ref, f32[48,8,256]{2,1,0:T(8,128)} %bitcast.23, bf16[4,4,2048,512]{3,2,1,0:T(8,128)(2,1)} %get-tuple-element.96.da_ref.refs_17_, ...), custom_call_target="tpu_custom_call" | custom-call | flops 9663676416 | bytes 20971520 | tf_op jit(solution)/shard_map/expert_dx/pallas_call | solution.py:627
  224.1 52.9 %expert_grad.6 = (bf16[4,4,2048,512]{3,2,1,0:T(8,128)(2,1)}, bf16[4,4,2048,512]{3,2,1,0:T(8,128)(2,1)}, bf16[4,4,2048,512]{3,2,1,0:T(8,128)(2,1)}, f32[4,1024,1024]{2,1,0:T(8,128)}, f32[4,512,1024]{2,1,0:T(8,128)}) custom-call(s32[512]{0:T(512)} %reshape.53.refs_0_.starts_ref, ...), custom_call_target="tpu_custom_call", output_to_operand_aliasing={{0}: (16, {}), {1}: (17, {}), {2}: (18, {})} | custom-call | flops 19327352832 | bytes 41943040 | tf_op jit(solution)/shard_map/expert_grad/pallas_call | solution.py:412
  277.0 3.3 collective-permute-start.26
  280.4 12.5 %collective-permute-done.17.refs_5_ = bf16[768,1024]{1,0:T(8,128)(2,1)} collective-permute-done((bf16[768,1024]{1,0:T(8,128)(2,1)}, bf16[768,1024]{1,0:T(8,128)(2,1)}, u32[]{:S(2)}, u32[]{:S(2)}) %collective-permute-start.17) | collective-permute-done | bytes 1572896 | tf_op jit(solution)/shard_map/ppermute | solution.py:941
  293.4 3.2 collective-permute-done.22.refs_4_
  298.8 53.8 %expert_grad.7 = (bf16[4,4,2048,512]{3,2,1,0:T(8,128)(2,1)}, bf16[4,4,2048,512]{3,2,1,0:T(8,128)(2,1)}, bf16[4,4,2048,512]{3,2,1,0:T(8,128)(2,1)}, bf16[4,1024,5...) custom-call(s32[512]{0:T(512)} %reshape.53.refs_0_.starts_ref, ...), custom_call_target="tpu_custom_call", output_to_operand_aliasing={{0}: (16, {}), {1}: (17, {}), {2}: (18, {})} | custom-call | flops 19327352832 | bytes 41943040 | tf_op jit(solution)/shard_map/expert_grad/pallas_call | solution.py:412
  352.6 69.7 %expert_y.3 = (bf16[36,256,1024]{2,1,0:T(8,128)(2,1)}, f32[36,8,256]{2,1,0:T(8,128)}) custom-call(s32[512]{0:T(512)} %reshape.53.refs_0_.starts_ref, s32[72]{0:T(128)} %constant.36.clone.bmap_ref, s32[6]{0:T(128)} %constant.37.clone.spans_ref, f32[48,8,256]{2,1,0:T(8,128)} %bitcast.26, bf16[4,4,2048,512]{3,2,1,0:T(8,128)(2,1)} %get-tuple-element.112.h_ref, ...), custom_call_target="tpu_custom_call" | custom-call | flops 19327352832 | bytes 20971520 | tf_op jit(solution)/shard_map/expert_y/pallas_call | solution.py:572
  423.5 13.6 %all_to_all.10 = f32[8,4,1664]{2,1,0:T(4,128)S(1)} all-to-all(f32[8,4,1664]{2,1,0:T(4,128)S(1)} %pad_maximum_fusion), channel_id=1, replica_groups=mesh['dp'=4,'ep'=8] {'ep'}, dimensions={0} | all-to-all | bytes 425984 | tf_op jit(solution)/shard_map/all_to_all | solution.py:1037
  438.6 5.7 router_grad.1
  445.1 61.0 %expert_dx.3 = bf16[36,256,1024]{2,1,0:T(8,128)(2,1)} custom-call(s32[512]{0:T(512)} %reshape.53.refs_0_.starts_ref, s32[72]{0:T(128)} %constant.36.clone.bmap_ref, s32[6]{0:T(128)} %constant.37.clone.spans_ref, f32[48,8,256]{2,1,0:T(8,128)} %bitcast.27, bf16[4,4,2048,512]{3,2,1,0:T(8,128)(2,1)} %get-tuple-element.119.da_ref, ...), custom_call_target="tpu_custom_call" | custom-call | flops 28991029248 | bytes 20971520 | tf_op jit(solution)/shard_map/expert_dx/pallas_call | solution.py:627
  506.1 345.9 %exchange.1 = (bf16[1536,1024]{1,0:T(8,128)(2,1)}, bf16[1536,1024]{1,0:T(8,128)(2,1)}, bf16[1536,1024]{1,0:T(8,128)(2,1)}, bf16[1536,1024]{1,0:T(8,128)(2,1)}, b...) custom-call(bf16[2,1536,1024]{2,1,0:T(8,128)(2,1)} %bitcast.38, ...), custom_call_target="tpu_custom_call" | custom-call | flops 137438953472 | bytes 209715200 | tf_op jit(solution)/shard_map/exchange/pallas_call | solution.py:910
  854.1 10.8 %final.1 = (bf16[1536,1024]{1,0:T(8,128)(2,1)}, bf16[1536,1024]{1,0:T(8,128)(2,1)}) custom-call(f32[32,1536]{1,0:T(8,128)} %get-tuple-element.115.dlog_ref, f32[32,1024]{1,0:T(8,128)} %bitcast.34, bf16[1536,1024]{1,0:T(8,128)(2,1)} %get-tuple-element.123.refs_0_, bf16[1536,1024]{1,0:T(8,128)(2,1)} %get-tuple-element.124.refs_1_, ...), custom_call_target="tpu_custom_call" | custom-call | flops 805306368 | bytes 25165824 | tf_op jit(solution)/shard_map/final/pallas_call | solution.py:694
  866.5 4.6 copy.50
  (93 shorter events, 45.0 us)
Async XLA Ops:
  7.2 29.5 %collective-permute-start.1 = (bf16[1536,1024]{1,0:T(8,128)(2,1)}, bf16[1536,1024]{1,0:T(8,128)(2,1)}, u32[]{:S(2)}, u32[]{:S(2)}) collective-permute-start(bf16[1536,1024]{1,0:T(8,128)(2,1)} %refs_0_.1), channel_id=1, source_target_pairs={{0,1},{1,0},{2,3},{3,2},{4,5},{5,4},{6,7},{7,6},{8,9},{9,8},{10,11... | collective-permute-start | bytes 9437192 | tf_op jit(solution)/shard_map/ppermute | solution.py:941
  7.7 30.4 %collective-permute-start = (bf16[1536,1024]{1,0:T(8,128)(2,1)}, bf16[1536,1024]{1,0:T(8,128)(2,1)}, u32[]{:S(2)}, u32[]{:S(2)}) collective-permute-start(bf16[1536,1024]{1,0:T(8,128)(2,1)} %x_ref.3), channel_id=1, source_target_pairs={{0,1},{1,0},{2,3},{3,2},{4,5},{5,4},{6,7},{7,6},{8,9},{9,8},{10,11... | collective-permute-start | bytes 9437192 | tf_op jit(solution)/shard_map/ppermute | solution.py:941
  17.3 13.9 %all-to-all-start = ((f32[8,8,1664]{2,1,0:T(8,128)}), f32[8,8,1664]{2,1,0:T(8,128)}, u32[]{:S(2)}, u32[]{:S(2)}) async-start(f32[8,8,1664]{2,1,0:T(8,128)} %get-tuple-element.72), calls=%async_computation | async-start | bytes 851968 | tf_op jit(solution)/shard_map/all_to_all | solution.py:991
  22.5 842.4 %all-reduce.3.cloned.1.call-start = ((), (), s32[]{:S(2)}) async-start(), calls=%async_computation.2 | async-start | bytes 262144 | tf_op jit(solution)/shard_map/psum | solution.py:1042
  33.4 87.2 %collective-permute-start.10 = (bf16[768,1024]{1,0:T(8,128)(2,1)}, bf16[768,1024]{1,0:T(8,128)(2,1)}, u32[]{:S(2)}, u32[]{:S(2)}) collective-permute-start(bf16[768,1024]{1,0:T(8,128)(2,1)} %get-tuple-element.83), channel_id=1, source_target_pairs={{0,2},{1,3},{2,0},{3,1},{4,6},{5,7},{6,4},{7,5},{8,10},{9,11},{10,... | collective-permute-start | bytes 4718600 | tf_op jit(solution)/shard_map/ppermute | solution.py:941
  33.9 86.6 %collective-permute-start.11 = (bf16[768,1024]{1,0:T(8,128)(2,1)}, bf16[768,1024]{1,0:T(8,128)(2,1)}, u32[]{:S(2)}, u32[]{:S(2)}) collective-permute-start(bf16[768,1024]{1,0:T(8,128)(2,1)} %get-tuple-element.83), channel_id=1, source_target_pairs={{0,4},{1,5},{2,6},{3,7},{4,0},{5,1},{6,2},{7,3},{8,12},{9,13},{10,... | collective-permute-start | bytes 4718600 | tf_op jit(solution)/shard_map/ppermute | solution.py:941
  35.2 86.9 %collective-permute-start.6 = (bf16[768,1024]{1,0:T(8,128)(2,1)}, bf16[768,1024]{1,0:T(8,128)(2,1)}, u32[]{:S(2)}, u32[]{:S(2)}) collective-permute-start(bf16[768,1024]{1,0:T(8,128)(2,1)} %get-tuple-element.80), channel_id=1, source_target_pairs={{0,2},{1,3},{2,0},{3,1},{4,6},{5,7},{6,4},{7,5},{8,10},{9,11},{10,... | collective-permute-start | bytes 4718600 | tf_op jit(solution)/shard_map/ppermute | solution.py:941
  36.6 85.4 %collective-permute-start.7 = (bf16[768,1024]{1,0:T(8,128)(2,1)}, bf16[768,1024]{1,0:T(8,128)(2,1)}, u32[]{:S(2)}, u32[]{:S(2)}) collective-permute-start(bf16[768,1024]{1,0:T(8,128)(2,1)} %get-tuple-element.80), channel_id=1, source_target_pairs={{0,4},{1,5},{2,6},{3,7},{4,0},{5,1},{6,2},{7,3},{8,12},{9,13},{10,... | collective-permute-start | bytes 4718600 | tf_op jit(solution)/shard_map/ppermute | solution.py:941
  122.5 10.5 %collective-permute-start.9 = (bf16[768,1024]{1,0:T(8,128)(2,1)}, bf16[768,1024]{1,0:T(8,128)(2,1)}, u32[]{:S(2)}, u32[]{:S(2)}) collective-permute-start(bf16[768,1024]{1,0:T(8,128)(2,1)} %collective-permute-done.7.refs_5_), channel_id=1, source_target_pairs={{0,1},{1,0},{2,3},{3,2},{4,5},{5,4},{6,7},{7,6},{8,9},{9,8},{10,11... | collective-permute-start | bytes 4718600 | tf_op jit(solution)/shard_map/ppermute | solution.py:941
  122.6 63.7 %collective-permute-start.14 = (bf16[768,1024]{1,0:T(8,128)(2,1)}, bf16[768,1024]{1,0:T(8,128)(2,1)}, u32[]{:S(2)}, u32[]{:S(2)}) collective-permute-start(bf16[768,1024]{1,0:T(8,128)(2,1)} %get-tuple-element.92), channel_id=1, source_target_pairs={{0,2},{1,3},{2,0},{3,1},{4,6},{5,7},{6,4},{7,5},{8,10},{9,11},{10,... | collective-permute-start | bytes 4718600 | tf_op jit(solution)/shard_map/ppermute | solution.py:941
  125.3 60.9 %collective-permute-start.15 = (bf16[768,1024]{1,0:T(8,128)(2,1)}, bf16[768,1024]{1,0:T(8,128)(2,1)}, u32[]{:S(2)}, u32[]{:S(2)}) collective-permute-start(bf16[768,1024]{1,0:T(8,128)(2,1)} %get-tuple-element.92), channel_id=1, source_target_pairs={{0,4},{1,5},{2,6},{3,7},{4,0},{5,1},{6,2},{7,3},{8,12},{9,13},{10,... | collective-permute-start | bytes 4718600 | tf_op jit(solution)/shard_map/ppermute | solution.py:941
  128.5 64.8 %collective-permute-start.4 = (bf16[768,1024]{1,0:T(8,128)(2,1)}, bf16[768,1024]{1,0:T(8,128)(2,1)}, u32[]{:S(2)}, u32[]{:S(2)}) collective-permute-start(bf16[768,1024]{1,0:T(8,128)(2,1)} %get-tuple-element.79), channel_id=1, source_target_pairs={{0,2},{1,3},{2,0},{3,1},{4,6},{5,7},{6,4},{7,5},{8,10},{9,11},{10,... | collective-permute-start | bytes 4718600 | tf_op jit(solution)/shard_map/ppermute | solution.py:941
  129.8 67.4 %collective-permute-start.5 = (bf16[768,1024]{1,0:T(8,128)(2,1)}, bf16[768,1024]{1,0:T(8,128)(2,1)}, u32[]{:S(2)}, u32[]{:S(2)}) collective-permute-start(bf16[768,1024]{1,0:T(8,128)(2,1)} %get-tuple-element.79), channel_id=1, source_target_pairs={{0,4},{1,5},{2,6},{3,7},{4,0},{5,1},{6,2},{7,3},{8,12},{9,13},{10,... | collective-permute-start | bytes 4718600 | tf_op jit(solution)/shard_map/ppermute | solution.py:941
  197.2 23.5 %collective-permute-start.20 = (bf16[768,1024]{1,0:T(8,128)(2,1)}, bf16[768,1024]{1,0:T(8,128)(2,1)}, u32[]{:S(2)}, u32[]{:S(2)}) collective-permute-start(bf16[768,1024]{1,0:T(8,128)(2,1)} %collective-permute-done.14.refs_7_.refs_4_), channel_id=1, source_target_pairs={{0,1},{1,0},{2,3},{3,2},{4,5},{5,4},{6,7},{7,6},{8,9},{9,8},{10,11... | collective-permute-start | bytes 4718600 | tf_op jit(solution)/shard_map/ppermute | solution.py:941
  197.2 24.8 %collective-permute-start.21 = (bf16[768,1024]{1,0:T(8,128)(2,1)}, bf16[768,1024]{1,0:T(8,128)(2,1)}, u32[]{:S(2)}, u32[]{:S(2)}) collective-permute-start(bf16[768,1024]{1,0:T(8,128)(2,1)} %collective-permute-done.15.refs_9_.refs_6_), channel_id=1, source_target_pairs={{0,1},{1,0},{2,3},{3,2},{4,5},{5,4},{6,7},{7,6},{8,9},{9,8},{10,11... | collective-permute-start | bytes 4718600 | tf_op jit(solution)/shard_map/ppermute | solution.py:941
  197.7 26.1 %collective-permute-start.18 = (bf16[768,1024]{1,0:T(8,128)(2,1)}, bf16[768,1024]{1,0:T(8,128)(2,1)}, u32[]{:S(2)}, u32[]{:S(2)}) collective-permute-start(bf16[768,1024]{1,0:T(8,128)(2,1)} %collective-permute-done.4.refs_3_), channel_id=1, source_target_pairs={{0,1},{1,0},{2,3},{3,2},{4,5},{5,4},{6,7},{7,6},{8,9},{9,8},{10,11... | collective-permute-start | bytes 4718600 | tf_op jit(solution)/shard_map/ppermute | solution.py:941
  197.8 26.3 %collective-permute-start.19 = (bf16[768,1024]{1,0:T(8,128)(2,1)}, bf16[768,1024]{1,0:T(8,128)(2,1)}, u32[]{:S(2)}, u32[]{:S(2)}) collective-permute-start(bf16[768,1024]{1,0:T(8,128)(2,1)} %collective-permute-done.5.refs_5_), channel_id=1, source_target_pairs={{0,1},{1,0},{2,3},{3,2},{4,5},{5,4},{6,7},{7,6},{8,9},{9,8},{10,11... | collective-permute-start | bytes 4718600 | tf_op jit(solution)/shard_map/ppermute | solution.py:941
  198.3 78.7 %collective-permute-start.24 = (bf16[768,1024]{1,0:T(8,128)(2,1)}, bf16[768,1024]{1,0:T(8,128)(2,1)}, u32[]{:S(2)}, u32[]{:S(2)}) collective-permute-start(bf16[768,1024]{1,0:T(8,128)(2,1)} %collective-permute-done.11.refs_9_.refs_2_), channel_id=1, source_target_pairs={{0,2},{1,3},{2,0},{3,1},{4,6},{5,7},{6,4},{7,5},{8,10},{9,11},{10,... | collective-permute-start | bytes 4718600 | tf_op jit(solution)/shard_map/ppermute | solution.py:941
  220.8 59.6 %collective-permute-start.16 = (bf16[768,1024]{1,0:T(8,128)(2,1)}, bf16[768,1024]{1,0:T(8,128)(2,1)}, u32[]{:S(2)}, u32[]{:S(2)}) collective-permute-start(bf16[768,1024]{1,0:T(8,128)(2,1)} %collective-permute-done.7.refs_5_), channel_id=1, source_target_pairs={{0,2},{1,3},{2,0},{3,1},{4,6},{5,7},{6,4},{7,5},{8,10},{9,11},{10,... | collective-permute-start | bytes 4718600 | tf_op jit(solution)/shard_map/ppermute | solution.py:941
  222.1 55.0 %collective-permute-start.25 = (bf16[768,1024]{1,0:T(8,128)(2,1)}, bf16[768,1024]{1,0:T(8,128)(2,1)}, u32[]{:S(2)}, u32[]{:S(2)}) collective-permute-start(bf16[768,1024]{1,0:T(8,128)(2,1)} %collective-permute-done.14.refs_7_.refs_4_), channel_id=1, source_target_pairs={{0,4},{1,5},{2,6},{3,7},{4,0},{5,1},{6,2},{7,3},{8,12},{9,13},{10,... | collective-permute-start | bytes 4718600 | tf_op jit(solution)/shard_map/ppermute | solution.py:941
  223.8 69.0 %collective-permute-start.17 = (bf16[768,1024]{1,0:T(8,128)(2,1)}, bf16[768,1024]{1,0:T(8,128)(2,1)}, u32[]{:S(2)}, u32[]{:S(2)}) collective-permute-start(bf16[768,1024]{1,0:T(8,128)(2,1)} %collective-permute-done.4.refs_3_), channel_id=1, source_target_pairs={{0,4},{1,5},{2,6},{3,7},{4,0},{5,1},{6,2},{7,3},{8,12},{9,13},{10,... | collective-permute-start | bytes 4718600 | tf_op jit(solution)/shard_map/ppermute | solution.py:941
  277.0 16.3 %collective-permute-start.26 = (bf16[768,1024]{1,0:T(8,128)(2,1)}, bf16[768,1024]{1,0:T(8,128)(2,1)}, u32[]{:S(2)}, u32[]{:S(2)}) collective-permute-start(bf16[768,1024]{1,0:T(8,128)(2,1)} %collective-permute-done.24.refs_7_.refs_8_), channel_id=1, source_target_pairs={{0,1},{1,0},{2,3},{3,2},{4,5},{5,4},{6,7},{7,6},{8,9},{9,8},{10,11... | collective-permute-start | bytes 4718600 | tf_op jit(solution)/shard_map/ppermute | solution.py:941
  280.3 13.1 %collective-permute-start.27 = (bf16[768,1024]{1,0:T(8,128)(2,1)}, bf16[768,1024]{1,0:T(8,128)(2,1)}, u32[]{:S(2)}, u32[]{:S(2)}) collective-permute-start(bf16[768,1024]{1,0:T(8,128)(2,1)} %collective-permute-done.25.refs_9_.refs_10_), channel_id=1, source_target_pairs={{0,1},{1,0},{2,3},{3,2},{4,5},{5,4},{6,7},{7,6},{8,9},{9,8},{10,11... | collective-permute-start | bytes 4718600 | tf_op jit(solution)/shard_map/ppermute | solution.py:941
  444.3 420.6 %all-reduce.5.cloned.1.call-start = ((), (), s32[]{:S(2)}) async-start(), calls=%async_computation.3 | async-start | bytes 8388608 | tf_op jit(solution)/shard_map/psum | solution.py:1029
  (13 other events, 190.7 us)
Sparse Core Ops, SparseCore 0:
  444.4 126.5 all-reduce.2
  573.9 255.6 all-reduce.4

commit v2 on v1

--- a/solution.py
+++ b/solution.py
@@ -301,43 +301,65 @@
     head_row = iota((ALIGN, d_model), FIRST)
     both = tuple(HALVES)
 
-    def dispatch(i, rows_at):
-        for k, (_, _, first) in enumerate(parts):
-            pl.when((e == FIRST) & (i == first))(lambda: wait(token_copies(k)))
-        tok = span(i * BLK, BLK)
-        infos = [blocks.info(i, e + q) for q in both]
-        places = [aligned(r) for r in rows_at]
-        flat = infos[FIRST][FIRST]
-
-        def picks(q, k):
+    def dispatch(step, rows_at):
+        todo = []
+        for i in (2 * step, 2 * step + 1):
+            for k, (_, _, first) in enumerate(parts):
+                pl.when((e == FIRST) & (i == first))(lambda: wait(token_copies(k)))
+            infos = [blocks.info(i, e + q) for q in both]
+            todo.append((span(i * BLK, BLK), infos, [aligned(r) for r in rows_at]))
+            rows_at = tuple(r + info[LAST] for r, info in zip(rows_at, infos))
+
+        def picks(block, q, k):
+            _, infos, places = block
+            flat, first, _ = infos[q]
             pos = tab_ref[flat, pl.ds(local + e + q, 1), :]
             gate = tab_ref[flat, pl.ds(e + q, 1), :]
-            pick = (pos + (places[q][1] - infos[q][1] - k * WIN).astype(f32)) == row_iota
+            pick = (pos + (places[q][1] - first - k * WIN).astype(f32)) == row_iota
             return one_hot(pick), lane_sum(where0(pick, gate + jnp.zeros_like(row_iota)))
 
-        def rows_for(one, gate_row):
+        def rows_for(block, one, gate_row):
+            tok = block[FIRST]
             return dot(one, xv[tok, :]).astype(bf16), (dot(one, dv[tok, :]) * gate_row).astype(bf16)
 
-        pair = [picks(q, i32(FIRST)) for q in both]
-        new = rows_for(*[jnp.concatenate(v, axis=FIRST) for v in zip(*pair)])
-        for q in both:
-            base, shift = places[q]
-            head = span(base, ALIGN)
-            for value, rows in zip(new, (xr, dr)):
-                value = value[q * WIN : (q + 1) * WIN]
-                rows[q, head, :] = jnp.where(head_row < shift, rows[q, head, :], value[:ALIGN])
-                rows[q, span(base + ALIGN, WIN - ALIGN, ALIGN), :] = value[ALIGN:]
-
-            def more(k):
-                for value, rows in zip(rows_for(*picks(q, k)), (xr, dr)):
-                    rows[q, span(base + k * WIN, WIN, ALIGN), :] = value
-
-            loop(1, window_count(shift, infos[q][LAST]), more)
-        return tuple(r + info[LAST] for r, info in zip(rows_at, infos))
+        def first_rows(block):
+            pair = [picks(block, q, i32(FIRST)) for q in both]
+            return rows_for(block, *[jnp.concatenate(v, axis=FIRST) for v in zip(*pair)])
+
+        def put(block, new):
+            for q in both:
+                base, shift = block[LAST][q]
+                head = span(base, ALIGN)
+                for value, rows in zip(new, (xr, dr)):
+                    value = value[q * WIN : (q + 1) * WIN]
+                    rows[q, head, :] = jnp.where(head_row < shift, rows[q, head, :], value[:ALIGN])
+                    rows[q, span(base + ALIGN, WIN - ALIGN, ALIGN), :] = value[ALIGN:]
+
+        windows = [[window_count(places[q][1], infos[q][LAST]) for q in both] for _, infos, places in todo]
+        simple = functools.reduce(jnp.logical_and, [w <= 1 for ws in windows for w in ws])
+
+        @pl.when(simple)
+        def _():
+            for block, new in zip(todo, [first_rows(block) for block in todo]):
+                put(block, new)
+
+        @pl.when(jnp.logical_not(simple))
+        def _():
+            for block, ws in zip(todo, windows):
+                put(block, first_rows(block))
+                for q in both:
+
+                    def more(k):
+                        for value, rows in zip(rows_for(block, *picks(block, q, k)), (xr, dr)):
+                            rows[q, span(block[LAST][q][FIRST] + k * WIN, WIN, ALIGN), :] = value
+
+                    loop(1, ws[q], more)
+
+        return rows_at
 
     @pl.when(slot == FIRST)
     def _():
-        totals = lax.fori_loop(FIRST, count, dispatch, (i32(FIRST),) * len(both))
+        totals = lax.fori_loop(FIRST, count // 2, dispatch, (i32(FIRST),) * len(both))
         for q in both:
 
             def clear(i):
@@ -349,7 +371,7 @@
     wait(in_copies(e, slot))
 
     def tile(at, size):
-        maybe_prefetch(at == FIRST)
+        maybe_prefetch((at == FIRST) & (slot == FIRST))
         rows = span(at, size)
         xt = xr[slot, rows, :]
         dt = dr[slot, rows, :]
@@ -372,8 +394,8 @@
         wait(copies)
 
     total = blocks.total(FIRST, count, e)
-    maybe_prefetch(total == FIRST)
     row_tiles(total, tile, 2 * TILE)
+    maybe_prefetch((total == FIRST) | (slot > FIRST))
 
     if last:
         for out, value in zip(outs, (acc13[slot, :, :d_ff], acc13[slot, :, d_ff:], acc2[slot])):
@@ -1006,7 +1028,7 @@
             if g:
                 ready = [p for p in group if not p[FIRST] & CORE]
                 for got in gathered:
-                    got.update(after({p: got[p] for p in ready}, (acc[LAST], dg_own)))
+                    got.update(after({p: got[p] for p in ready}, acc[LAST]))
                 for got in gathered:
                     if g < len(GROUPS) - 1:
                         pass_on(got, g - 1)
@@ -1015,6 +1037,9 @@
                             got[src | CORE, *part] = hop(got[src, *part], CORE)
                 here = after(starts, [[got[p] for p in ready] for got in gathered])
                 if g == 2:
+                    y_own, dg_own = y_of(own, here)
+                    starts = after(starts, dg_own)
+                if g > 2:
                     dx_own = dx_of(own, here)
                     starts = after(starts, dx_own)
             rows, acc = run_grad(starts, tab, g, *[[got[p] for p in group] for got in gathered], (w1, w3, w2), acc, rows, nb, row_cap)
@@ -1022,8 +1047,7 @@
                 stats = jnp.sum(after(tab_rel[:, :local, tokens:], acc[LAST]), axis=FIRST)
                 for step in (1, 2):
                     stats = stats + lax.ppermute(stats, "dp", [(i, i ^ step) for i in range(dp_size)])
-                y_own, dg_own = y_of(own, after(starts, stats))
-                starts = after(starts, dg_own)
+                starts = after(starts, stats)
         dw1, dw3, dw2 = acc
         starts, dw2 = lax.optimization_barrier((starts, dw2))
         dw2_sum = lax.psum(dw2, "dp")

time: 888 us -> 890 us (level)
  Pallas kernels: 757 us -> 736 us
  waiting for transfers between devices: 41.3 us -> 61.1 us
    ppermute x26, waiting for transfers between devices: 32.8 us -> 54.3 us  [hop(): return lax.ppermute(v, 'ep', [(i, i ^ bit) for i in SOURCES])]
    pallas_call x4, Pallas kernels: 209 us -> 190 us  [run_grad(): pl.pallas_call(functools.partial(grad_kernel, g, last, local, pieces), gr...]
  transfers between devices with their start and end apart: 31 -> 31, of which waited for: 10 -> 8; matrix products, arithmetic and copies ran while one was open for 1% -> 1% of each run, Pallas kernels for 71% -> 69%
where the time goes in v2:
time: 890 us; the launch traced here: 881 us
  Pallas kernels  736 us (83%)
  waiting for transfers between devices  61.1 us (7%)
  starting transfers between devices  27.2 us (3%)
  local copies, waits for them, and re-layouts  22.7 us (3%)
  between operations  16.4 us (2%)
  blocking collectives  12 us (1%)
    pallas_call x1, Pallas kernels, run_exchange(): pl.pallas_call(functools.partial(exchange_kernel, half, len(dws)), in_spe...  345 us
    pallas_call x4, Pallas kernels, run_grad(): pl.pallas_call(functools.partial(grad_kernel, g, last, local, pieces), gr...  190 us
    pallas_call x2, Pallas kernels, run_y(): pl.pallas_call(functools.partial(y_kernel, groups, local), grid=(len(grou...  94.3 us
    pallas_call x2, Pallas kernels, run_dx(): pl.pallas_call(functools.partial(dx_kernel, local), grid=(len(groups), lo...  83.1 us
    ppermute x26, waiting for transfers between devices, hop(): return lax.ppermute(v, 'ep', [(i, i ^ bit) for i in SOURCES])  54.3 us
  transfers between devices with their start and end apart: 31, of which 8 were waited for; matrix products, arithmetic and copies ran while one was open for 1% of the time, Pallas kernels for 69%

profile of v2, /device:TPU:0, one launch (start us, length us, event | category | flops | bytes accessed | tf_op | source)
XLA Modules:
  0.0 880.7 jit_solution(15413870210880065739)
XLA Ops:
  9.7 7.6 router.1
  17.3 5.1 all-to-all-start
  22.5 4.0 fusion.1
  26.5 2.0 fusion.2
  28.5 2.7 all-to-all-done
  38.0 46.8 %expert_grad.4 = (bf16[4,4,2048,512]{3,2,1,0:T(8,128)(2,1)}, bf16[4,4,2048,512]{3,2,1,0:T(8,128)(2,1)}, bf16[4,4,2048,512]{3,2,1,0:T(8,128)(2,1)}, f32[4,1024,1024]{2,1,0:T(8,128)}, f32[4,512,1024]{2,1,0:T(8,128)}) custom-call(s32[512]{0:T(512)} %reshape.53.refs_0_.starts_ref, s32[24]{0:T(128)} %constant.31.clone.refs_1_.bmap_ref, f32[48,8,256]{2,1,0:T(8,128)} %bitcast.20, ...), custom_call_target="tpu_custom_call" | custom-call | flops 19327352832 | bytes 41943040 | tf_op jit(solution)/shard_map/expert_grad/pallas_call | solution.py:434
  86.8 13.6 %collective-permute-done.6.refs_3_ = bf16[768,1024]{1,0:T(8,128)(2,1)} collective-permute-done((bf16[768,1024]{1,0:T(8,128)(2,1)}, bf16[768,1024]{1,0:T(8,128)(2,1)}, u32[]{:S(2)}, u32[]{:S(2)}) %collective-permute-start.6) | collective-permute-done | bytes 1572896 | tf_op jit(solution)/shard_map/ppermute | solution.py:963
  106.1 2.9 collective-permute-start.3
  115.2 46.5 %expert_grad.5 = (bf16[4,4,2048,512]{3,2,1,0:T(8,128)(2,1)}, bf16[4,4,2048,512]{3,2,1,0:T(8,128)(2,1)}, bf16[4,4,2048,512]{3,2,1,0:T(8,128)(2,1)}, f32[4,1024,1024]{2,1,0:T(8,128)}, f32[4,512,1024]{2,1,0:T(8,128)}) custom-call(s32[512]{0:T(512)} %reshape.53.refs_0_.starts_ref, ...), custom_call_target="tpu_custom_call", output_to_operand_aliasing={{0}: (16, {}), {1}: (17, {}), {2}: (18, {})} | custom-call | flops 19327352832 | bytes 41943040 | tf_op jit(solution)/shard_map/expert_grad/pallas_call | solution.py:434
  161.7 17.1 %collective-permute-done.4.refs_3_ = bf16[768,1024]{1,0:T(8,128)(2,1)} collective-permute-done((bf16[768,1024]{1,0:T(8,128)(2,1)}, bf16[768,1024]{1,0:T(8,128)(2,1)}, u32[]{:S(2)}, u32[]{:S(2)}) %collective-permute-start.4) | collective-permute-done | bytes 1572896 | tf_op jit(solution)/shard_map/ppermute | solution.py:963
  182.7 24.5 %expert_y.2 = (bf16[12,256,1024]{2,1,0:T(8,128)(2,1)}, f32[12,8,256]{2,1,0:T(8,128)}) custom-call(s32[512]{0:T(512)} %reshape.53.refs_0_.starts_ref, s32[24]{0:T(128)} %constant.31.clone.refs_1_.bmap_ref, s32[2]{0:T(128)} %iota_multiply_fusion.spans_ref, f32[48,8,256]{2,1,0:T(8,128)} %bitcast.22, bf16[4,4,2048,512]{3,2,1,0:T(8,128)(2,1)} %get-tuple-element.95.h_ref.refs_16_, ...), custom_call_target="tpu_custom_call" | custom-call | flops 6442450944 | bytes 20971520 | tf_op jit(solution)/shard_map/expert_y/pallas_call | solution.py:594
  209.4 46.5 %expert_grad.6 = (bf16[4,4,2048,512]{3,2,1,0:T(8,128)(2,1)}, bf16[4,4,2048,512]{3,2,1,0:T(8,128)(2,1)}, bf16[4,4,2048,512]{3,2,1,0:T(8,128)(2,1)}, f32[4,1024,1024]{2,1,0:T(8,128)}, f32[4,512,1024]{2,1,0:T(8,128)}) custom-call(s32[512]{0:T(512)} %reshape.53.refs_0_.starts_ref, ...), custom_call_target="tpu_custom_call", output_to_operand_aliasing={{0}: (16, {}), {1}: (17, {}), {2}: (18, {})} | custom-call | flops 19327352832 | bytes 41943040 | tf_op jit(solution)/shard_map/expert_grad/pallas_call | solution.py:434
  255.9 21.5 %collective-permute-done.17.refs_5_ = bf16[768,1024]{1,0:T(8,128)(2,1)} collective-permute-done((bf16[768,1024]{1,0:T(8,128)(2,1)}, bf16[768,1024]{1,0:T(8,128)(2,1)}, u32[]{:S(2)}, u32[]{:S(2)}) %collective-permute-start.17) | collective-permute-done | bytes 1572896 | tf_op jit(solution)/shard_map/ppermute | solution.py:963
  278.4 22.2 %expert_dx.2 = bf16[12,256,1024]{2,1,0:T(8,128)(2,1)} custom-call(s32[512]{0:T(512)} %reshape.53.refs_0_.starts_ref, s32[24]{0:T(128)} %constant.31.clone.refs_1_.bmap_ref, s32[2]{0:T(128)} %iota_multiply_fusion.spans_ref, f32[48,8,256]{2,1,0:T(8,128)} %bitcast.24, bf16[4,4,2048,512]{3,2,1,0:T(8,128)(2,1)} %get-tuple-element.107.da_ref.refs_17_, ...), custom_call_target="tpu_custom_call" | custom-call | flops 9663676416 | bytes 20971520 | tf_op jit(solution)/shard_map/expert_dx/pallas_call | solution.py:649
  300.7 49.8 %expert_grad.7 = (bf16[4,4,2048,512]{3,2,1,0:T(8,128)(2,1)}, bf16[4,4,2048,512]{3,2,1,0:T(8,128)(2,1)}, bf16[4,4,2048,512]{3,2,1,0:T(8,128)(2,1)}, bf16[4,1024,5...) custom-call(s32[512]{0:T(512)} %reshape.53.refs_0_.starts_ref, ...), custom_call_target="tpu_custom_call", output_to_operand_aliasing={{0}: (16, {}), {1}: (17, {}), {2}: (18, {})} | custom-call | flops 19327352832 | bytes 41943040 | tf_op jit(solution)/shard_map/expert_grad/pallas_call | solution.py:434
  350.5 69.8 %expert_y.3 = (bf16[36,256,1024]{2,1,0:T(8,128)(2,1)}, f32[36,8,256]{2,1,0:T(8,128)}) custom-call(s32[512]{0:T(512)} %reshape.53.refs_0_.starts_ref, s32[72]{0:T(128)} %constant.36.clone.bmap_ref, s32[6]{0:T(128)} %constant.37.clone.spans_ref, f32[48,8,256]{2,1,0:T(8,128)} %bitcast.26, bf16[4,4,2048,512]{3,2,1,0:T(8,128)(2,1)} %get-tuple-element.114.h_ref, ...), custom_call_target="tpu_custom_call" | custom-call | flops 19327352832 | bytes 20971520 | tf_op jit(solution)/shard_map/expert_y/pallas_call | solution.py:594
  421.6 12.0 %all_to_all.10 = f32[8,4,1664]{2,1,0:T(4,128)S(1)} all-to-all(f32[8,4,1664]{2,1,0:T(4,128)S(1)} %pad_maximum_fusion), channel_id=1, replica_groups=mesh['dp'=4,'ep'=8] {'ep'}, dimensions={0} | all-to-all | bytes 425984 | tf_op jit(solution)/shard_map/all_to_all | solution.py:1061
  435.0 5.7 router_grad.1
  441.5 60.8 %expert_dx.3 = bf16[36,256,1024]{2,1,0:T(8,128)(2,1)} custom-call(s32[512]{0:T(512)} %reshape.53.refs_0_.starts_ref, s32[72]{0:T(128)} %constant.36.clone.bmap_ref, s32[6]{0:T(128)} %constant.37.clone.spans_ref, f32[48,8,256]{2,1,0:T(8,128)} %bitcast.27, bf16[4,4,2048,512]{3,2,1,0:T(8,128)(2,1)} %get-tuple-element.121.da_ref, ...), custom_call_target="tpu_custom_call" | custom-call | flops 28991029248 | bytes 20971520 | tf_op jit(solution)/shard_map/expert_dx/pallas_call | solution.py:649
  502.4 345.3 %exchange.1 = (bf16[1536,1024]{1,0:T(8,128)(2,1)}, bf16[1536,1024]{1,0:T(8,128)(2,1)}, bf16[1536,1024]{1,0:T(8,128)(2,1)}, bf16[1536,1024]{1,0:T(8,128)(2,1)}, b...) custom-call(bf16[2,1536,1024]{2,1,0:T(8,128)(2,1)} %bitcast.38, ...), custom_call_target="tpu_custom_call" | custom-call | flops 137438953472 | bytes 209715200 | tf_op jit(solution)/shard_map/exchange/pallas_call | solution.py:932
  849.8 10.7 %final.1 = (bf16[1536,1024]{1,0:T(8,128)(2,1)}, bf16[1536,1024]{1,0:T(8,128)(2,1)}) custom-call(f32[32,1536]{1,0:T(8,128)} %get-tuple-element.117.dlog_ref, f32[32,1024]{1,0:T(8,128)} %bitcast.34, bf16[1536,1024]{1,0:T(8,128)(2,1)} %get-tuple-element.125.refs_0_, bf16[1536,1024]{1,0:T(8,128)(2,1)} %get-tuple-element.126.refs_1_, ...), custom_call_target="tpu_custom_call" | custom-call | flops 805306368 | bytes 25165824 | tf_op jit(solution)/shard_map/final/pallas_call | solution.py:716
  862.2 4.6 copy.50
  866.8 2.1 copy.51
  870.5 2.0 copy.52
  (93 shorter events, 38.2 us)
Async XLA Ops:
  7.2 29.4 %collective-permute-start.1 = (bf16[1536,1024]{1,0:T(8,128)(2,1)}, bf16[1536,1024]{1,0:T(8,128)(2,1)}, u32[]{:S(2)}, u32[]{:S(2)}) collective-permute-start(bf16[1536,1024]{1,0:T(8,128)(2,1)} %refs_0_.1), channel_id=1, source_target_pairs={{0,1},{1,0},{2,3},{3,2},{4,5},{5,4},{6,7},{7,6},{8,9},{9,8},{10,11... | collective-permute-start | bytes 9437192 | tf_op jit(solution)/shard_map/ppermute | solution.py:963
  7.7 30.3 %collective-permute-start = (bf16[1536,1024]{1,0:T(8,128)(2,1)}, bf16[1536,1024]{1,0:T(8,128)(2,1)}, u32[]{:S(2)}, u32[]{:S(2)}) collective-permute-start(bf16[1536,1024]{1,0:T(8,128)(2,1)} %x_ref.3), channel_id=1, source_target_pairs={{0,1},{1,0},{2,3},{3,2},{4,5},{5,4},{6,7},{7,6},{8,9},{9,8},{10,11... | collective-permute-start | bytes 9437192 | tf_op jit(solution)/shard_map/ppermute | solution.py:963
  22.5 838.1 %all-reduce.3.cloned.1.call-start = ((), (), s32[]{:S(2)}) async-start(), calls=%async_computation.2 | async-start | bytes 262144 | tf_op jit(solution)/shard_map/psum | solution.py:1066
  31.2 53.6 %collective-permute-start.10 = (bf16[768,1024]{1,0:T(8,128)(2,1)}, bf16[768,1024]{1,0:T(8,128)(2,1)}, u32[]{:S(2)}, u32[]{:S(2)}) collective-permute-start(bf16[768,1024]{1,0:T(8,128)(2,1)} %get-tuple-element.81), channel_id=1, source_target_pairs={{0,2},{1,3},{2,0},{3,1},{4,6},{5,7},{6,4},{7,5},{8,10},{9,11},{10,... | collective-permute-start | bytes 4718600 | tf_op jit(solution)/shard_map/ppermute | solution.py:963
  31.8 53.1 %collective-permute-start.11 = (bf16[768,1024]{1,0:T(8,128)(2,1)}, bf16[768,1024]{1,0:T(8,128)(2,1)}, u32[]{:S(2)}, u32[]{:S(2)}) collective-permute-start(bf16[768,1024]{1,0:T(8,128)(2,1)} %get-tuple-element.81), channel_id=1, source_target_pairs={{0,4},{1,5},{2,6},{3,7},{4,0},{5,1},{6,2},{7,3},{8,12},{9,13},{10,... | collective-permute-start | bytes 4718600 | tf_op jit(solution)/shard_map/ppermute | solution.py:963
  35.1 65.3 %collective-permute-start.6 = (bf16[768,1024]{1,0:T(8,128)(2,1)}, bf16[768,1024]{1,0:T(8,128)(2,1)}, u32[]{:S(2)}, u32[]{:S(2)}) collective-permute-start(bf16[768,1024]{1,0:T(8,128)(2,1)} %get-tuple-element.78), channel_id=1, source_target_pairs={{0,2},{1,3},{2,0},{3,1},{4,6},{5,7},{6,4},{7,5},{8,10},{9,11},{10,... | collective-permute-start | bytes 4718600 | tf_op jit(solution)/shard_map/ppermute | solution.py:963
  36.6 65.3 %collective-permute-start.7 = (bf16[768,1024]{1,0:T(8,128)(2,1)}, bf16[768,1024]{1,0:T(8,128)(2,1)}, u32[]{:S(2)}, u32[]{:S(2)}) collective-permute-start(bf16[768,1024]{1,0:T(8,128)(2,1)} %get-tuple-element.78), channel_id=1, source_target_pairs={{0,4},{1,5},{2,6},{3,7},{4,0},{5,1},{6,2},{7,3},{8,12},{9,13},{10,... | collective-permute-start | bytes 4718600 | tf_op jit(solution)/shard_map/ppermute | solution.py:963
  84.9 26.6 %collective-permute-start.13 = (bf16[768,1024]{1,0:T(8,128)(2,1)}, bf16[768,1024]{1,0:T(8,128)(2,1)}, u32[]{:S(2)}, u32[]{:S(2)}) collective-permute-start(bf16[768,1024]{1,0:T(8,128)(2,1)} %collective-permute-done.11.refs_9_.refs_2_), channel_id=1, source_target_pairs={{0,1},{1,0},{2,3},{3,2},{4,5},{5,4},{6,7},{7,6},{8,9},{9,8},{10,11... | collective-permute-start | bytes 4718600 | tf_op jit(solution)/shard_map/ppermute | solution.py:963
  86.7 25.2 %collective-permute-start.12 = (bf16[768,1024]{1,0:T(8,128)(2,1)}, bf16[768,1024]{1,0:T(8,128)(2,1)}, u32[]{:S(2)}, u32[]{:S(2)}) collective-permute-start(bf16[768,1024]{1,0:T(8,128)(2,1)} %collective-permute-done.10.refs_7_.refs_0_), channel_id=1, source_target_pairs={{0,1},{1,0},{2,3},{3,2},{4,5},{5,4},{6,7},{7,6},{8,9},{9,8},{10,11... | collective-permute-start | bytes 4718600 | tf_op jit(solution)/shard_map/ppermute | solution.py:963
  110.6 51.2 %collective-permute-start.14 = (bf16[768,1024]{1,0:T(8,128)(2,1)}, bf16[768,1024]{1,0:T(8,128)(2,1)}, u32[]{:S(2)}, u32[]{:S(2)}) collective-permute-start(bf16[768,1024]{1,0:T(8,128)(2,1)} %get-tuple-element.91), channel_id=1, source_target_pairs={{0,2},{1,3},{2,0},{3,1},{4,6},{5,7},{6,4},{7,5},{8,10},{9,11},{10,... | collective-permute-start | bytes 4718600 | tf_op jit(solution)/shard_map/ppermute | solution.py:963
  111.4 50.3 %collective-permute-start.15 = (bf16[768,1024]{1,0:T(8,128)(2,1)}, bf16[768,1024]{1,0:T(8,128)(2,1)}, u32[]{:S(2)}, u32[]{:S(2)}) collective-permute-start(bf16[768,1024]{1,0:T(8,128)(2,1)} %get-tuple-element.91), channel_id=1, source_target_pairs={{0,4},{1,5},{2,6},{3,7},{4,0},{5,1},{6,2},{7,3},{8,12},{9,13},{10,... | collective-permute-start | bytes 4718600 | tf_op jit(solution)/shard_map/ppermute | solution.py:963
  111.9 66.9 %collective-permute-start.4 = (bf16[768,1024]{1,0:T(8,128)(2,1)}, bf16[768,1024]{1,0:T(8,128)(2,1)}, u32[]{:S(2)}, u32[]{:S(2)}) collective-permute-start(bf16[768,1024]{1,0:T(8,128)(2,1)} %get-tuple-element.77), channel_id=1, source_target_pairs={{0,2},{1,3},{2,0},{3,1},{4,6},{5,7},{6,4},{7,5},{8,10},{9,11},{10,... | collective-permute-start | bytes 4718600 | tf_op jit(solution)/shard_map/ppermute | solution.py:963
  113.6 65.8 %collective-permute-start.5 = (bf16[768,1024]{1,0:T(8,128)(2,1)}, bf16[768,1024]{1,0:T(8,128)(2,1)}, u32[]{:S(2)}, u32[]{:S(2)}) collective-permute-start(bf16[768,1024]{1,0:T(8,128)(2,1)} %get-tuple-element.77), channel_id=1, source_target_pairs={{0,4},{1,5},{2,6},{3,7},{4,0},{5,1},{6,2},{7,3},{8,12},{9,13},{10,... | collective-permute-start | bytes 4718600 | tf_op jit(solution)/shard_map/ppermute | solution.py:963
  179.4 27.7 %collective-permute-start.20 = (bf16[768,1024]{1,0:T(8,128)(2,1)}, bf16[768,1024]{1,0:T(8,128)(2,1)}, u32[]{:S(2)}, u32[]{:S(2)}) collective-permute-start(bf16[768,1024]{1,0:T(8,128)(2,1)} %collective-permute-done.14.refs_7_.refs_4_), channel_id=1, source_target_pairs={{0,1},{1,0},{2,3},{3,2},{4,5},{5,4},{6,7},{7,6},{8,9},{9,8},{10,11... | collective-permute-start | bytes 4718600 | tf_op jit(solution)/shard_map/ppermute | solution.py:963
  179.4 27.8 %collective-permute-start.21 = (bf16[768,1024]{1,0:T(8,128)(2,1)}, bf16[768,1024]{1,0:T(8,128)(2,1)}, u32[]{:S(2)}, u32[]{:S(2)}) collective-permute-start(bf16[768,1024]{1,0:T(8,128)(2,1)} %collective-permute-done.15.refs_9_.refs_6_), channel_id=1, source_target_pairs={{0,1},{1,0},{2,3},{3,2},{4,5},{5,4},{6,7},{7,6},{8,9},{9,8},{10,11... | collective-permute-start | bytes 4718600 | tf_op jit(solution)/shard_map/ppermute | solution.py:963
  179.9 27.8 %collective-permute-start.18 = (bf16[768,1024]{1,0:T(8,128)(2,1)}, bf16[768,1024]{1,0:T(8,128)(2,1)}, u32[]{:S(2)}, u32[]{:S(2)}) collective-permute-start(bf16[768,1024]{1,0:T(8,128)(2,1)} %collective-permute-done.4.refs_3_), channel_id=1, source_target_pairs={{0,1},{1,0},{2,3},{3,2},{4,5},{5,4},{6,7},{7,6},{8,9},{9,8},{10,11... | collective-permute-start | bytes 4718600 | tf_op jit(solution)/shard_map/ppermute | solution.py:963
  179.9 29.4 %collective-permute-start.19 = (bf16[768,1024]{1,0:T(8,128)(2,1)}, bf16[768,1024]{1,0:T(8,128)(2,1)}, u32[]{:S(2)}, u32[]{:S(2)}) collective-permute-start(bf16[768,1024]{1,0:T(8,128)(2,1)} %collective-permute-done.5.refs_5_), channel_id=1, source_target_pairs={{0,1},{1,0},{2,3},{3,2},{4,5},{5,4},{6,7},{7,6},{8,9},{9,8},{10,11... | collective-permute-start | bytes 4718600 | tf_op jit(solution)/shard_map/ppermute | solution.py:963
  181.0 74.9 %collective-permute-start.22 = (bf16[768,1024]{1,0:T(8,128)(2,1)}, bf16[768,1024]{1,0:T(8,128)(2,1)}, u32[]{:S(2)}, u32[]{:S(2)}) collective-permute-start(bf16[768,1024]{1,0:T(8,128)(2,1)} %collective-permute-done.11.refs_9_.refs_2_), channel_id=1, source_target_pairs={{0,2},{1,3},{2,0},{3,1},{4,6},{5,7},{6,4},{7,5},{8,10},{9,11},{10,... | collective-permute-start | bytes 4718600 | tf_op jit(solution)/shard_map/ppermute | solution.py:963
  207.2 48.7 %collective-permute-start.16 = (bf16[768,1024]{1,0:T(8,128)(2,1)}, bf16[768,1024]{1,0:T(8,128)(2,1)}, u32[]{:S(2)}, u32[]{:S(2)}) collective-permute-start(bf16[768,1024]{1,0:T(8,128)(2,1)} %collective-permute-done.7.refs_5_), channel_id=1, source_target_pairs={{0,2},{1,3},{2,0},{3,1},{4,6},{5,7},{6,4},{7,5},{8,10},{9,11},{10,... | collective-permute-start | bytes 4718600 | tf_op jit(solution)/shard_map/ppermute | solution.py:963
  207.3 48.6 %collective-permute-start.23 = (bf16[768,1024]{1,0:T(8,128)(2,1)}, bf16[768,1024]{1,0:T(8,128)(2,1)}, u32[]{:S(2)}, u32[]{:S(2)}) collective-permute-start(bf16[768,1024]{1,0:T(8,128)(2,1)} %collective-permute-done.14.refs_7_.refs_4_), channel_id=1, source_target_pairs={{0,4},{1,5},{2,6},{3,7},{4,0},{5,1},{6,2},{7,3},{8,12},{9,13},{10,... | collective-permute-start | bytes 4718600 | tf_op jit(solution)/shard_map/ppermute | solution.py:963
  207.7 69.7 %collective-permute-start.17 = (bf16[768,1024]{1,0:T(8,128)(2,1)}, bf16[768,1024]{1,0:T(8,128)(2,1)}, u32[]{:S(2)}, u32[]{:S(2)}) collective-permute-start(bf16[768,1024]{1,0:T(8,128)(2,1)} %collective-permute-done.4.refs_3_), channel_id=1, source_target_pairs={{0,4},{1,5},{2,6},{3,7},{4,0},{5,1},{6,2},{7,3},{8,12},{9,13},{10,... | collective-permute-start | bytes 4718600 | tf_op jit(solution)/shard_map/ppermute | solution.py:963
  277.4 23.3 %collective-permute-start.26 = (bf16[768,1024]{1,0:T(8,128)(2,1)}, bf16[768,1024]{1,0:T(8,128)(2,1)}, u32[]{:S(2)}, u32[]{:S(2)}) collective-permute-start(bf16[768,1024]{1,0:T(8,128)(2,1)} %collective-permute-done.22.refs_7_.refs_8_), channel_id=1, source_target_pairs={{0,1},{1,0},{2,3},{3,2},{4,5},{5,4},{6,7},{7,6},{8,9},{9,8},{10,11... | collective-permute-start | bytes 4718600 | tf_op jit(solution)/shard_map/ppermute | solution.py:963
  277.4 23.3 %collective-permute-start.27 = (bf16[768,1024]{1,0:T(8,128)(2,1)}, bf16[768,1024]{1,0:T(8,128)(2,1)}, u32[]{:S(2)}, u32[]{:S(2)}) collective-permute-start(bf16[768,1024]{1,0:T(8,128)(2,1)} %collective-permute-done.23.refs_9_.refs_10_), channel_id=1, source_target_pairs={{0,1},{1,0},{2,3},{3,2},{4,5},{5,4},{6,7},{7,6},{8,9},{9,8},{10,11... | collective-permute-start | bytes 4718600 | tf_op jit(solution)/shard_map/ppermute | solution.py:963
  440.8 419.9 %all-reduce.5.cloned.1.call-start = ((), (), s32[]{:S(2)}) async-start(), calls=%async_computation.3 | async-start | bytes 8388608 | tf_op jit(solution)/shard_map/psum | solution.py:1053
  (13 other events, 246.6 us)
Sparse Core Ops, SparseCore 0:
  440.9 125.9 all-reduce.2
  569.8 255.5 all-reduce.4

commit v3 on v2

--- a/solution.py
+++ b/solution.py
@@ -461,6 +461,34 @@
     return pl.BlockSpec((1, *shape), lambda g, e: (e,) + (FIRST,) * len(shape))
 
 
+class BlockRows:
+    def __init__(self, owner, i, rows_at):
+        ee = range(owner.local)
+        self.owner, self.i = owner, i
+        self.infos = [owner.blocks.info(i, k) for k in ee]
+        self.places = [aligned(r) for r in rows_at]
+        self.windows = [window_count(self.places[k][1], self.infos[k][LAST]) for k in ee]
+        self.simple = functools.reduce(jnp.logical_and, [w <= 1 for w in self.windows])
+        self.flat = self.infos[FIRST][FIRST]
+        self.tok = span((i - owner.first) * BLK, BLK)
+        self.out = owner.ring.at[i % RING]
+        self.after = tuple(r + info[LAST] for r, info in zip(rows_at, self.infos))
+
+    def load(self):
+        self.tab_t = jnp.transpose(self.owner.tab_ref[self.flat])
+
+    def gate(self, ee):
+        return self.tab_t[:, ee : ee + 1]
+
+    def pick(self, ee, k=FIRST):
+        at = self.owner.local + ee
+        shift = self.places[ee][1] - self.infos[ee][1] - k * WIN
+        return one_hot((self.tab_t[:, at : at + 1] + shift.astype(f32)) == self.owner.lane)
+
+    def held(self, ee, k=FIRST, cols=slice(None)):
+        return self.owner.rows_ref[ee, span(self.places[ee][FIRST] + k * WIN, WIN, ALIGN), cols]
+
+
 class Combine:
     def __init__(self, local, starts_ref, bmap_ref, spans_ref, tab_ref, rows_ref, out_ref, ring, sems):
         step = pl.program_id(FIRST)
@@ -476,38 +504,43 @@
         rows = span(padded(self.total), WIN)
         self.rows_ref[self.e, rows, :] = jnp.zeros((WIN, self.rows_ref.shape[LAST]), bf16)
 
-    def pick(self, ee, k):
-        place, info = self.places[ee], self.infos[ee]
-        pos = self.tab_t[:, self.local + ee : self.local + ee + 1]
-        return one_hot((pos + (place[1] - info[1] - k * WIN).astype(f32)) == self.lane)
-
-    def held(self, ee, k, cols=slice(None)):
-        return self.rows_ref[ee, span(self.places[ee][FIRST] + k * WIN, WIN, ALIGN), cols]
-
     def out_copy(self, i):
         slot = i % RING
         place = self.blocks.bmap[2 * i] - self.blocks.bmap[FIRST]
         return pltpu.make_async_copy(self.ring.at[slot], self.out_ref.at[place], self.sems.at[slot])
 
     def run(self, simple_body, full_body):
-        def block(i, rows_at):
-            ee = range(self.local)
-            self.infos = [self.blocks.info(i, k) for k in ee]
-            self.places = [aligned(r) for r in rows_at]
-            self.windows = [window_count(self.places[k][1], self.infos[k][LAST]) for k in ee]
-            self.flat = self.infos[FIRST][FIRST]
-            self.tab_t = jnp.transpose(self.tab_ref[self.flat])
-            self.tok = span((i - self.first) * BLK, BLK)
-            pl.when(i - self.first >= RING)(lambda: self.out_copy(i - RING).wait())
-            simple = functools.reduce(jnp.logical_and, [w <= 1 for w in self.windows])
-            out = self.ring.at[i % RING]
-            pl.when(simple)(lambda: simple_body(out))
-            pl.when(jnp.logical_not(simple))(lambda: full_body(out))
-            self.out_copy(i).start()
-            return tuple(r + info[LAST] for r, info in zip(rows_at, self.infos))
+        def pair(step, rows_at):
+            i = self.first + 2 * step
+            one = BlockRows(self, i, rows_at)
+            two = BlockRows(self, i + 1, one.after)
+            for block in (one, two):
+                pl.when(block.i - self.first >= RING)(lambda: self.out_copy(block.i - RING).wait())
+            simple = one.simple & two.simple
+
+            @pl.when(simple)
+            def _():
+                for block in (one, two):
+                    block.load()
+                for block in (one, two):
+                    simple_body(block)
+
+            @pl.when(jnp.logical_not(simple))
+            def _():
+                def full(k, rows_at):
+                    block = BlockRows(self, i + k, rows_at)
+                    block.load()
+                    full_body(block)
+                    return block.after
+
+                lax.fori_loop(FIRST, 2, full, rows_at)
+
+            for block in (one, two):
+                self.out_copy(block.i).start()
+            return two.after
 
         stop = self.first + self.count
-        lax.fori_loop(self.first, stop, block, (i32(FIRST),) * self.local)
+        lax.fori_loop(FIRST, self.count // 2, pair, (i32(FIRST),) * self.local)
         loop(stop - RING, stop, lambda i: self.out_copy(i).wait())
 
 
@@ -541,41 +574,38 @@
         width = 2 * LANES
         columns = [slice(k * width, (k + 1) * width) for k in range(d_model // width)]
 
-        def gate(ee):
-            return all_rows.tab_t[:, ee : ee + 1]
-
-        def put_dg(sums):
+        def put_dg(block, sums):
             dg = sum(where0(dg_lane == ee, lane_sum(s) + jnp.zeros((BLK, LANES), f32)) for ee, s in enumerate(sums))
-            dg_ref[all_rows.flat - all_rows.blocks.bmap[FIRST]] = jnp.transpose(dg)[: 2 * local, :]
-
-        def simple(out):
-            picks = [all_rows.pick(ee, i32(FIRST)) for ee in range(local)]
+            dg_ref[block.flat - all_rows.blocks.bmap[FIRST]] = jnp.transpose(dg)[: 2 * local, :]
+
+        def simple(block):
+            picks = [block.pick(ee) for ee in range(local)]
             sums = [None] * local
             for cols in columns:
-                dy = dv[all_rows.tok, cols].astype(f32)
+                dy = dv[block.tok, cols].astype(f32)
                 y = None
                 for ee in range(local):
-                    z = dot(picks[ee], all_rows.held(ee, i32(FIRST), cols))
+                    z = dot(picks[ee], block.held(ee, cols=cols))
                     prod = dy * z
                     part = prod[:, :LANES] + prod[:, LANES:]
                     sums[ee] = part if sums[ee] is None else sums[ee] + part
-                    y = gate(ee) * z if y is None else y + gate(ee) * z
-                out[:, cols] = y.astype(bf16)
-            put_dg(sums)
-
-        def full(out):
+                    y = block.gate(ee) * z if y is None else y + block.gate(ee) * z
+                block.out[:, cols] = y.astype(bf16)
+            put_dg(block, sums)
+
+        def full(block):
             yacc[...] = jnp.zeros_like(yacc)
             for ee in range(local):
                 zacc[...] = jnp.zeros_like(zacc)
 
                 def more(k):
-                    zacc[...] += dot(all_rows.pick(ee, k), all_rows.held(ee, k))
-
-                loop(FIRST, all_rows.windows[ee], more)
-                yacc[...] += gate(ee) * zacc[...]
-                dgacc[ee] = lane_sum(dv[all_rows.tok, :].astype(f32) * zacc[...]) * jnp.where(dg_lane == FIRST, 1.0, 0.0)
-            out[...] = yacc[...].astype(bf16)
-            put_dg([dgacc[ee] for ee in range(local)])
+                    zacc[...] += dot(block.pick(ee, k), block.held(ee, k))
+
+                loop(FIRST, block.windows[ee], more)
+                yacc[...] += block.gate(ee) * zacc[...]
+                dgacc[ee] = lane_sum(dv[block.tok, :].astype(f32) * zacc[...]) * jnp.where(dg_lane == FIRST, 1.0, 0.0)
+            block.out[...] = yacc[...].astype(bf16)
+            put_dg(block, [dgacc[ee] for ee in range(local)])
 
         all_rows.run(simple, full)
 
@@ -618,24 +648,23 @@
 
     @pl.when(e == local - 1)
     def _():
-        def simple(out):
+        def simple(block):
             pairs = [(ee, ee + 1) for ee in range(FIRST, local, 2)]
-            zero = i32(FIRST)
             sums = [
-                dot(jnp.concatenate([all_rows.pick(ee, zero) for ee in pair], axis=1), jnp.concatenate([all_rows.held(ee, zero) for ee in pair], axis=FIRST))
+                dot(jnp.concatenate([block.pick(ee) for ee in pair], axis=1), jnp.concatenate([block.held(ee) for ee in pair], axis=FIRST))
                 for pair in pairs
             ]
-            out[...] = sum(sums[1:], sums[FIRST]).astype(bf16)
-
-        def full(out):
+            block.out[...] = sum(sums[1:], sums[FIRST]).astype(bf16)
+
+        def full(block):
             zacc[...] = jnp.zeros_like(zacc)
             for ee in range(local):
 
                 def more(k):
-                    zacc[...] += dot(all_rows.pick(ee, k), all_rows.held(ee, k))
-
-                loop(FIRST, all_rows.windows[ee], more)
-            out[...] = zacc[...].astype(bf16)
+                    zacc[...] += dot(block.pick(ee, k), block.held(ee, k))
+
+                loop(FIRST, block.windows[ee], more)
+            block.out[...] = zacc[...].astype(bf16)
 
         all_rows.run(simple, full)
 
@@ -1028,7 +1057,7 @@
             if g:
                 ready = [p for p in group if not p[FIRST] & CORE]
                 for got in gathered:
-                    got.update(after({p: got[p] for p in ready}, acc[LAST]))
+                    got.update(after({p: got[p] for p in ready}, (acc[LAST], dg_own)))
                 for got in gathered:
                     if g < len(GROUPS) - 1:
                         pass_on(got, g - 1)
@@ -1037,9 +1066,6 @@
                             got[src | CORE, *part] = hop(got[src, *part], CORE)
                 here = after(starts, [[got[p] for p in ready] for got in gathered])
                 if g == 2:
-                    y_own, dg_own = y_of(own, here)
-                    starts = after(starts, dg_own)
-                if g > 2:
                     dx_own = dx_of(own, here)
                     starts = after(starts, dx_own)
             rows, acc = run_grad(starts, tab, g, *[[got[p] for p in group] for got in gathered], (w1, w3, w2), acc, rows, nb, row_cap)
@@ -1047,7 +1073,8 @@
                 stats = jnp.sum(after(tab_rel[:, :local, tokens:], acc[LAST]), axis=FIRST)
                 for step in (1, 2):
                     stats = stats + lax.ppermute(stats, "dp", [(i, i ^ step) for i in range(dp_size)])
-                starts = after(starts, stats)
+                y_own, dg_own = y_of(own, after(starts, stats))
+                starts = after(starts, dg_own)
         dw1, dw3, dw2 = acc
         starts, dw2 = lax.optimization_barrier((starts, dw2))
         dw2_sum = lax.psum(dw2, "dp")

time: 890 us -> 882 us (level)
  transfers between devices with their start and end apart: 31 -> 31, of which waited for: 8 -> 10; matrix products, arithmetic and copies ran while one was open for 1% -> 2% of each run, Pallas kernels for 69% -> 70%
where the time goes in v3:
time: 882 us; the launch traced here: 873 us
  Pallas kernels  733 us (83%)
  waiting for transfers between devices  55.5 us (6%)
  starting transfers between devices  29.1 us (3%)
  local copies, waits for them, and re-layouts  22.7 us (3%)
  between operations  16.6 us (2%)
  blocking collectives  11.8 us (1%)
    pallas_call x1, Pallas kernels, run_exchange(): pl.pallas_call(functools.partial(exchange_kernel, half, len(dws)), in_spe...  346 us
    pallas_call x4, Pallas kernels, run_grad(): pl.pallas_call(functools.partial(grad_kernel, g, last, local, pieces), gr...  189 us
    pallas_call x2, Pallas kernels, run_y(): pl.pallas_call(functools.partial(y_kernel, groups, local), grid=(len(grou...  94.8 us
    pallas_call x2, Pallas kernels, run_dx(): pl.pallas_call(functools.partial(dx_kernel, local), grid=(len(groups), lo...  78.6 us
    ppermute x26, waiting for transfers between devices, hop(): return lax.ppermute(v, 'ep', [(i, i ^ bit) for i in SOURCES])  47 us
    ppermute x26, starting transfers between devices, hop(): return lax.ppermute(v, 'ep', [(i, i ^ bit) for i in SOURCES])  21.3 us
  transfers between devices with their start and end apart: 31, of which 10 were waited for; matrix products, arithmetic and copies ran while one was open for 2% of the time, Pallas kernels for 70%

profile of v3, /device:TPU:0, one launch (start us, length us, event | category | flops | bytes accessed | tf_op | source)
XLA Modules:
  0.0 873.5 jit_solution(11778999677794283757)
XLA Ops:
  9.7 7.6 router.1
  17.3 5.1 all-to-all-start
  22.5 4.0 fusion.1
  38.1 46.8 %expert_grad.4 = (bf16[4,4,2048,512]{3,2,1,0:T(8,128)(2,1)}, bf16[4,4,2048,512]{3,2,1,0:T(8,128)(2,1)}, bf16[4,4,2048,512]{3,2,1,0:T(8,128)(2,1)}, f32[4,1024,1024]{2,1,0:T(8,128)}, f32[4,512,1024]{2,1,0:T(8,128)}) custom-call(s32[512]{0:T(512)} %reshape.53.refs_0_.starts_ref, s32[24]{0:T(128)} %constant.31.clone.refs_1_.bmap_ref, f32[48,8,256]{2,1,0:T(8,128)} %bitcast.20, ...), custom_call_target="tpu_custom_call" | custom-call | flops 19327352832 | bytes 41943040 | tf_op jit(solution)/shard_map/expert_grad/pallas_call | solution.py:434
  85.0 3.6 collective-permute-done.2
  93.7 24.8 %expert_y.2 = (bf16[12,256,1024]{2,1,0:T(8,128)(2,1)}, f32[12,8,256]{2,1,0:T(8,128)}) custom-call(s32[512]{0:T(512)} %reshape.53.refs_0_.starts_ref, s32[24]{0:T(128)} %constant.31.clone.refs_1_.bmap_ref, s32[2]{0:T(128)} %iota_multiply_fusion.spans_ref, f32[48,8,256]{2,1,0:T(8,128)} %bitcast.21, bf16[4,4,2048,512]{3,2,1,0:T(8,128)(2,1)} %get-tuple-element.76.h_ref.refs_16_, ...), custom_call_target="tpu_custom_call" | custom-call | flops 6442450944 | bytes 20971520 | tf_op jit(solution)/shard_map/expert_y/pallas_call | solution.py:624
  121.3 2.8 collective-permute-done.12.refs_8_.refs_1_
  124.0 2.9 collective-permute-start.15
  128.5 2.9 collective-permute-start.5
  131.4 46.3 %expert_grad.5 = (bf16[4,4,2048,512]{3,2,1,0:T(8,128)(2,1)}, bf16[4,4,2048,512]{3,2,1,0:T(8,128)(2,1)}, bf16[4,4,2048,512]{3,2,1,0:T(8,128)(2,1)}, f32[4,1024,1024]{2,1,0:T(8,128)}, f32[4,512,1024]{2,1,0:T(8,128)}) custom-call(s32[512]{0:T(512)} %reshape.53.refs_0_.starts_ref, ...), custom_call_target="tpu_custom_call", output_to_operand_aliasing={{0}: (16, {}), {1}: (17, {}), {2}: (18, {})} | custom-call | flops 19327352832 | bytes 41943040 | tf_op jit(solution)/shard_map/expert_grad/pallas_call | solution.py:434
  177.8 14.2 %collective-permute-done.4.refs_3_ = bf16[768,1024]{1,0:T(8,128)(2,1)} collective-permute-done((bf16[768,1024]{1,0:T(8,128)(2,1)}, bf16[768,1024]{1,0:T(8,128)(2,1)}, u32[]{:S(2)}, u32[]{:S(2)}) %collective-permute-start.4) | collective-permute-done | bytes 1572896 | tf_op jit(solution)/shard_map/ppermute | solution.py:992
  192.0 3.7 collective-permute-done.5.refs_5_
  196.9 21.1 %expert_dx.2 = bf16[12,256,1024]{2,1,0:T(8,128)(2,1)} custom-call(s32[512]{0:T(512)} %reshape.53.refs_0_.starts_ref, s32[24]{0:T(128)} %constant.31.clone.refs_1_.bmap_ref, s32[2]{0:T(128)} %iota_multiply_fusion.spans_ref, f32[48,8,256]{2,1,0:T(8,128)} %bitcast.23, bf16[4,4,2048,512]{3,2,1,0:T(8,128)(2,1)} %get-tuple-element.96.da_ref.refs_17_, ...), custom_call_target="tpu_custom_call" | custom-call | flops 9663676416 | bytes 20971520 | tf_op jit(solution)/shard_map/expert_dx/pallas_call | solution.py:678
  221.4 46.5 %expert_grad.6 = (bf16[4,4,2048,512]{3,2,1,0:T(8,128)(2,1)}, bf16[4,4,2048,512]{3,2,1,0:T(8,128)(2,1)}, bf16[4,4,2048,512]{3,2,1,0:T(8,128)(2,1)}, f32[4,1024,1024]{2,1,0:T(8,128)}, f32[4,512,1024]{2,1,0:T(8,128)}) custom-call(s32[512]{0:T(512)} %reshape.53.refs_0_.starts_ref, ...), custom_call_target="tpu_custom_call", output_to_operand_aliasing={{0}: (16, {}), {1}: (17, {}), {2}: (18, {})} | custom-call | flops 19327352832 | bytes 41943040 | tf_op jit(solution)/shard_map/expert_grad/pallas_call | solution.py:434
  270.7 19.5 %collective-permute-done.17.refs_5_ = bf16[768,1024]{1,0:T(8,128)(2,1)} collective-permute-done((bf16[768,1024]{1,0:T(8,128)(2,1)}, bf16[768,1024]{1,0:T(8,128)(2,1)}, u32[]{:S(2)}, u32[]{:S(2)}) %collective-permute-start.17) | collective-permute-done | bytes 1572896 | tf_op jit(solution)/shard_map/ppermute | solution.py:992
  290.7 3.2 collective-permute-done.22.refs_4_
  296.2 49.6 %expert_grad.7 = (bf16[4,4,2048,512]{3,2,1,0:T(8,128)(2,1)}, bf16[4,4,2048,512]{3,2,1,0:T(8,128)(2,1)}, bf16[4,4,2048,512]{3,2,1,0:T(8,128)(2,1)}, bf16[4,1024,5...) custom-call(s32[512]{0:T(512)} %reshape.53.refs_0_.starts_ref, ...), custom_call_target="tpu_custom_call", output_to_operand_aliasing={{0}: (16, {}), {1}: (17, {}), {2}: (18, {})} | custom-call | flops 19327352832 | bytes 41943040 | tf_op jit(solution)/shard_map/expert_grad/pallas_call | solution.py:434
  345.8 70.0 %expert_y.3 = (bf16[36,256,1024]{2,1,0:T(8,128)(2,1)}, f32[36,8,256]{2,1,0:T(8,128)}) custom-call(s32[512]{0:T(512)} %reshape.53.refs_0_.starts_ref, s32[72]{0:T(128)} %constant.36.clone.bmap_ref, s32[6]{0:T(128)} %constant.37.clone.spans_ref, f32[48,8,256]{2,1,0:T(8,128)} %bitcast.26, bf16[4,4,2048,512]{3,2,1,0:T(8,128)(2,1)} %get-tuple-element.112.h_ref, ...), custom_call_target="tpu_custom_call" | custom-call | flops 19327352832 | bytes 20971520 | tf_op jit(solution)/shard_map/expert_y/pallas_call | solution.py:624
  417.0 11.8 %all_to_all.10 = f32[8,4,1664]{2,1,0:T(4,128)S(1)} all-to-all(f32[8,4,1664]{2,1,0:T(4,128)S(1)} %pad_maximum_fusion), channel_id=1, replica_groups=mesh['dp'=4,'ep'=8] {'ep'}, dimensions={0} | all-to-all | bytes 425984 | tf_op jit(solution)/shard_map/all_to_all | solution.py:1088
  430.3 5.7 router_grad.1
  436.8 57.5 %expert_dx.3 = bf16[36,256,1024]{2,1,0:T(8,128)(2,1)} custom-call(s32[512]{0:T(512)} %reshape.53.refs_0_.starts_ref, s32[72]{0:T(128)} %constant.36.clone.bmap_ref, s32[6]{0:T(128)} %constant.37.clone.spans_ref, f32[48,8,256]{2,1,0:T(8,128)} %bitcast.27, bf16[4,4,2048,512]{3,2,1,0:T(8,128)(2,1)} %get-tuple-element.119.da_ref, ...), custom_call_target="tpu_custom_call" | custom-call | flops 28991029248 | bytes 20971520 | tf_op jit(solution)/shard_map/expert_dx/pallas_call | solution.py:678
  494.2 345.9 %exchange.1 = (bf16[1536,1024]{1,0:T(8,128)(2,1)}, bf16[1536,1024]{1,0:T(8,128)(2,1)}, bf16[1536,1024]{1,0:T(8,128)(2,1)}, bf16[1536,1024]{1,0:T(8,128)(2,1)}, b...) custom-call(bf16[2,1536,1024]{2,1,0:T(8,128)(2,1)} %bitcast.38, ...), custom_call_target="tpu_custom_call" | custom-call | flops 137438953472 | bytes 209715200 | tf_op jit(solution)/shard_map/exchange/pallas_call | solution.py:961
  842.3 10.8 %final.1 = (bf16[1536,1024]{1,0:T(8,128)(2,1)}, bf16[1536,1024]{1,0:T(8,128)(2,1)}) custom-call(f32[32,1536]{1,0:T(8,128)} %get-tuple-element.115.dlog_ref, f32[32,1024]{1,0:T(8,128)} %bitcast.34, bf16[1536,1024]{1,0:T(8,128)(2,1)} %get-tuple-element.123.refs_0_, bf16[1536,1024]{1,0:T(8,128)(2,1)} %get-tuple-element.124.refs_1_, ...), custom_call_target="tpu_custom_call" | custom-call | flops 805306368 | bytes 25165824 | tf_op jit(solution)/shard_map/final/pallas_call | solution.py:745
  854.7 4.6 copy.50
  (93 shorter events, 45.9 us)
Async XLA Ops:
  7.2 29.5 %collective-permute-start.1 = (bf16[1536,1024]{1,0:T(8,128)(2,1)}, bf16[1536,1024]{1,0:T(8,128)(2,1)}, u32[]{:S(2)}, u32[]{:S(2)}) collective-permute-start(bf16[1536,1024]{1,0:T(8,128)(2,1)} %refs_0_.1), channel_id=1, source_target_pairs={{0,1},{1,0},{2,3},{3,2},{4,5},{5,4},{6,7},{7,6},{8,9},{9,8},{10,11... | collective-permute-start | bytes 9437192 | tf_op jit(solution)/shard_map/ppermute | solution.py:992
  7.7 30.4 %collective-permute-start = (bf16[1536,1024]{1,0:T(8,128)(2,1)}, bf16[1536,1024]{1,0:T(8,128)(2,1)}, u32[]{:S(2)}, u32[]{:S(2)}) collective-permute-start(bf16[1536,1024]{1,0:T(8,128)(2,1)} %x_ref.3), channel_id=1, source_target_pairs={{0,1},{1,0},{2,3},{3,2},{4,5},{5,4},{6,7},{7,6},{8,9},{9,8},{10,11... | collective-permute-start | bytes 9437192 | tf_op jit(solution)/shard_map/ppermute | solution.py:992
  17.3 13.9 %all-to-all-start = ((f32[8,8,1664]{2,1,0:T(8,128)}), f32[8,8,1664]{2,1,0:T(8,128)}, u32[]{:S(2)}, u32[]{:S(2)}) async-start(f32[8,8,1664]{2,1,0:T(8,128)} %get-tuple-element.72), calls=%async_computation | async-start | bytes 851968 | tf_op jit(solution)/shard_map/all_to_all | solution.py:1042
  22.5 830.6 %all-reduce.3.cloned.1.call-start = ((), (), s32[]{:S(2)}) async-start(), calls=%async_computation.2 | async-start | bytes 262144 | tf_op jit(solution)/shard_map/psum | solution.py:1093
  33.4 85.1 %collective-permute-start.10 = (bf16[768,1024]{1,0:T(8,128)(2,1)}, bf16[768,1024]{1,0:T(8,128)(2,1)}, u32[]{:S(2)}, u32[]{:S(2)}) collective-permute-start(bf16[768,1024]{1,0:T(8,128)(2,1)} %get-tuple-element.83), channel_id=1, source_target_pairs={{0,2},{1,3},{2,0},{3,1},{4,6},{5,7},{6,4},{7,5},{8,10},{9,11},{10,... | collective-permute-start | bytes 4718600 | tf_op jit(solution)/shard_map/ppermute | solution.py:992
  33.9 84.6 %collective-permute-start.11 = (bf16[768,1024]{1,0:T(8,128)(2,1)}, bf16[768,1024]{1,0:T(8,128)(2,1)}, u32[]{:S(2)}, u32[]{:S(2)}) collective-permute-start(bf16[768,1024]{1,0:T(8,128)(2,1)} %get-tuple-element.83), channel_id=1, source_target_pairs={{0,4},{1,5},{2,6},{3,7},{4,0},{5,1},{6,2},{7,3},{8,12},{9,13},{10,... | collective-permute-start | bytes 4718600 | tf_op jit(solution)/shard_map/ppermute | solution.py:992
  35.2 85.6 %collective-permute-start.6 = (bf16[768,1024]{1,0:T(8,128)(2,1)}, bf16[768,1024]{1,0:T(8,128)(2,1)}, u32[]{:S(2)}, u32[]{:S(2)}) collective-permute-start(bf16[768,1024]{1,0:T(8,128)(2,1)} %get-tuple-element.80), channel_id=1, source_target_pairs={{0,2},{1,3},{2,0},{3,1},{4,6},{5,7},{6,4},{7,5},{8,10},{9,11},{10,... | collective-permute-start | bytes 4718600 | tf_op jit(solution)/shard_map/ppermute | solution.py:992
  36.6 84.1 %collective-permute-start.7 = (bf16[768,1024]{1,0:T(8,128)(2,1)}, bf16[768,1024]{1,0:T(8,128)(2,1)}, u32[]{:S(2)}, u32[]{:S(2)}) collective-permute-start(bf16[768,1024]{1,0:T(8,128)(2,1)} %get-tuple-element.80), channel_id=1, source_target_pairs={{0,4},{1,5},{2,6},{3,7},{4,0},{5,1},{6,2},{7,3},{8,12},{9,13},{10,... | collective-permute-start | bytes 4718600 | tf_op jit(solution)/shard_map/ppermute | solution.py:992
  121.2 10.3 %collective-permute-start.9 = (bf16[768,1024]{1,0:T(8,128)(2,1)}, bf16[768,1024]{1,0:T(8,128)(2,1)}, u32[]{:S(2)}, u32[]{:S(2)}) collective-permute-start(bf16[768,1024]{1,0:T(8,128)(2,1)} %collective-permute-done.7.refs_5_), channel_id=1, source_target_pairs={{0,1},{1,0},{2,3},{3,2},{4,5},{5,4},{6,7},{7,6},{8,9},{9,8},{10,11... | collective-permute-start | bytes 4718600 | tf_op jit(solution)/shard_map/ppermute | solution.py:992
  121.3 56.5 %collective-permute-start.14 = (bf16[768,1024]{1,0:T(8,128)(2,1)}, bf16[768,1024]{1,0:T(8,128)(2,1)}, u32[]{:S(2)}, u32[]{:S(2)}) collective-permute-start(bf16[768,1024]{1,0:T(8,128)(2,1)} %get-tuple-element.92), channel_id=1, source_target_pairs={{0,2},{1,3},{2,0},{3,1},{4,6},{5,7},{6,4},{7,5},{8,10},{9,11},{10,... | collective-permute-start | bytes 4718600 | tf_op jit(solution)/shard_map/ppermute | solution.py:992
  124.0 53.8 %collective-permute-start.15 = (bf16[768,1024]{1,0:T(8,128)(2,1)}, bf16[768,1024]{1,0:T(8,128)(2,1)}, u32[]{:S(2)}, u32[]{:S(2)}) collective-permute-start(bf16[768,1024]{1,0:T(8,128)(2,1)} %get-tuple-element.92), channel_id=1, source_target_pairs={{0,4},{1,5},{2,6},{3,7},{4,0},{5,1},{6,2},{7,3},{8,12},{9,13},{10,... | collective-permute-start | bytes 4718600 | tf_op jit(solution)/shard_map/ppermute | solution.py:992
  127.0 65.1 %collective-permute-start.4 = (bf16[768,1024]{1,0:T(8,128)(2,1)}, bf16[768,1024]{1,0:T(8,128)(2,1)}, u32[]{:S(2)}, u32[]{:S(2)}) collective-permute-start(bf16[768,1024]{1,0:T(8,128)(2,1)} %get-tuple-element.79), channel_id=1, source_target_pairs={{0,2},{1,3},{2,0},{3,1},{4,6},{5,7},{6,4},{7,5},{8,10},{9,11},{10,... | collective-permute-start | bytes 4718600 | tf_op jit(solution)/shard_map/ppermute | solution.py:992
  128.5 67.1 %collective-permute-start.5 = (bf16[768,1024]{1,0:T(8,128)(2,1)}, bf16[768,1024]{1,0:T(8,128)(2,1)}, u32[]{:S(2)}, u32[]{:S(2)}) collective-permute-start(bf16[768,1024]{1,0:T(8,128)(2,1)} %get-tuple-element.79), channel_id=1, source_target_pairs={{0,4},{1,5},{2,6},{3,7},{4,0},{5,1},{6,2},{7,3},{8,12},{9,13},{10,... | collective-permute-start | bytes 4718600 | tf_op jit(solution)/shard_map/ppermute | solution.py:992
  195.7 22.4 %collective-permute-start.20 = (bf16[768,1024]{1,0:T(8,128)(2,1)}, bf16[768,1024]{1,0:T(8,128)(2,1)}, u32[]{:S(2)}, u32[]{:S(2)}) collective-permute-start(bf16[768,1024]{1,0:T(8,128)(2,1)} %collective-permute-done.14.refs_7_.refs_4_), channel_id=1, source_target_pairs={{0,1},{1,0},{2,3},{3,2},{4,5},{5,4},{6,7},{7,6},{8,9},{9,8},{10,11... | collective-permute-start | bytes 4718600 | tf_op jit(solution)/shard_map/ppermute | solution.py:992
  195.7 23.7 %collective-permute-start.21 = (bf16[768,1024]{1,0:T(8,128)(2,1)}, bf16[768,1024]{1,0:T(8,128)(2,1)}, u32[]{:S(2)}, u32[]{:S(2)}) collective-permute-start(bf16[768,1024]{1,0:T(8,128)(2,1)} %collective-permute-done.15.refs_9_.refs_6_), channel_id=1, source_target_pairs={{0,1},{1,0},{2,3},{3,2},{4,5},{5,4},{6,7},{7,6},{8,9},{9,8},{10,11... | collective-permute-start | bytes 4718600 | tf_op jit(solution)/shard_map/ppermute | solution.py:992
  196.2 25.0 %collective-permute-start.18 = (bf16[768,1024]{1,0:T(8,128)(2,1)}, bf16[768,1024]{1,0:T(8,128)(2,1)}, u32[]{:S(2)}, u32[]{:S(2)}) collective-permute-start(bf16[768,1024]{1,0:T(8,128)(2,1)} %collective-permute-done.4.refs_3_), channel_id=1, source_target_pairs={{0,1},{1,0},{2,3},{3,2},{4,5},{5,4},{6,7},{7,6},{8,9},{9,8},{10,11... | collective-permute-start | bytes 4718600 | tf_op jit(solution)/shard_map/ppermute | solution.py:992
  196.2 25.2 %collective-permute-start.19 = (bf16[768,1024]{1,0:T(8,128)(2,1)}, bf16[768,1024]{1,0:T(8,128)(2,1)}, u32[]{:S(2)}, u32[]{:S(2)}) collective-permute-start(bf16[768,1024]{1,0:T(8,128)(2,1)} %collective-permute-done.5.refs_5_), channel_id=1, source_target_pairs={{0,1},{1,0},{2,3},{3,2},{4,5},{5,4},{6,7},{7,6},{8,9},{9,8},{10,11... | collective-permute-start | bytes 4718600 | tf_op jit(solution)/shard_map/ppermute | solution.py:992
  196.7 71.2 %collective-permute-start.24 = (bf16[768,1024]{1,0:T(8,128)(2,1)}, bf16[768,1024]{1,0:T(8,128)(2,1)}, u32[]{:S(2)}, u32[]{:S(2)}) collective-permute-start(bf16[768,1024]{1,0:T(8,128)(2,1)} %collective-permute-done.11.refs_9_.refs_2_), channel_id=1, source_target_pairs={{0,2},{1,3},{2,0},{3,1},{4,6},{5,7},{6,4},{7,5},{8,10},{9,11},{10,... | collective-permute-start | bytes 4718600 | tf_op jit(solution)/shard_map/ppermute | solution.py:992
  218.1 52.5 %collective-permute-start.16 = (bf16[768,1024]{1,0:T(8,128)(2,1)}, bf16[768,1024]{1,0:T(8,128)(2,1)}, u32[]{:S(2)}, u32[]{:S(2)}) collective-permute-start(bf16[768,1024]{1,0:T(8,128)(2,1)} %collective-permute-done.7.refs_5_), channel_id=1, source_target_pairs={{0,2},{1,3},{2,0},{3,1},{4,6},{5,7},{6,4},{7,5},{8,10},{9,11},{10,... | collective-permute-start | bytes 4718600 | tf_op jit(solution)/shard_map/ppermute | solution.py:992
  219.4 48.5 %collective-permute-start.25 = (bf16[768,1024]{1,0:T(8,128)(2,1)}, bf16[768,1024]{1,0:T(8,128)(2,1)}, u32[]{:S(2)}, u32[]{:S(2)}) collective-permute-start(bf16[768,1024]{1,0:T(8,128)(2,1)} %collective-permute-done.14.refs_7_.refs_4_), channel_id=1, source_target_pairs={{0,4},{1,5},{2,6},{3,7},{4,0},{5,1},{6,2},{7,3},{8,12},{9,13},{10,... | collective-permute-start | bytes 4718600 | tf_op jit(solution)/shard_map/ppermute | solution.py:992
  221.1 69.0 %collective-permute-start.17 = (bf16[768,1024]{1,0:T(8,128)(2,1)}, bf16[768,1024]{1,0:T(8,128)(2,1)}, u32[]{:S(2)}, u32[]{:S(2)}) collective-permute-start(bf16[768,1024]{1,0:T(8,128)(2,1)} %collective-permute-done.4.refs_3_), channel_id=1, source_target_pairs={{0,4},{1,5},{2,6},{3,7},{4,0},{5,1},{6,2},{7,3},{8,12},{9,13},{10,... | collective-permute-start | bytes 4718600 | tf_op jit(solution)/shard_map/ppermute | solution.py:992
  267.9 22.8 %collective-permute-start.26 = (bf16[768,1024]{1,0:T(8,128)(2,1)}, bf16[768,1024]{1,0:T(8,128)(2,1)}, u32[]{:S(2)}, u32[]{:S(2)}) collective-permute-start(bf16[768,1024]{1,0:T(8,128)(2,1)} %collective-permute-done.24.refs_7_.refs_8_), channel_id=1, source_target_pairs={{0,1},{1,0},{2,3},{3,2},{4,5},{5,4},{6,7},{7,6},{8,9},{9,8},{10,11... | collective-permute-start | bytes 4718600 | tf_op jit(solution)/shard_map/ppermute | solution.py:992
  270.6 20.1 %collective-permute-start.27 = (bf16[768,1024]{1,0:T(8,128)(2,1)}, bf16[768,1024]{1,0:T(8,128)(2,1)}, u32[]{:S(2)}, u32[]{:S(2)}) collective-permute-start(bf16[768,1024]{1,0:T(8,128)(2,1)} %collective-permute-done.25.refs_9_.refs_10_), channel_id=1, source_target_pairs={{0,1},{1,0},{2,3},{3,2},{4,5},{5,4},{6,7},{7,6},{8,9},{9,8},{10,11... | collective-permute-start | bytes 4718600 | tf_op jit(solution)/shard_map/ppermute | solution.py:992
  436.0 417.1 %all-reduce.5.cloned.1.call-start = ((), (), s32[]{:S(2)}) async-start(), calls=%async_computation.3 | async-start | bytes 8388608 | tf_op jit(solution)/shard_map/psum | solution.py:1080
  (13 other events, 191.8 us)
Sparse Core Ops, SparseCore 0:
  436.1 126.5 all-reduce.2
  565.7 254.2 all-reduce.4

commit v4 on v3

--- a/solution.py
+++ b/solution.py
@@ -121,19 +121,20 @@
     return functools.reduce(jnp.logical_or, [rows == ids[j : j + 1, :] for j in range(ids.shape[FIRST])])
 
 
-def router_kernel(capacity, local, x_ref, w_ref, ids_ref, tab_ref, prob_ref, carry):
+def router_kernel(capacity, local, x_ref, wt_ref, ids_ref, tab_ref, prob_ref, stat_ref, carry):
     step = pl.program_id(FIRST)
     steps = pl.num_programs(FIRST)
-    experts = w_ref.shape[1]
+    experts = wt_ref.shape[FIRST]
 
     @pl.when(step == FIRST)
     def _():
         carry[...] = jnp.zeros_like(carry)
+        stat_ref[...] = jnp.zeros_like(stat_ref)
         tab_ref[...] = jnp.zeros_like(tab_ref)
 
     x = x_ref[...]
-    hi, mid, low = [dot(x, part) for part in split3(w_ref[...])]
-    logits = jnp.transpose(hi + (mid + low))
+    hi, mid, low = [dot_nt(part, x) for part in split3(wt_ref[...])]
+    logits = hi + (mid + low)
     expo = jnp.exp(logits - jnp.max(logits, axis=FIRST, keepdims=True))
     prob = expo / row_sum(expo)
     chosen = chosen_mask(ids_ref[...], experts)
@@ -148,34 +149,33 @@
     lane = iota((experts, LANES), 1)
     first = where0(lane == step, jnp.minimum(before, capacity) + jnp.zeros((experts, LANES), f32))
     first = first + where0((lane == step + 1) & (step == steps - 1), jnp.minimum(after, capacity) + jnp.zeros((experts, LANES), f32))
-    stat = where0(lane == FIRST, lane_sum(hits) + jnp.zeros((experts, LANES), f32))
-    stat = stat + where0(lane == 1, lane_sum(prob) + jnp.zeros((experts, LANES), f32))
+    stat_ref[...] += where0(lane == FIRST, lane_sum(hits) + jnp.zeros((experts, LANES), f32))
+    stat_ref[...] += where0(lane == 1, lane_sum(prob) + jnp.zeros((experts, LANES), f32))
     tail = slice(tab_ref.shape[LAST] - LANES, None)
     for d in range(experts // local):
         rows = slice(d * local, (d + 1) * local)
         tab_ref[d, :local, span(step * BLK, BLK)] = gate[rows]
         tab_ref[d, local:, span(step * BLK, BLK)] = pos[rows]
-        tab_ref[d, :local, tail] += stat[rows]
         tab_ref[d, local:, tail] += first[rows]
     carry[:, :1] = after
 
 
-def run_router(x_loc, w_router, ids_t, capacity, local, devices):
+def run_router(x_loc, w_t, ids_t, capacity, local, devices):
     tokens, d_model = x_loc.shape
-    experts = w_router.shape[1]
+    experts = w_t.shape[FIRST]
     top_k = ids_t.shape[FIRST]
     table = (devices, 2 * local, tokens + LANES)
     return pl.pallas_call(
         functools.partial(router_kernel, capacity, local),
         grid=(tokens // BLK,),
         in_specs=[pl.BlockSpec((BLK, d_model), lambda i: (i, FIRST)), VMEM, pl.BlockSpec((top_k, BLK), lambda i: (FIRST, i))],
-        out_specs=[VMEM, pl.BlockSpec((experts, BLK), lambda i: (FIRST, i))],
-        out_shape=[Shape(table, f32), Shape((experts, tokens), f32)],
+        out_specs=[VMEM, pl.BlockSpec((experts, BLK), lambda i: (FIRST, i)), VMEM],
+        out_shape=[Shape(table, f32), Shape((experts, tokens), f32), Shape((experts, LANES), f32)],
         scratch_shapes=[pltpu.VMEM((experts, LANES), f32)],
         compiler_params=params(),
         cost_estimate=cost(2 * tokens * d_model * BLK, 2 * tokens * d_model),
         name="router",
-    )(x_loc, w_router, ids_t)
+    )(x_loc, w_t, ids_t)
 
 
 class Blocks:
@@ -242,6 +242,10 @@
 
 def block_rows(first, count):
     return pl.ds(first * BLK, count * BLK)
+
+
+def tokens_in(ref, which):
+    return ref.at[which] if len(ref.shape) == 3 else ref
 
 
 def grad_kernel(g, last, local, pieces, *refs):
@@ -268,7 +272,7 @@
     def token_copies(k):
         c, at, to = parts[k]
         src_rows, dst_rows = block_rows(at, 3), block_rows(to, 3)
-        return [pltpu.make_async_copy(src[c].at[src_rows], dst.at[dst_rows], tok_sem.at[w, k]) for w, (src, dst) in enumerate(zip(tok_refs, (xv, dv)))]
+        return [pltpu.make_async_copy(tokens_in(src[c], w).at[src_rows], dst.at[dst_rows], tok_sem.at[w, k]) for w, (src, dst) in enumerate(zip(tok_refs, (xv, dv)))]
 
     def in_copies(ee, ss):
         return [pltpu.make_async_copy(src.at[ee], dst.at[ss], in_sem.at[ss, k]) for k, (src, dst) in enumerate(zip(acc_in, accs))]
@@ -453,10 +457,6 @@
     return np.asarray([v for k, c in enumerate(counts) for v in (sum(counts[:k]), c)], np.int32)
 
 
-def per_group(groups, *shape):
-    return pl.BlockSpec((1, 1, *shape), lambda step, e: (step + groups[FIRST], e) + (FIRST,) * len(shape))
-
-
 def per_local(*shape):
     return pl.BlockSpec((1, *shape), lambda g, e: (e,) + (FIRST,) * len(shape))
 
@@ -494,6 +494,7 @@
         step = pl.program_id(FIRST)
         self.e = pl.program_id(1)
         self.blocks = Blocks(starts_ref, bmap_ref)
+        self.spans = spans_ref
         self.first, self.count = spans_ref[2 * step], spans_ref[2 * step + 1]
         self.total = self.blocks.total(self.first, self.count, self.e)
         self.local, self.tab_ref, self.rows_ref = local, tab_ref, rows_ref
@@ -503,6 +504,25 @@
     def zero_tail(self):
         rows = span(padded(self.total), WIN)
         self.rows_ref[self.e, rows, :] = jnp.zeros((WIN, self.rows_ref.shape[LAST]), bf16)
+
+    def fetch(self, groups, arrays, held, sems):
+        now = pl.program_id(FIRST) * self.local + self.e
+
+        def each(step, act):
+            k, e = step // self.local, step % self.local
+            total = self.blocks.total(self.spans[2 * k], self.spans[2 * k + 1], e)
+
+            def one(i):
+                rows = span(i * TILE, TILE)
+                for w, array in enumerate(arrays):
+                    act(pltpu.make_async_copy(array.at[k + groups[FIRST], e, rows], held.at[step % 2, w, rows], sems.at[step % 2, w]))
+
+            loop(FIRST, padded(total) // TILE, one)
+
+        pl.when(now == FIRST)(lambda: each(now, lambda cp: cp.start()))
+        pl.when(now + 1 < self.local * len(groups))(lambda: each(now + 1, lambda cp: cp.start()))
+        each(now, lambda cp: cp.wait())
+        return now % 2
 
     def out_copy(self, i):
         slot = i % RING
@@ -544,24 +564,26 @@
         loop(stop - RING, stop, lambda i: self.out_copy(i).wait())
 
 
-def y_kernel(groups, local, starts_ref, bmap_ref, spans_ref, tab_ref, h_ref, w2_ref, *refs):
+def y_kernel(groups, local, starts_ref, bmap_ref, spans_ref, tab_ref, h_rows, w2_ref, *refs):
     take = taker(refs)
     d_refs = [take(len(GROUPS[g])) for g in groups]
-    y_ref, dg_ref, o_rows, dv, ring, zacc, yacc, dgacc, tok_sem, out_sem = take()
+    y_ref, dg_ref, o_rows, dv, ring, zacc, yacc, dgacc, tok_sem, out_sem, held, row_sem = take()
     all_rows = Combine(local, starts_ref, bmap_ref, spans_ref, tab_ref, o_rows, y_ref, ring, out_sem)
     e = all_rows.e
     d_model = dv.shape[1]
 
     def token_copies(step):
         spots = offsets(GROUPS[groups[step]])
-        return [pltpu.make_async_copy(src, dv.at[block_rows(*spot)], tok_sem.at[c]) for c, (src, spot) in enumerate(zip(d_refs[step], spots))]
+        return [pltpu.make_async_copy(tokens_in(src, 1), dv.at[block_rows(*spot)], tok_sem.at[c]) for c, (src, spot) in enumerate(zip(d_refs[step], spots))]
 
     for step in range(len(groups)):
         pl.when((pl.program_id(FIRST) == step) & (e == FIRST))(lambda: start(token_copies(step)))
 
+    slot = all_rows.fetch(groups, [h_rows], held, row_sem)
+
     def tile(at, size):
         rows = span(at, size)
-        o_rows[e, rows, :] = dot(h_ref[FIRST, FIRST, rows, :], w2_ref[FIRST]).astype(bf16)
+        o_rows[e, rows, :] = dot(held[slot, FIRST, rows, :], w2_ref[FIRST]).astype(bf16)
 
     row_tiles(all_rows.total, tile, 2 * TILE)
     all_rows.zero_tail()
@@ -624,23 +646,25 @@
     return pl.pallas_call(
         functools.partial(y_kernel, groups, local),
         grid=(len(groups), local),
-        in_specs=[SMEM, SMEM, SMEM, VMEM, per_group(groups, row_cap, d_ff), per_local(d_ff, d_model)] + [ANY] * len(pieces),
+        in_specs=[SMEM, SMEM, SMEM, VMEM, ANY, per_local(d_ff, d_model)] + [ANY] * len(pieces),
         out_specs=[ANY, VMEM],
         out_shape=[Shape((blocks, BLK, d_model), bf16), Shape((blocks, 2 * local, BLK), f32)],
-        scratch_shapes=rows + [pltpu.VMEM((max(spans[1::2]) * BLK, d_model), bf16)] + work + [work[LAST], pltpu.VMEM((local, BLK, LANES), f32), DMA((4,)), DMA((RING,))],
+        scratch_shapes=rows + [pltpu.VMEM((max(spans[1::2]) * BLK, d_model), bf16)] + work + [work[LAST], pltpu.VMEM((local, BLK, LANES), f32), DMA((4,)), DMA((RING,)), pltpu.VMEM((2, 1, row_cap, d_ff), bf16), DMA((2, 1))],
         compiler_params=grid_params(2),
         cost_estimate=cost(4 * blocks * BLK * d_model * d_ff, 20 << 20),
         name="expert_y",
     )(starts, block_map(pieces, nb), spans, tab, h_rows, w2, *[ds[p] for p in pieces])
 
 
-def dx_kernel(local, starts_ref, bmap_ref, spans_ref, tab_ref, da_ref, db_ref, w1_ref, w3_ref, dx_ref, o_rows, ring, zacc, out_sem):
+def dx_kernel(groups, local, starts_ref, bmap_ref, spans_ref, tab_ref, da_rows, db_rows, w1_ref, w3_ref, dx_ref, o_rows, ring, zacc, out_sem, held, row_sem):
     all_rows = Combine(local, starts_ref, bmap_ref, spans_ref, tab_ref, o_rows, dx_ref, ring, out_sem)
     e = all_rows.e
 
+    slot = all_rows.fetch(groups, [da_rows, db_rows], held, row_sem)
+
     def tile(at, size):
         rows = span(at, size)
-        grad = dot_nt(da_ref[FIRST, FIRST, rows, :], w1_ref[FIRST]) + dot_nt(db_ref[FIRST, FIRST, rows, :], w3_ref[FIRST])
+        grad = dot_nt(held[slot, FIRST, rows, :], w1_ref[FIRST]) + dot_nt(held[slot, 1, rows, :], w3_ref[FIRST])
         o_rows[e, rows, :] = grad.astype(bf16)
 
     row_tiles(all_rows.total, tile, 2 * TILE)
@@ -676,12 +700,12 @@
     blocks = block_count(pieces)
     rows, work = combine_scratch(local, row_cap, d_model)
     return pl.pallas_call(
-        functools.partial(dx_kernel, local),
+        functools.partial(dx_kernel, groups, local),
         grid=(len(groups), local),
-        in_specs=[SMEM, SMEM, SMEM, VMEM] + [per_group(groups, row_cap, d_ff)] * 2 + [per_local(d_model, d_ff)] * 2,
+        in_specs=[SMEM, SMEM, SMEM, VMEM] + [ANY] * 2 + [per_local(d_model, d_ff)] * 2,
         out_specs=ANY,
         out_shape=Shape((blocks, BLK, d_model), bf16),
-        scratch_shapes=rows + work + [DMA((RING,))],
+        scratch_shapes=rows + work + [DMA((RING,)), pltpu.VMEM((2, 2, row_cap, d_ff), bf16), DMA((2, 2))],
         compiler_params=grid_params(2),
         cost_estimate=cost(6 * blocks * BLK * d_model * d_ff, 20 << 20),
         name="expert_dx",
@@ -996,19 +1020,23 @@
     return lax.optimization_barrier((values, token))[FIRST]
 
 
-def send_own(v, token):
-    got = {(FIRST, *WHOLE): v, (CORE, *WHOLE): hop(v, CORE)}
-    pieces = after([v[first * BLK : (first + count) * BLK] for first, count in PARTS], token)
-    for part, piece in zip(PARTS, pieces):
-        got.update({(bit, *part): hop(piece, bit) for bit in NEAR})
+def send_own(x_loc, dy_loc, token):
+    got = {(FIRST, *WHOLE): (x_loc, dy_loc), (CORE, *WHOLE): (hop(x_loc, CORE), hop(dy_loc, CORE))}
+    both = [jnp.stack([v[first * BLK : (first + count) * BLK] for v in (x_loc, dy_loc)]) for first, count in PARTS]
+    for part, piece in zip(PARTS, after(both, token)):
+        got.update({(bit, *part): (hop(piece, bit),) * 2 for bit in NEAR})
     return got
 
 
 def pass_on(got, h):
     part = PARTS[h]
-    got[FAR, *part] = hop(got[(Y, X)[h], *part], NEAR[h])
+    got[FAR, *part] = (hop(got[(Y, X)[h], *part][FIRST], NEAR[h]),) * 2
     for bit in NEAR:
-        got[bit | CORE, *part] = hop(got[bit, *part], CORE)
+        pass_core(got, bit, part)
+
+
+def pass_core(got, bits, part):
+    got[bits | CORE, *part] = (hop(got[bits, *part][FIRST], CORE),) * 2
 
 
 def relative(v, me):
@@ -1038,15 +1066,19 @@
         me = lax.axis_index("ep")
 
         ids_t = ids_loc.T
-        send_tab, prob_t = run_router(x_loc, w_router, ids_t, capacity, local, ep_size)
+        w_t = w_router.T
+        send_tab, prob_t, stats = run_router(x_loc, w_t, ids_t, capacity, local, ep_size)
         tables = lax.all_to_all(send_tab, "ep", FIRST, FIRST, tiled=True)
-        gathered = [send_own(v, tables) for v in (x_loc, dy_loc)]
+        stats = jnp.pad(stats[:, :2].T, ((0, local - 2), (0, LANES - experts)))
+        for step in (1, 2):
+            stats = stats + lax.ppermute(stats, "dp", [(i, i ^ step) for i in range(dp_size)])
+        gathered = send_own(x_loc, dy_loc, (tables, stats))
         tab_rel = relative(tables, me)
         tab = tab_rel[:, :, :tokens].reshape(ep_size, 2 * local, nb, BLK).transpose(0, 2, 1, 3).reshape(ep_size * nb, 2 * local, BLK)
         starts = tab_rel[:, local:, tokens : tokens + ALIGN].astype(i32).reshape(LAST)
 
         def y_of(groups, starts):
-            return run_y(groups, starts, tab, rows[FIRST], w2, gathered[1], nb)
+            return run_y(groups, starts, tab, rows[FIRST], w2, {p: v[1] for p, v in gathered.items()}, nb)
 
         def dx_of(groups, starts):
             return run_dx(groups, starts, tab, rows[1], rows[2], w1, w3, nb)
@@ -1056,24 +1088,20 @@
         for g, group in enumerate(GROUPS):
             if g:
                 ready = [p for p in group if not p[FIRST] & CORE]
-                for got in gathered:
-                    got.update(after({p: got[p] for p in ready}, (acc[LAST], dg_own)))
-                for got in gathered:
-                    if g < len(GROUPS) - 1:
-                        pass_on(got, g - 1)
-                    else:
-                        for src, *part in ready:
-                            got[src | CORE, *part] = hop(got[src, *part], CORE)
-                here = after(starts, [[got[p] for p in ready] for got in gathered])
+                arrived = after([gathered[p][FIRST] for p in ready], (acc[LAST], dg_own))
+                gathered.update({p: (v, v) for p, v in zip(ready, arrived)})
+                if g < len(GROUPS) - 1:
+                    pass_on(gathered, g - 1)
+                else:
+                    for src, *part in ready:
+                        pass_core(gathered, src, part)
+                here = after(starts, arrived)
                 if g == 2:
                     dx_own = dx_of(own, here)
                     starts = after(starts, dx_own)
-            rows, acc = run_grad(starts, tab, g, *[[got[p] for p in group] for got in gathered], (w1, w3, w2), acc, rows, nb, row_cap)
+            rows, acc = run_grad(starts, tab, g, *zip(*[gathered[p] for p in group]), (w1, w3, w2), acc, rows, nb, row_cap)
             if not g:
-                stats = jnp.sum(after(tab_rel[:, :local, tokens:], acc[LAST]), axis=FIRST)
-                for step in (1, 2):
-                    stats = stats + lax.ppermute(stats, "dp", [(i, i ^ step) for i in range(dp_size)])
-                y_own, dg_own = y_of(own, after(starts, stats))
+                y_own, dg_own = y_of(own, after(starts, acc[LAST]))
                 starts = after(starts, dg_own)
         dw1, dw3, dw2 = acc
         starts, dw2 = lax.optimization_barrier((starts, dw2))
@@ -1085,16 +1113,17 @@
         dg = jnp.concatenate([relative(dg, me), jnp.broadcast_to(stats, (ep_size, *stats.shape))], axis=2)
         starts, dg = lax.optimization_barrier((starts, dg))
         dx_rest = dx_of(rest, starts)
-        dg_all = lax.all_to_all(dg, "ep", FIRST, FIRST, tiled=True).reshape(experts, tokens + LANES)
-        load = dg_all[:, tokens:]
+        dg_all = lax.all_to_all(dg, "ep", FIRST, FIRST, tiled=True)
+        load, prob_sum = jnp.sum(dg_all[:, :2, tokens : tokens + experts], axis=FIRST)
         share = AUX_COEF * experts / (n_total * top_k * n_total)
-        aux_loss = share * jnp.sum(load[:, FIRST] * load[:, 1])
-        dlog_t, dwr_t = run_router_grad(x_loc, prob_t, dg_all[:, :tokens], ids_t, load, share)
+        aux_loss = share * jnp.sum(load * prob_sum)
+        load = jnp.broadcast_to(load[:, None], (experts, LANES))
+        dlog_t, dwr_t = run_router_grad(x_loc, prob_t, dg_all[:, :, :tokens].reshape(experts, tokens), ids_t, load, share)
         dw_router = lax.psum(dwr_t, ("dp", "ep")).T
 
         parts = [[v.reshape(LAST, tokens, d_model) for v in pair] for pair in ((y_own, y_rest), (dx_own, dx_rest))]
         sums, grads = run_exchange(parts, [dw1, dw3])
-        y_loc, dx_loc = run_final(dlog_t, w_router.T, *sums)
+        y_loc, dx_loc = run_final(dlog_t, w_t, *sums)
         return y_loc, aux_loss, dx_loc, dw_router, *grads, dw2_sum
 
     return jax.shard_map(

time: 882 us -> 862 us (0.977)
  waiting for transfers between devices: 55.5 us -> 37.2 us
    ppermute x26 -> x14, waiting for transfers between devices: 47 us -> 33.5 us  [hop(): return lax.ppermute(v, 'ep', [(i, i ^ bit) for i in SOURCES])]
    ppermute x26 -> x14, starting transfers between devices: 21.3 us -> 16.6 us  [hop(): return lax.ppermute(v, 'ep', [(i, i ^ bit) for i in SOURCES])]
  transfers between devices with their start and end apart: 31 -> 19, of which waited for: 10 -> 7; matrix products, arithmetic and copies ran while one was open for 2% -> 1% of each run, Pallas kernels for 70% -> 72%
where the time goes in v4:
time: 862 us; the launch traced here: 853 us
  Pallas kernels  740 us (86%)
  waiting for transfers between devices  37.2 us (4%)
  starting transfers between devices  25.8 us (3%)
  local copies, waits for them, and re-layouts  18.7 us (2%)
  between operations  16.6 us (2%)
  blocking collectives  9.25 us (1%)
    pallas_call x1, Pallas kernels, run_exchange(): pl.pallas_call(functools.partial(exchange_kernel, half, len(dws)), in_spe...  347 us
    pallas_call x4, Pallas kernels, run_grad(): pl.pallas_call(functools.partial(grad_kernel, g, last, local, pieces), gr...  189 us
    pallas_call x2, Pallas kernels, run_y(): pl.pallas_call(functools.partial(y_kernel, groups, local), grid=(len(grou...  100 us
    pallas_call x2, Pallas kernels, run_dx(): pl.pallas_call(functools.partial(dx_kernel, groups, local), grid=(len(gro...  80 us
    ppermute x14, waiting for transfers between devices, hop(): return lax.ppermute(v, 'ep', [(i, i ^ bit) for i in SOURCES])  33.5 us
  transfers between devices with their start and end apart: 19, of which 7 were waited for; matrix products, arithmetic and copies ran while one was open for 1% of the time, Pallas kernels for 72%

profile of v4, /device:TPU:0, one launch (start us, length us, event | category | flops | bytes accessed | tf_op | source)
XLA Modules:
  0.0 852.5 jit_solution(4731871655341600187)
XLA Ops:
  7.7 6.8 router.1
  14.5 4.8 all-to-all-start
  24.7 3.0 pad_maximum_fusion
  27.7 2.7 collective-permute-start.3
  30.9 3.0 collective-permute-done.3
  39.0 46.9 %expert_grad.4 = (bf16[4,4,2048,512]{3,2,1,0:T(8,128)(2,1)}, bf16[4,4,2048,512]{3,2,1,0:T(8,128)(2,1)}, bf16[4,4,2048,512]{3,2,1,0:T(8,128)(2,1)}, f32[4,1024,1024]{2,1,0:T(8,128)}, f32[4,512,1024]{2,1,0:T(8,128)}) custom-call(s32[512]{0:T(512)} %reshape.53.refs_0_.starts_ref, s32[24]{0:T(128)} %constant.32.clone.refs_1_.bmap_ref, f32[48,8,256]{2,1,0:T(8,128)} %bitcast.38, ...), custom_call_target="tpu_custom_call" | custom-call | flops 19327352832 | bytes 41943040 | tf_op jit(solution)/shard_map/expert_grad/pallas_call | solution.py:438
  85.9 26.8 %expert_y.2 = (bf16[12,256,1024]{2,1,0:T(8,128)(2,1)}, f32[12,8,256]{2,1,0:T(8,128)}) custom-call(s32[512]{0:T(512)} %reshape.53.refs_0_.starts_ref, s32[24]{0:T(128)} %constant.32.clone.refs_1_.bmap_ref, s32[2]{0:T(128)} %iota_multiply_fusion.spans_ref, f32[48,8,256]{2,1,0:T(8,128)} %bitcast.39, ...), custom_call_target="tpu_custom_call" | custom-call | flops 6442450944 | bytes 20971520 | tf_op jit(solution)/shard_map/expert_y/pallas_call | solution.py:646
  112.7 3.9 collective-permute-start.8
  118.5 3.7 collective-permute-done.8.refs_4_.refs_8_.refs_1_
  122.2 4.5 collective-permute-done.9.refs_6_.refs_10_.refs_3_
  126.7 46.3 %expert_grad.5 = (bf16[4,4,2048,512]{3,2,1,0:T(8,128)(2,1)}, bf16[4,4,2048,512]{3,2,1,0:T(8,128)(2,1)}, bf16[4,4,2048,512]{3,2,1,0:T(8,128)(2,1)}, f32[4,1024,1024]{2,1,0:T(8,128)}, f32[4,512,1024]{2,1,0:T(8,128)}) custom-call(s32[512]{0:T(512)} %reshape.53.refs_0_.starts_ref, ...), custom_call_target="tpu_custom_call", output_to_operand_aliasing={{0}: (16, {}), {1}: (17, {}), {2}: (18, {})} | custom-call | flops 19327352832 | bytes 41943040 | tf_op jit(solution)/shard_map/expert_grad/pallas_call | solution.py:438
  173.0 14.4 %collective-permute-done.4.refs_3_.refs_7_.refs_4_ = bf16[2,768,1024]{2,1,0:T(8,128)(2,1)} collective-permute-done((bf16[2,768,1024]{2,1,0:T(8,128)(2,1)}, bf16[2,768,1024]{2,1,0:T(8,128)(2,1)}, u32[]{:S(2)}, u32[]{:S(2)}) %collective-permute-start.4) | collective-permute-done | bytes 3145760 | tf_op jit(solution)/shard_map/ppermute | solution.py:1016
  191.2 21.2 %expert_dx.2 = bf16[12,256,1024]{2,1,0:T(8,128)(2,1)} custom-call(s32[512]{0:T(512)} %reshape.53.refs_0_.starts_ref, s32[24]{0:T(128)} %constant.32.clone.refs_1_.bmap_ref, s32[2]{0:T(128)} %iota_multiply_fusion.spans_ref, f32[48,8,256]{2,1,0:T(8,128)} %bitcast.41, bf16[4,4,2048,512]{3,2,1,0:T(8,128)(2,1)} %get-tuple-element.82.da_rows.refs_17_, ...), custom_call_target="tpu_custom_call" | custom-call | flops 9663676416 | bytes 20971520 | tf_op jit(solution)/shard_map/expert_dx/pallas_call | solution.py:702
  212.4 46.5 %expert_grad.6 = (bf16[4,4,2048,512]{3,2,1,0:T(8,128)(2,1)}, bf16[4,4,2048,512]{3,2,1,0:T(8,128)(2,1)}, bf16[4,4,2048,512]{3,2,1,0:T(8,128)(2,1)}, f32[4,1024,1024]{2,1,0:T(8,128)}, f32[4,512,1024]{2,1,0:T(8,128)}) custom-call(s32[512]{0:T(512)} %reshape.53.refs_0_.starts_ref, ...), custom_call_target="tpu_custom_call", output_to_operand_aliasing={{0}: (16, {}), {1}: (17, {}), {2}: (18, {})} | custom-call | flops 19327352832 | bytes 41943040 | tf_op jit(solution)/shard_map/expert_grad/pallas_call | solution.py:438
  262.4 5.5 collective-permute-done.14.refs_4_.refs_8_.refs_9_
  267.9 4.5 collective-permute-done.15.refs_6_.refs_10_.refs_11_
  272.4 49.6 %expert_grad.7 = (bf16[4,4,2048,512]{3,2,1,0:T(8,128)(2,1)}, bf16[4,4,2048,512]{3,2,1,0:T(8,128)(2,1)}, bf16[4,4,2048,512]{3,2,1,0:T(8,128)(2,1)}, bf16[4,1024,5...) custom-call(s32[512]{0:T(512)} %reshape.53.refs_0_.starts_ref, ...), custom_call_target="tpu_custom_call", output_to_operand_aliasing={{0}: (16, {}), {1}: (17, {}), {2}: (18, {})} | custom-call | flops 19327352832 | bytes 41943040 | tf_op jit(solution)/shard_map/expert_grad/pallas_call | solution.py:438
  322.1 73.2 %expert_y.3 = (bf16[36,256,1024]{2,1,0:T(8,128)(2,1)}, f32[36,8,256]{2,1,0:T(8,128)}) custom-call(s32[512]{0:T(512)} %reshape.53.refs_0_.starts_ref, s32[72]{0:T(128)} %constant.37.clone.bmap_ref, s32[6]{0:T(128)} %constant.38.clone.spans_ref, f32[48,8,256]{2,1,0:T(8,128)} %bitcast.44, bf16[4,4,2048,512]{3,2,1,0:T(8,128)(2,1)} %get-tuple-element.96.h_rows, ...), custom_call_target="tpu_custom_call" | custom-call | flops 19327352832 | bytes 20971520 | tf_op jit(solution)/shard_map/expert_y/pallas_call | solution.py:646
  396.5 9.3 %all_to_all.10 = f32[8,4,1664]{2,1,0:T(4,128)S(1)} all-to-all(f32[8,4,1664]{2,1,0:T(4,128)S(1)} %pad_maximum_fusion.2), channel_id=1, replica_groups=mesh['dp'=4,'ep'=8] {'ep'}, dimensions={0} | all-to-all | bytes 425984 | tf_op jit(solution)/shard_map/all_to_all | solution.py:1116
  407.8 5.7 router_grad.1
  414.3 58.8 %expert_dx.3 = bf16[36,256,1024]{2,1,0:T(8,128)(2,1)} custom-call(s32[512]{0:T(512)} %reshape.53.refs_0_.starts_ref, s32[72]{0:T(128)} %constant.37.clone.bmap_ref, s32[6]{0:T(128)} %constant.38.clone.spans_ref, f32[48,8,256]{2,1,0:T(8,128)} %bitcast.45, bf16[4,4,2048,512]{3,2,1,0:T(8,128)(2,1)} %get-tuple-element.103.da_rows, ...), custom_call_target="tpu_custom_call" | custom-call | flops 28991029248 | bytes 20971520 | tf_op jit(solution)/shard_map/expert_dx/pallas_call | solution.py:702
  473.1 346.9 %exchange.1 = (bf16[1536,1024]{1,0:T(8,128)(2,1)}, bf16[1536,1024]{1,0:T(8,128)(2,1)}, bf16[1536,1024]{1,0:T(8,128)(2,1)}, bf16[1536,1024]{1,0:T(8,128)(2,1)}, b...) custom-call(bf16[2,1536,1024]{2,1,0:T(8,128)(2,1)} %bitcast.58, ...), custom_call_target="tpu_custom_call" | custom-call | flops 137438953472 | bytes 209715200 | tf_op jit(solution)/shard_map/exchange/pallas_call | solution.py:985
  821.3 10.7 %final.1 = (bf16[1536,1024]{1,0:T(8,128)(2,1)}, bf16[1536,1024]{1,0:T(8,128)(2,1)}) custom-call(f32[32,1536]{1,0:T(8,128)} %get-tuple-element.99.dlog_ref, f32[32,1024]{1,0:T(8,128)} %bitcast.53, bf16[1536,1024]{1,0:T(8,128)(2,1)} %get-tuple-element.107.refs_0_, bf16[1536,1024]{1,0:T(8,128)(2,1)} %get-tuple-element.108.refs_1_, ...), custom_call_target="tpu_custom_call" | custom-call | flops 805306368 | bytes 25165824 | tf_op jit(solution)/shard_map/final/pallas_call | solution.py:769
  833.7 4.6 copy.50
  (72 shorter events, 32.5 us)
Async XLA Ops:
  7.2 31.8 %collective-permute-start = (bf16[1536,1024]{1,0:T(8,128)(2,1)}, bf16[1536,1024]{1,0:T(8,128)(2,1)}, u32[]{:S(2)}, u32[]{:S(2)}) collective-permute-start(bf16[1536,1024]{1,0:T(8,128)(2,1)} %x_ref.3), channel_id=1, source_target_pairs={{0,1},{1,0},{2,3},{3,2},{4,5},{5,4},{6,7},{7,6},{8,9},{9,8},{10,11... | collective-permute-start | bytes 9437192 | tf_op jit(solution)/shard_map/ppermute | solution.py:1016
  14.5 19.4 %all-to-all-start = ((f32[8,8,1664]{2,1,0:T(8,128)}), f32[8,8,1664]{2,1,0:T(8,128)S(1)}, u32[]{:S(2)}, u32[]{:S(2)}) async-start(f32[8,8,1664]{2,1,0:T(8,128)} %get-tuple-element.64), calls=%async_computation | async-start | bytes 851968 | tf_op jit(solution)/shard_map/all_to_all | solution.py:1071
  19.3 812.8 %all-reduce.4.cloned.1.call-start = ((), (), s32[]{:S(2)}) async-start(), calls=%async_computation.2 | async-start | bytes 262144 | tf_op jit(solution)/shard_map/psum | solution.py:1122
  19.4 19.6 %collective-permute-start.1 = (bf16[1536,1024]{1,0:T(8,128)(2,1)}, bf16[1536,1024]{1,0:T(8,128)(2,1)}, u32[]{:S(2)}, u32[]{:S(2)}) collective-permute-start(bf16[1536,1024]{1,0:T(8,128)(2,1)} %refs_0_.1), channel_id=1, source_target_pairs={{0,1},{1,0},{2,3},{3,2},{4,5},{5,4},{6,7},{7,6},{8,9},{9,8},{10,11... | collective-permute-start | bytes 9437192 | tf_op jit(solution)/shard_map/ppermute | solution.py:1016
  20.6 3.8 copy-start
  20.6 7.2 collective-permute-start.2
  27.7 6.2 collective-permute-start.3
  34.0 78.7 %collective-permute-start.6 = (bf16[2,768,1024]{2,1,0:T(8,128)(2,1)}, bf16[2,768,1024]{2,1,0:T(8,128)(2,1)}, u32[]{:S(2)}, u32[]{:S(2)}) collective-permute-start(bf16[2,768,1024]{2,1,0:T(8,128)(2,1)} %get-tuple-element.72), channel_id=1, source_target_pairs={{0,2},{1,3},{2,0},{3,1},{4,6},{5,7},{6,4},{7,5},{8,10},{9,11},{10,... | collective-permute-start | bytes 9437192 | tf_op jit(solution)/shard_map/ppermute | solution.py:1016
  35.9 76.8 %collective-permute-start.7 = (bf16[2,768,1024]{2,1,0:T(8,128)(2,1)}, bf16[2,768,1024]{2,1,0:T(8,128)(2,1)}, u32[]{:S(2)}, u32[]{:S(2)}) collective-permute-start(bf16[2,768,1024]{2,1,0:T(8,128)(2,1)} %get-tuple-element.72), channel_id=1, source_target_pairs={{0,4},{1,5},{2,6},{3,7},{4,0},{5,1},{6,2},{7,3},{8,12},{9,13},{10,... | collective-permute-start | bytes 9437192 | tf_op jit(solution)/shard_map/ppermute | solution.py:1016
  112.7 9.5 %collective-permute-start.8 = (bf16[2,768,1024]{2,1,0:T(8,128)(2,1)}, bf16[2,768,1024]{2,1,0:T(8,128)(2,1)}, u32[]{:S(2)}, u32[]{:S(2)}) collective-permute-start(bf16[2,768,1024]{2,1,0:T(8,128)(2,1)} %collective-permute-done.6.refs_3_.refs_7_.refs_0_), channel_id=1, source_target_pairs={{0,1},{1,0},{2,3},{3,2},{4,5},{5,4},{6,7},{7,6},{8,9},{9,8},{10,11... | collective-permute-start | bytes 9437192 | tf_op jit(solution)/shard_map/ppermute | solution.py:1016
  116.6 10.1 %collective-permute-start.9 = (bf16[2,768,1024]{2,1,0:T(8,128)(2,1)}, bf16[2,768,1024]{2,1,0:T(8,128)(2,1)}, u32[]{:S(2)}, u32[]{:S(2)}) collective-permute-start(bf16[2,768,1024]{2,1,0:T(8,128)(2,1)} %collective-permute-done.7.refs_5_.refs_9_.refs_2_), channel_id=1, source_target_pairs={{0,1},{1,0},{2,3},{3,2},{4,5},{5,4},{6,7},{7,6},{8,9},{9,8},{10,11... | collective-permute-start | bytes 9437192 | tf_op jit(solution)/shard_map/ppermute | solution.py:1016
  116.7 70.8 %collective-permute-start.4 = (bf16[2,768,1024]{2,1,0:T(8,128)(2,1)}, bf16[2,768,1024]{2,1,0:T(8,128)(2,1)}, u32[]{:S(2)}, u32[]{:S(2)}) collective-permute-start(bf16[2,768,1024]{2,1,0:T(8,128)(2,1)} %get-tuple-element.71), channel_id=1, source_target_pairs={{0,2},{1,3},{2,0},{3,1},{4,6},{5,7},{6,4},{7,5},{8,10},{9,11},{10,... | collective-permute-start | bytes 9437192 | tf_op jit(solution)/shard_map/ppermute | solution.py:1016
  116.7 70.8 %collective-permute-start.5 = (bf16[2,768,1024]{2,1,0:T(8,128)(2,1)}, bf16[2,768,1024]{2,1,0:T(8,128)(2,1)}, u32[]{:S(2)}, u32[]{:S(2)}) collective-permute-start(bf16[2,768,1024]{2,1,0:T(8,128)(2,1)} %get-tuple-element.71), channel_id=1, source_target_pairs={{0,4},{1,5},{2,6},{3,7},{4,0},{5,1},{6,2},{7,3},{8,12},{9,13},{10,... | collective-permute-start | bytes 9437192 | tf_op jit(solution)/shard_map/ppermute | solution.py:1016
  187.4 24.9 %collective-permute-start.12 = (bf16[2,768,1024]{2,1,0:T(8,128)(2,1)}, bf16[2,768,1024]{2,1,0:T(8,128)(2,1)}, u32[]{:S(2)}, u32[]{:S(2)}) collective-permute-start(bf16[2,768,1024]{2,1,0:T(8,128)(2,1)} %collective-permute-done.4.refs_3_.refs_7_.refs_4_), channel_id=1, source_target_pairs={{0,1},{1,0},{2,3},{3,2},{4,5},{5,4},{6,7},{7,6},{8,9},{9,8},{10,11... | collective-permute-start | bytes 9437192 | tf_op jit(solution)/shard_map/ppermute | solution.py:1016
  187.4 25.0 %collective-permute-start.13 = (bf16[2,768,1024]{2,1,0:T(8,128)(2,1)}, bf16[2,768,1024]{2,1,0:T(8,128)(2,1)}, u32[]{:S(2)}, u32[]{:S(2)}) collective-permute-start(bf16[2,768,1024]{2,1,0:T(8,128)(2,1)} %collective-permute-done.5.refs_5_.refs_9_.refs_6_), channel_id=1, source_target_pairs={{0,1},{1,0},{2,3},{3,2},{4,5},{5,4},{6,7},{7,6},{8,9},{9,8},{10,11... | collective-permute-start | bytes 9437192 | tf_op jit(solution)/shard_map/ppermute | solution.py:1016
  187.9 70.9 %collective-permute-start.10 = (bf16[2,768,1024]{2,1,0:T(8,128)(2,1)}, bf16[2,768,1024]{2,1,0:T(8,128)(2,1)}, u32[]{:S(2)}, u32[]{:S(2)}) collective-permute-start(bf16[2,768,1024]{2,1,0:T(8,128)(2,1)} %collective-permute-done.7.refs_5_.refs_9_.refs_2_), channel_id=1, source_target_pairs={{0,2},{1,3},{2,0},{3,1},{4,6},{5,7},{6,4},{7,5},{8,10},{9,11},{10,... | collective-permute-start | bytes 9437192 | tf_op jit(solution)/shard_map/ppermute | solution.py:1016
  189.7 70.0 %collective-permute-start.11 = (bf16[2,768,1024]{2,1,0:T(8,128)(2,1)}, bf16[2,768,1024]{2,1,0:T(8,128)(2,1)}, u32[]{:S(2)}, u32[]{:S(2)}) collective-permute-start(bf16[2,768,1024]{2,1,0:T(8,128)(2,1)} %collective-permute-done.4.refs_3_.refs_7_.refs_4_), channel_id=1, source_target_pairs={{0,4},{1,5},{2,6},{3,7},{4,0},{5,1},{6,2},{7,3},{8,12},{9,13},{10,... | collective-permute-start | bytes 9437192 | tf_op jit(solution)/shard_map/ppermute | solution.py:1016
  259.7 8.2 collective-permute-start.14
  262.3 10.1 %collective-permute-start.15 = (bf16[2,768,1024]{2,1,0:T(8,128)(2,1)}, bf16[2,768,1024]{2,1,0:T(8,128)(2,1)}, u32[]{:S(2)}, u32[]{:S(2)}) collective-permute-start(bf16[2,768,1024]{2,1,0:T(8,128)(2,1)} %collective-permute-done.11.refs_5_.refs_9_.refs_10_), channel_id=1, source_target_pairs={{0,1},{1,0},{2,3},{3,2},{4,5},{5,4},{6,7},{7,6},{8,9},{9,8},{10,11... | collective-permute-start | bytes 9437192 | tf_op jit(solution)/shard_map/ppermute | solution.py:1016
  322.1 73.3 %copy-start.3 = (f32[12,8,256]{2,1,0:T(8,128)S(1)}, f32[12,8,256]{2,1,0:T(8,128)}, u32[]{:S(2)}) copy-start(f32[12,8,256]{2,1,0:T(8,128)} %get-tuple-element.68) | copy-start | bytes 294916
  413.5 418.6 %all-reduce.6.cloned.1.call-start = ((), (), s32[]{:S(2)}) async-start(), calls=%async_computation.3 | async-start | bytes 8388608 | tf_op jit(solution)/shard_map/psum | solution.py:1108
  473.1 347.0 %copy-start.5 = (f32[2,32]{1,0:T(2,128)S(1)}, f32[2,32]{1,0:T(2,128)}, u32[]{:S(2)}) copy-start(f32[2,32]{1,0:T(2,128)} %copy-done.4) | copy-start | bytes 772
  833.7 4.6 copy-start.2
  838.3 3.7 copy-start.1
  (1 other events, 0.6 us)
Sparse Core Ops, SparseCore 0:
  413.7 129.6 all-reduce.3
  546.3 255.2 all-reduce.5

commit v5 on v4

--- a/solution.py
+++ b/solution.py
@@ -457,6 +457,16 @@
     return np.asarray([v for k, c in enumerate(counts) for v in (sum(counts[:k]), c)], np.int32)
 
 
+def row_totals(groups, starts):
+    firsts = starts.reshape(len(SOURCES), LAST, ALIGN)
+    use = np.zeros((len(groups), len(SOURCES), 1, ALIGN), np.int32)
+    for k, g in enumerate(groups):
+        for src, first, count in GROUPS[g]:
+            use[k, src, FIRST, first + count] += 1
+            use[k, src, FIRST, first] -= 1
+    return jnp.sum(use * firsts, axis=(1, 3)).reshape(LAST)
+
+
 def per_local(*shape):
     return pl.BlockSpec((1, *shape), lambda g, e: (e,) + (FIRST,) * len(shape))
 
@@ -490,13 +500,13 @@
 
 
 class Combine:
-    def __init__(self, local, starts_ref, bmap_ref, spans_ref, tab_ref, rows_ref, out_ref, ring, sems):
+    def __init__(self, local, starts_ref, bmap_ref, spans_ref, totals_ref, tab_ref, rows_ref, out_ref, ring, sems):
         step = pl.program_id(FIRST)
+        self.totals = totals_ref
         self.e = pl.program_id(1)
         self.blocks = Blocks(starts_ref, bmap_ref)
-        self.spans = spans_ref
         self.first, self.count = spans_ref[2 * step], spans_ref[2 * step + 1]
-        self.total = self.blocks.total(self.first, self.count, self.e)
+        self.total = totals_ref[step * local + self.e]
         self.local, self.tab_ref, self.rows_ref = local, tab_ref, rows_ref
         self.out_ref, self.ring, self.sems = out_ref, ring, sems
         self.lane = iota((BLK, WIN), 1).astype(f32)
@@ -510,14 +520,13 @@
 
         def each(step, act):
             k, e = step // self.local, step % self.local
-            total = self.blocks.total(self.spans[2 * k], self.spans[2 * k + 1], e)
 
             def one(i):
                 rows = span(i * TILE, TILE)
                 for w, array in enumerate(arrays):
                     act(pltpu.make_async_copy(array.at[k + groups[FIRST], e, rows], held.at[step % 2, w, rows], sems.at[step % 2, w]))
 
-            loop(FIRST, padded(total) // TILE, one)
+            loop(FIRST, padded(self.totals[step]) // TILE, one)
 
         pl.when(now == FIRST)(lambda: each(now, lambda cp: cp.start()))
         pl.when(now + 1 < self.local * len(groups))(lambda: each(now + 1, lambda cp: cp.start()))
@@ -564,11 +573,11 @@
         loop(stop - RING, stop, lambda i: self.out_copy(i).wait())
 
 
-def y_kernel(groups, local, starts_ref, bmap_ref, spans_ref, tab_ref, h_rows, w2_ref, *refs):
+def y_kernel(groups, local, starts_ref, bmap_ref, spans_ref, totals_ref, tab_ref, h_rows, w2_ref, *refs):
     take = taker(refs)
     d_refs = [take(len(GROUPS[g])) for g in groups]
     y_ref, dg_ref, o_rows, dv, ring, zacc, yacc, dgacc, tok_sem, out_sem, held, row_sem = take()
-    all_rows = Combine(local, starts_ref, bmap_ref, spans_ref, tab_ref, o_rows, y_ref, ring, out_sem)
+    all_rows = Combine(local, starts_ref, bmap_ref, spans_ref, totals_ref, tab_ref, o_rows, y_ref, ring, out_sem)
     e = all_rows.e
     d_model = dv.shape[1]
 
@@ -646,18 +655,18 @@
     return pl.pallas_call(
         functools.partial(y_kernel, groups, local),
         grid=(len(groups), local),
-        in_specs=[SMEM, SMEM, SMEM, VMEM, ANY, per_local(d_ff, d_model)] + [ANY] * len(pieces),
+        in_specs=[SMEM, SMEM, SMEM, SMEM, VMEM, ANY, per_local(d_ff, d_model)] + [ANY] * len(pieces),
         out_specs=[ANY, VMEM],
         out_shape=[Shape((blocks, BLK, d_model), bf16), Shape((blocks, 2 * local, BLK), f32)],
         scratch_shapes=rows + [pltpu.VMEM((max(spans[1::2]) * BLK, d_model), bf16)] + work + [work[LAST], pltpu.VMEM((local, BLK, LANES), f32), DMA((4,)), DMA((RING,)), pltpu.VMEM((2, 1, row_cap, d_ff), bf16), DMA((2, 1))],
         compiler_params=grid_params(2),
         cost_estimate=cost(4 * blocks * BLK * d_model * d_ff, 20 << 20),
         name="expert_y",
-    )(starts, block_map(pieces, nb), spans, tab, h_rows, w2, *[ds[p] for p in pieces])
-
-
-def dx_kernel(groups, local, starts_ref, bmap_ref, spans_ref, tab_ref, da_rows, db_rows, w1_ref, w3_ref, dx_ref, o_rows, ring, zacc, out_sem, held, row_sem):
-    all_rows = Combine(local, starts_ref, bmap_ref, spans_ref, tab_ref, o_rows, dx_ref, ring, out_sem)
+    )(starts, block_map(pieces, nb), spans, row_totals(groups, starts), tab, h_rows, w2, *[ds[p] for p in pieces])
+
+
+def dx_kernel(groups, local, starts_ref, bmap_ref, spans_ref, totals_ref, tab_ref, da_rows, db_rows, w1_ref, w3_ref, dx_ref, o_rows, ring, zacc, out_sem, held, row_sem):
+    all_rows = Combine(local, starts_ref, bmap_ref, spans_ref, totals_ref, tab_ref, o_rows, dx_ref, ring, out_sem)
     e = all_rows.e
 
     slot = all_rows.fetch(groups, [da_rows, db_rows], held, row_sem)
@@ -702,14 +711,14 @@
     return pl.pallas_call(
         functools.partial(dx_kernel, groups, local),
         grid=(len(groups), local),
-        in_specs=[SMEM, SMEM, SMEM, VMEM] + [ANY] * 2 + [per_local(d_model, d_ff)] * 2,
+        in_specs=[SMEM, SMEM, SMEM, SMEM, VMEM] + [ANY] * 2 + [per_local(d_model, d_ff)] * 2,
         out_specs=ANY,
         out_shape=Shape((blocks, BLK, d_model), bf16),
         scratch_shapes=rows + work + [DMA((RING,)), pltpu.VMEM((2, 2, row_cap, d_ff), bf16), DMA((2, 2))],
         compiler_params=grid_params(2),
         cost_estimate=cost(6 * blocks * BLK * d_model * d_ff, 20 << 20),
         name="expert_dx",
-    )(starts, block_map(pieces, nb), group_spans(groups), tab, da_rows, db_rows, w1, w3)
+    )(starts, block_map(pieces, nb), group_spans(groups), row_totals(groups, starts), tab, da_rows, db_rows, w1, w3)
 
 
 def router_grad_kernel(scale, x_ref, prob_ref, dg_ref, ids_ref, load_ref, dlog_ref, dw_ref):

time: 862 us -> 856 us (level)
  Pallas kernels: 740 us -> 729 us
  blocking collectives: 9.25 us -> 0 us
    all_to_all x1 -> x0, blocking collectives: 9.25 us -> none  [per_device(): dg_all = lax.all_to_all(dg, 'ep', FIRST, FIRST, tiled=True)]
  transfers between devices with their start and end apart: 19 -> 20, of which waited for: 7 -> 8; matrix products, arithmetic and copies ran while one was open for 1% -> 1% of each run, Pallas kernels for 72% -> 71%
where the time goes in v5:
time: 856 us; the launch traced here: 846 us
  Pallas kernels  729 us (85%)
  waiting for transfers between devices  43.3 us (5%)
  starting transfers between devices  29 us (3%)
  local copies, waits for them, and re-layouts  19.7 us (2%)
  between operations  16.7 us (2%)
    pallas_call x1, Pallas kernels, run_exchange(): pl.pallas_call(functools.partial(exchange_kernel, half, len(dws)), in_spe...  346 us
    pallas_call x4, Pallas kernels, run_grad(): pl.pallas_call(functools.partial(grad_kernel, g, last, local, pieces), gr...  189 us
    pallas_call x2, Pallas kernels, run_y(): pl.pallas_call(functools.partial(y_kernel, groups, local), grid=(len(grou...  96.2 us
    pallas_call x2, Pallas kernels, run_dx(): pl.pallas_call(functools.partial(dx_kernel, groups, local), grid=(len(gro...  74.5 us
    ppermute x14, waiting for transfers between devices, hop(): return lax.ppermute(v, 'ep', [(i, i ^ bit) for i in SOURCES])  34.1 us
  transfers between devices with their start and end apart: 20, of which 8 were waited for; matrix products, arithmetic and copies ran while one was open for 1% of the time, Pallas kernels for 71%

profile of v5, /device:TPU:0, one launch (start us, length us, event | category | flops | bytes accessed | tf_op | source)
XLA Modules:
  0.0 845.8 jit_solution(7784682562865103187)
XLA Ops:
  7.7 6.8 router.1
  14.5 4.8 all-to-all-start
  24.7 3.0 pad_maximum_fusion
  30.9 2.9 collective-permute-done.3
  39.0 46.8 %expert_grad.4 = (bf16[4,4,2048,512]{3,2,1,0:T(8,128)(2,1)}, bf16[4,4,2048,512]{3,2,1,0:T(8,128)(2,1)}, bf16[4,4,2048,512]{3,2,1,0:T(8,128)(2,1)}, f32[4,1024,1024]{2,1,0:T(8,128)}, f32[4,512,1024]{2,1,0:T(8,128)}) custom-call(s32[512]{0:T(512)} %reshape.95.refs_0_.starts_ref, s32[24]{0:T(128)} %constant.36.clone.refs_1_.bmap_ref, f32[48,8,256]{2,1,0:T(8,128)} %bitcast.38, ...), custom_call_target="tpu_custom_call" | custom-call | flops 19327352832 | bytes 41943040 | tf_op jit(solution)/shard_map/expert_grad/pallas_call | solution.py:438
  86.6 25.7 %expert_y.2 = (bf16[12,256,1024]{2,1,0:T(8,128)(2,1)}, f32[12,8,256]{2,1,0:T(8,128)}) custom-call(s32[512]{0:T(512)} %reshape.95.refs_0_.starts_ref, s32[24]{0:T(128)} %constant.36.clone.refs_1_.bmap_ref, s32[2]{0:T(128)} %iota_multiply_fusion.spans_ref, s32[4]{0:T(128)} %multiply_reduce_fusion.3.totals_ref, f32[48,8,256]{2,1,0:T(8,128)} %bitcast.39, ...), custom_call_target="tpu_custom_call" | custom-call | flops 6442450944 | bytes 20971520 | tf_op jit(solution)/shard_map/expert_y/pallas_call | solution.py:655
  112.4 3.8 collective-permute-start.8
  118.1 3.7 collective-permute-done.8.refs_4_.refs_8_.refs_1_
  121.8 4.5 collective-permute-done.9.refs_6_.refs_10_.refs_3_
  126.3 46.3 %expert_grad.5 = (bf16[4,4,2048,512]{3,2,1,0:T(8,128)(2,1)}, bf16[4,4,2048,512]{3,2,1,0:T(8,128)(2,1)}, bf16[4,4,2048,512]{3,2,1,0:T(8,128)(2,1)}, f32[4,1024,1024]{2,1,0:T(8,128)}, f32[4,512,1024]{2,1,0:T(8,128)}) custom-call(s32[512]{0:T(512)} %reshape.95.refs_0_.starts_ref, ...), custom_call_target="tpu_custom_call", output_to_operand_aliasing={{0}: (16, {}), {1}: (17, {}), {2}: (18, {})} | custom-call | flops 19327352832 | bytes 41943040 | tf_op jit(solution)/shard_map/expert_grad/pallas_call | solution.py:438
  172.5 14.4 %collective-permute-done.4.refs_3_.refs_7_.refs_4_ = bf16[2,768,1024]{2,1,0:T(8,128)(2,1)} collective-permute-done((bf16[2,768,1024]{2,1,0:T(8,128)(2,1)}, bf16[2,768,1024]{2,1,0:T(8,128)(2,1)}, u32[]{:S(2)}, u32[]{:S(2)}) %collective-permute-start.4) | collective-permute-done | bytes 3145760 | tf_op jit(solution)/shard_map/ppermute | solution.py:1025
  191.4 20.0 %expert_dx.2 = bf16[12,256,1024]{2,1,0:T(8,128)(2,1)} custom-call(s32[512]{0:T(512)} %reshape.95.refs_0_.starts_ref, s32[24]{0:T(128)} %constant.36.clone.refs_1_.bmap_ref, s32[2]{0:T(128)} %iota_multiply_fusion.spans_ref, s32[4]{0:T(128)} %multiply_reduce_fusion.2.totals_ref, f32[48,8,256]{2,1,0:T(8,128)} %bitcast.41, ...), custom_call_target="tpu_custom_call" | custom-call | flops 9663676416 | bytes 20971520 | tf_op jit(solution)/shard_map/expert_dx/pallas_call | solution.py:711
  211.5 46.4 %expert_grad.6 = (bf16[4,4,2048,512]{3,2,1,0:T(8,128)(2,1)}, bf16[4,4,2048,512]{3,2,1,0:T(8,128)(2,1)}, bf16[4,4,2048,512]{3,2,1,0:T(8,128)(2,1)}, f32[4,1024,1024]{2,1,0:T(8,128)}, f32[4,512,1024]{2,1,0:T(8,128)}) custom-call(s32[512]{0:T(512)} %reshape.95.refs_0_.starts_ref, ...), custom_call_target="tpu_custom_call", output_to_operand_aliasing={{0}: (16, {}), {1}: (17, {}), {2}: (18, {})} | custom-call | flops 19327352832 | bytes 41943040 | tf_op jit(solution)/shard_map/expert_grad/pallas_call | solution.py:438
  261.4 5.5 collective-permute-done.14.refs_4_.refs_8_.refs_9_
  266.9 4.5 collective-permute-done.15.refs_6_.refs_10_.refs_11_
  271.4 49.6 %expert_grad.7 = (bf16[4,4,2048,512]{3,2,1,0:T(8,128)(2,1)}, bf16[4,4,2048,512]{3,2,1,0:T(8,128)(2,1)}, bf16[4,4,2048,512]{3,2,1,0:T(8,128)(2,1)}, bf16[4,1024,5...) custom-call(s32[512]{0:T(512)} %reshape.95.refs_0_.starts_ref, ...), custom_call_target="tpu_custom_call", output_to_operand_aliasing={{0}: (16, {}), {1}: (17, {}), {2}: (18, {})} | custom-call | flops 19327352832 | bytes 41943040 | tf_op jit(solution)/shard_map/expert_grad/pallas_call | solution.py:438
  322.1 70.5 %expert_y.3 = (bf16[36,256,1024]{2,1,0:T(8,128)(2,1)}, f32[36,8,256]{2,1,0:T(8,128)}) custom-call(s32[512]{0:T(512)} %reshape.95.refs_0_.starts_ref, s32[72]{0:T(128)} %constant.43.clone.bmap_ref, s32[6]{0:T(128)} %constant.44.clone.spans_ref, s32[12]{0:T(128)} %reshape.98.totals_ref, f32[48,8,256]{2,1,0:T(8,128)} %bitcast.44, ...), custom_call_target="tpu_custom_call" | custom-call | flops 19327352832 | bytes 20971520 | tf_op jit(solution)/shard_map/expert_y/pallas_call | solution.py:655
  394.4 3.7 all-to-all-start.1
  398.2 6.2 all-to-all-done.1
  406.0 5.7 router_grad.1
  412.7 54.5 %expert_dx.3 = bf16[36,256,1024]{2,1,0:T(8,128)(2,1)} custom-call(s32[512]{0:T(512)} %reshape.95.refs_0_.starts_ref, s32[72]{0:T(128)} %constant.43.clone.bmap_ref, s32[6]{0:T(128)} %constant.44.clone.spans_ref, s32[12]{0:T(128)} %reshape.105.totals_ref, f32[48,8,256]{2,1,0:T(8,128)} %bitcast.45, bf16[4,4,2048,512]{3,2,1,0:T(8,128)(2,1)} %get-tuple-element.103.da_rows, ...), custom_call_target="tpu_custom_call" | custom-call | flops 28991029248 | bytes 20971520 | tf_op jit(solution)/shard_map/expert_dx/pallas_call | solution.py:711
  467.2 346.1 %exchange.1 = (bf16[1536,1024]{1,0:T(8,128)(2,1)}, bf16[1536,1024]{1,0:T(8,128)(2,1)}, bf16[1536,1024]{1,0:T(8,128)(2,1)}, bf16[1536,1024]{1,0:T(8,128)(2,1)}, b...) custom-call(bf16[2,1536,1024]{2,1,0:T(8,128)(2,1)} %bitcast.58, ...), custom_call_target="tpu_custom_call" | custom-call | flops 137438953472 | bytes 209715200 | tf_op jit(solution)/shard_map/exchange/pallas_call | solution.py:994
  814.6 10.7 %final.1 = (bf16[1536,1024]{1,0:T(8,128)(2,1)}, bf16[1536,1024]{1,0:T(8,128)(2,1)}) custom-call(f32[32,1536]{1,0:T(8,128)} %get-tuple-element.99.dlog_ref, f32[32,1024]{1,0:T(8,128)} %bitcast.53, bf16[1536,1024]{1,0:T(8,128)(2,1)} %get-tuple-element.107.refs_0_, bf16[1536,1024]{1,0:T(8,128)(2,1)} %get-tuple-element.108.refs_1_, ...), custom_call_target="tpu_custom_call" | custom-call | flops 805306368 | bytes 25165824 | tf_op jit(solution)/shard_map/final/pallas_call | solution.py:778
  827.0 4.6 copy.62
  (97 shorter events, 38.3 us)
Async XLA Ops:
  7.2 31.8 %collective-permute-start = (bf16[1536,1024]{1,0:T(8,128)(2,1)}, bf16[1536,1024]{1,0:T(8,128)(2,1)}, u32[]{:S(2)}, u32[]{:S(2)}) collective-permute-start(bf16[1536,1024]{1,0:T(8,128)(2,1)} %x_ref.3), channel_id=1, source_target_pairs={{0,1},{1,0},{2,3},{3,2},{4,5},{5,4},{6,7},{7,6},{8,9},{9,8},{10,11... | collective-permute-start | bytes 9437192 | tf_op jit(solution)/shard_map/ppermute | solution.py:1025
  14.5 19.3 %all-to-all-start = ((f32[8,8,1664]{2,1,0:T(8,128)}), f32[8,8,1664]{2,1,0:T(8,128)S(1)}, u32[]{:S(2)}, u32[]{:S(2)}) async-start(f32[8,8,1664]{2,1,0:T(8,128)} %get-tuple-element.64), calls=%async_computation | async-start | bytes 851968 | tf_op jit(solution)/shard_map/all_to_all | solution.py:1080
  19.3 19.7 %collective-permute-start.1 = (bf16[1536,1024]{1,0:T(8,128)(2,1)}, bf16[1536,1024]{1,0:T(8,128)(2,1)}, u32[]{:S(2)}, u32[]{:S(2)}) collective-permute-start(bf16[1536,1024]{1,0:T(8,128)(2,1)} %refs_0_.1), channel_id=1, source_target_pairs={{0,1},{1,0},{2,3},{3,2},{4,5},{5,4},{6,7},{7,6},{8,9},{9,8},{10,11... | collective-permute-start | bytes 9437192 | tf_op jit(solution)/shard_map/ppermute | solution.py:1025
  20.6 7.2 collective-permute-start.2
  27.7 6.1 collective-permute-start.3
  33.9 78.5 %collective-permute-start.6 = (bf16[2,768,1024]{2,1,0:T(8,128)(2,1)}, bf16[2,768,1024]{2,1,0:T(8,128)(2,1)}, u32[]{:S(2)}, u32[]{:S(2)}) collective-permute-start(bf16[2,768,1024]{2,1,0:T(8,128)(2,1)} %get-tuple-element.72), channel_id=1, source_target_pairs={{0,2},{1,3},{2,0},{3,1},{4,6},{5,7},{6,4},{7,5},{8,10},{9,11},{10,... | collective-permute-start | bytes 9437192 | tf_op jit(solution)/shard_map/ppermute | solution.py:1025
  35.9 76.4 %collective-permute-start.7 = (bf16[2,768,1024]{2,1,0:T(8,128)(2,1)}, bf16[2,768,1024]{2,1,0:T(8,128)(2,1)}, u32[]{:S(2)}, u32[]{:S(2)}) collective-permute-start(bf16[2,768,1024]{2,1,0:T(8,128)(2,1)} %get-tuple-element.72), channel_id=1, source_target_pairs={{0,4},{1,5},{2,6},{3,7},{4,0},{5,1},{6,2},{7,3},{8,12},{9,13},{10,... | collective-permute-start | bytes 9437192 | tf_op jit(solution)/shard_map/ppermute | solution.py:1025
  112.4 9.4 %collective-permute-start.8 = (bf16[2,768,1024]{2,1,0:T(8,128)(2,1)}, bf16[2,768,1024]{2,1,0:T(8,128)(2,1)}, u32[]{:S(2)}, u32[]{:S(2)}) collective-permute-start(bf16[2,768,1024]{2,1,0:T(8,128)(2,1)} %collective-permute-done.6.refs_3_.refs_7_.refs_0_), channel_id=1, source_target_pairs={{0,1},{1,0},{2,3},{3,2},{4,5},{5,4},{6,7},{7,6},{8,9},{9,8},{10,11... | collective-permute-start | bytes 9437192 | tf_op jit(solution)/shard_map/ppermute | solution.py:1025
  116.1 10.1 %collective-permute-start.9 = (bf16[2,768,1024]{2,1,0:T(8,128)(2,1)}, bf16[2,768,1024]{2,1,0:T(8,128)(2,1)}, u32[]{:S(2)}, u32[]{:S(2)}) collective-permute-start(bf16[2,768,1024]{2,1,0:T(8,128)(2,1)} %collective-permute-done.7.refs_5_.refs_9_.refs_2_), channel_id=1, source_target_pairs={{0,1},{1,0},{2,3},{3,2},{4,5},{5,4},{6,7},{7,6},{8,9},{9,8},{10,11... | collective-permute-start | bytes 9437192 | tf_op jit(solution)/shard_map/ppermute | solution.py:1025
  116.2 70.8 %collective-permute-start.4 = (bf16[2,768,1024]{2,1,0:T(8,128)(2,1)}, bf16[2,768,1024]{2,1,0:T(8,128)(2,1)}, u32[]{:S(2)}, u32[]{:S(2)}) collective-permute-start(bf16[2,768,1024]{2,1,0:T(8,128)(2,1)} %get-tuple-element.71), channel_id=1, source_target_pairs={{0,2},{1,3},{2,0},{3,1},{4,6},{5,7},{6,4},{7,5},{8,10},{9,11},{10,... | collective-permute-start | bytes 9437192 | tf_op jit(solution)/shard_map/ppermute | solution.py:1025
  116.2 70.8 %collective-permute-start.5 = (bf16[2,768,1024]{2,1,0:T(8,128)(2,1)}, bf16[2,768,1024]{2,1,0:T(8,128)(2,1)}, u32[]{:S(2)}, u32[]{:S(2)}) collective-permute-start(bf16[2,768,1024]{2,1,0:T(8,128)(2,1)} %get-tuple-element.71), channel_id=1, source_target_pairs={{0,4},{1,5},{2,6},{3,7},{4,0},{5,1},{6,2},{7,3},{8,12},{9,13},{10,... | collective-permute-start | bytes 9437192 | tf_op jit(solution)/shard_map/ppermute | solution.py:1025
  126.3 64.4 %copy-start.4 = (s32[512]{0:T(512)S(1)}, s32[512]{0:T(512)}, u32[]{:S(2)}) copy-start(s32[512]{0:T(512)} %reshape.95.refs_0_.starts_ref) | copy-start | bytes 6148
  187.0 24.5 %collective-permute-start.12 = (bf16[2,768,1024]{2,1,0:T(8,128)(2,1)}, bf16[2,768,1024]{2,1,0:T(8,128)(2,1)}, u32[]{:S(2)}, u32[]{:S(2)}) collective-permute-start(bf16[2,768,1024]{2,1,0:T(8,128)(2,1)} %collective-permute-done.4.refs_3_.refs_7_.refs_4_), channel_id=1, source_target_pairs={{0,1},{1,0},{2,3},{3,2},{4,5},{5,4},{6,7},{7,6},{8,9},{9,8},{10,11... | collective-permute-start | bytes 9437192 | tf_op jit(solution)/shard_map/ppermute | solution.py:1025
  187.0 24.5 %collective-permute-start.13 = (bf16[2,768,1024]{2,1,0:T(8,128)(2,1)}, bf16[2,768,1024]{2,1,0:T(8,128)(2,1)}, u32[]{:S(2)}, u32[]{:S(2)}) collective-permute-start(bf16[2,768,1024]{2,1,0:T(8,128)(2,1)} %collective-permute-done.5.refs_5_.refs_9_.refs_6_), channel_id=1, source_target_pairs={{0,1},{1,0},{2,3},{3,2},{4,5},{5,4},{6,7},{7,6},{8,9},{9,8},{10,11... | collective-permute-start | bytes 9437192 | tf_op jit(solution)/shard_map/ppermute | solution.py:1025
  187.5 70.3 %collective-permute-start.10 = (bf16[2,768,1024]{2,1,0:T(8,128)(2,1)}, bf16[2,768,1024]{2,1,0:T(8,128)(2,1)}, u32[]{:S(2)}, u32[]{:S(2)}) collective-permute-start(bf16[2,768,1024]{2,1,0:T(8,128)(2,1)} %collective-permute-done.7.refs_5_.refs_9_.refs_2_), channel_id=1, source_target_pairs={{0,2},{1,3},{2,0},{3,1},{4,6},{5,7},{6,4},{7,5},{8,10},{9,11},{10,... | collective-permute-start | bytes 9437192 | tf_op jit(solution)/shard_map/ppermute | solution.py:1025
  189.2 70.0 %collective-permute-start.11 = (bf16[2,768,1024]{2,1,0:T(8,128)(2,1)}, bf16[2,768,1024]{2,1,0:T(8,128)(2,1)}, u32[]{:S(2)}, u32[]{:S(2)}) collective-permute-start(bf16[2,768,1024]{2,1,0:T(8,128)(2,1)} %collective-permute-done.4.refs_3_.refs_7_.refs_4_), channel_id=1, source_target_pairs={{0,4},{1,5},{2,6},{3,7},{4,0},{5,1},{6,2},{7,3},{8,12},{9,13},{10,... | collective-permute-start | bytes 9437192 | tf_op jit(solution)/shard_map/ppermute | solution.py:1025
  259.3 7.6 collective-permute-start.14
  261.3 10.1 %collective-permute-start.15 = (bf16[2,768,1024]{2,1,0:T(8,128)(2,1)}, bf16[2,768,1024]{2,1,0:T(8,128)(2,1)}, u32[]{:S(2)}, u32[]{:S(2)}) collective-permute-start(bf16[2,768,1024]{2,1,0:T(8,128)(2,1)} %collective-permute-done.11.refs_5_.refs_9_.refs_10_), channel_id=1, source_target_pairs={{0,1},{1,0},{2,3},{3,2},{4,5},{5,4},{6,7},{7,6},{8,9},{9,8},{10,11... | collective-permute-start | bytes 9437192 | tf_op jit(solution)/shard_map/ppermute | solution.py:1025
  322.1 70.5 %copy-start.7 = (f32[12,8,256]{2,1,0:T(8,128)S(1)}, f32[12,8,256]{2,1,0:T(8,128)}, u32[]{:S(2)}) copy-start(f32[12,8,256]{2,1,0:T(8,128)} %get-tuple-element.68) | copy-start | bytes 294916
  322.1 76.1 %copy-start.6 = (s32[512]{0:T(512)S(1)}, s32[512]{0:T(512)}, u32[]{:S(2)}) copy-start(s32[512]{0:T(512)} %reshape.95.refs_0_.starts_ref) | copy-start | bytes 6148
  394.4 10.1 %all-to-all-start.1 = ((f32[8,4,1664]{2,1,0:T(4,128)}), f32[8,4,1664]{2,1,0:T(4,128)S(1)}, u32[]{:S(2)}, u32[]{:S(2)}) async-start(f32[8,4,1664]{2,1,0:T(4,128)} %pad_maximum_fusion.2), calls=%async_computation.1 | async-start | bytes 425984 | tf_op jit(solution)/shard_map/all_to_all | solution.py:1125
  398.1 427.3 %all-reduce.4.cloned.1.call-start = ((), (), s32[]{:S(2)}) async-start(), calls=%async_computation.2 | async-start | bytes 262144 | tf_op jit(solution)/shard_map/psum | solution.py:1131
  411.7 413.7 %all-reduce.6.cloned.1.call-start = ((), (), s32[]{:S(2)}) async-start(), calls=%async_computation.3 | async-start | bytes 8388608 | tf_op jit(solution)/shard_map/psum | solution.py:1117
  467.2 346.1 %copy-start.11 = (f32[2,32]{1,0:T(2,128)S(1)}, f32[2,32]{1,0:T(2,128)}, u32[]{:S(2)}) copy-start(f32[2,32]{1,0:T(2,128)} %copy-done.10) | copy-start | bytes 772
  (8 other events, 211.7 us)
Sparse Core Ops, SparseCore 0:
  411.8 129.1 all-reduce.3
  544.0 254.3 all-reduce.5
